TPU v7x, 32 devices: a whole 2x2x4 slice. The times are simulated.
32 devices in a mesh: batch: 4 (over x, core), seq: 2 (over y), heads: 4 (over z).
Axes of the slice: x: 2, y: 2, z: 4, core: 2. Of those that a mesh axis runs over, the one named last changes fastest.
Arguments:
- hidden_in: bfloat16 [48, 5120], P('batch', 'seq'), may hold values from -7 to 7
- lengths: int32 [48], P('batch'), may hold values from 1 to 512
- draft_ids: int32 [48], P('batch'), may hold values from 0 to 31999
- input_gain: float32 [5120], P('seq'), may hold values from 0.5 to 1.5
- w_query: bfloat16 [5120, 5120], P('seq', 'heads'), may hold values from -0.078125 to 0.078125
- w_latent: bfloat16 [5120, 4, 640], P('seq', 'heads'), may hold values from -0.078125 to 0.078125
- latent_cache: bfloat16 [48, 4, 512, 640], P('batch', 'heads', 'seq'), may hold values from -1200 to 1200
- key_up: bfloat16 [4, 320, 1280], P('heads'), may hold values from -0.3125 to 0.3125
- value_up: bfloat16 [4, 320, 1280], P('heads'), may hold values from -0.3125 to 0.3125
- w_out: bfloat16 [5120, 5120], P('heads', 'seq'), may hold values from -0.078125 to 0.078125
- final_gain: float32 [5120], P('seq'), may hold values from 0.1 to 1.9
- w_vocab: bfloat16 [5120, 32000], P('seq', 'heads'), may hold values from -0.26 to 0.26
Outputs:
- new_hidden: bfloat16 [48, 5120], P('batch', 'seq')
- log_probs: float32 [48, 32000], P('batch', 'heads')
- draft_logprob: float32 [48], P('batch')
Inputs may be any that keep to these rules, and one draw needn't show every extreme that they name: `lengths`: cache positions below a request's length are its live context.
All inputs are finite; a program needn't handle non-finite values.
Results may differ from a plain program's by a relative error of at most 0.012.
The roundings to bfloat16 on the way count: a program that leaves them out, or rounds other values in their place, can miss the bound.
Values sent between devices are 32-bit elements; how exact they have to be, the bound alone decides.
No kernel may reach another device: no remote copies, remote signals or barrier semaphores. Data moves between devices by JAX's collectives and lax.ppermute only.
A program may use at most 128 MiB of HBM per device.

v0:
```python
import math

import jax
import jax.numpy as jnp
from jax import lax
from jax.sharding import PartitionSpec as P

D = 5120
HEAD_DIM = 128
GROUP_HEADS = 10
GROUP_RANK = 320


epsilon = 1e-05
negative_fill = -1e30


def merged(part, axis, combine):
    gathered = jax.tree.map(lambda a: lax.all_gather(a, axis), part)

    def take(source):
        return jax.tree.map(lambda a: lax.dynamic_index_in_dim(a, source, 0, False), gathered)

    return lax.fori_loop(
        1, lax.axis_size(axis), lambda source, state: combine(state, take(source)), take(0)
    )


def softmax_join(left_part, right_part):
    left_max, left_total, left_mixed = left_part
    right_max, right_total, right_mixed = right_part
    joined = jnp.maximum(left_max, right_max)
    left_scale = jnp.exp(left_max - joined)
    right_scale = jnp.exp(right_max - joined)
    return (
        joined,
        left_total * left_scale + right_total * right_scale,
        left_mixed * left_scale[..., None] + right_mixed * right_scale[..., None],
    )


def vocab_join(left_part, right_part):
    left_max, left_total, left_pick = left_part
    right_max, right_total, right_pick = right_part
    joined = jnp.maximum(left_max, right_max)
    return (
        joined,
        left_total * jnp.exp(left_max - joined) + right_total * jnp.exp(right_max - joined),
        left_pick + right_pick,
    )


def vocab_stats(logits, columns, draft_ids):
    picked_local = jnp.sum(jnp.where(columns[None, :] == draft_ids[:, None], logits, 0.0), axis=1)
    local_top = jnp.max(logits, axis=1)
    return (picked_local, local_top)


def body(
    hidden_in,
    lengths,
    draft_ids,
    input_gain,
    w_query,
    w_latent,
    latent_cache,
    key_up,
    value_up,
    w_out,
    final_gain,
    w_vocab,
):
    batch_rows = hidden_in.shape[0]
    scaling = 1.0 / math.sqrt(HEAD_DIM)
    highest_prec = lax.Precision.HIGHEST
    states = hidden_in.astype(jnp.float32)
    gained = (states * input_gain).astype(jnp.bfloat16)
    query_part = jnp.dot(gained, w_query, preferred_element_type=jnp.float32)
    latent_matrix = w_latent.reshape(w_latent.shape[0], 2 * GROUP_RANK)
    latent_part = jnp.dot(gained, latent_matrix, preferred_element_type=jnp.float32)
    square_part = jnp.sum(states * states, axis=1)
    query_sum, latent_sum, square_sum = lax.psum((query_part, latent_part, square_part), "seq")
    inv_rms = lax.rsqrt(square_sum / D + epsilon)[:, None]
    query_rows = (inv_rms * query_sum).astype(jnp.bfloat16)
    latent = (inv_rms * latent_sum).astype(jnp.bfloat16)
    key_table = key_up[0].reshape(GROUP_RANK, GROUP_HEADS, HEAD_DIM)
    absorbed = jnp.einsum(
        "bhd,rhd->bhr",
        query_rows.reshape(batch_rows, GROUP_HEADS, HEAD_DIM),
        key_table,
        preferred_element_type=jnp.float32,
    ).astype(jnp.bfloat16)
    cache_rows = latent_cache[:, 0]
    local_span = cache_rows.shape[1]
    scores = (
        jnp.einsum(
            "bhr,btr->bht",
            absorbed,
            cache_rows[:, :, :GROUP_RANK],
            preferred_element_type=jnp.float32,
        )
        * scaling
    )
    positions = lax.axis_index("seq") * local_span + jnp.arange(local_span, dtype=jnp.int32)
    live_mask = positions[None, None, :] < lengths[:, None, None]
    scores = jnp.where(live_mask, scores, negative_fill)
    local_max = jnp.max(scores, axis=2)
    weights = jnp.where(live_mask, jnp.exp(scores - local_max[..., None]), 0.0)
    local_total = jnp.sum(weights, axis=2)
    local_mixed = jnp.einsum(
        "bht,btr->bhr",
        weights.astype(jnp.bfloat16),
        cache_rows[:, :, GROUP_RANK:],
        preferred_element_type=jnp.float32,
    )
    own_score = (
        jnp.einsum(
            "bhr,br->bh", absorbed, latent[:, :GROUP_RANK], preferred_element_type=jnp.float32
        )
        * scaling
    )
    own_value = latent[:, None, GROUP_RANK:].astype(jnp.float32)
    value_table = value_up[0].astype(jnp.float32).reshape(GROUP_RANK, GROUP_HEADS, HEAD_DIM)
    merged_max, merged_total, merged_mixed = merged(
        (local_max, local_total, local_mixed), "seq", softmax_join
    )
    highest = jnp.maximum(merged_max, own_score)
    cache_scale = jnp.exp(merged_max - highest)
    own_weight = jnp.exp(own_score - highest)
    denominator = merged_total * cache_scale + own_weight
    mixed_sum = merged_mixed * cache_scale[..., None] + own_weight[..., None] * own_value
    latent_out = mixed_sum / denominator[..., None]
    head_out = jnp.einsum("bhr,rhd->bhd", latent_out, value_table, precision=highest_prec).astype(
        jnp.bfloat16
    )
    head_out = head_out.reshape(batch_rows, GROUP_HEADS * HEAD_DIM)
    attn_part = jnp.dot(head_out, w_out, preferred_element_type=jnp.float32)
    attn_sum = lax.psum(attn_part, "heads")
    updated = states + attn_sum
    new_hidden = updated.astype(jnp.bfloat16)
    final_terms = jnp.dot(
        (updated * final_gain).astype(jnp.bfloat16), w_vocab, preferred_element_type=jnp.float32
    )
    final_squares = jnp.sum(updated * updated, axis=1)
    vocab_width = w_vocab.shape[1]
    vocab_start = lax.axis_index("heads") * vocab_width
    logit_sum, square_total = lax.psum((final_terms, final_squares), "seq")
    logits = lax.rsqrt(square_total / D + epsilon)[:, None] * logit_sum
    columns = vocab_start + jnp.arange(vocab_width, dtype=jnp.int32)
    picked_local, local_top = vocab_stats(logits, columns, draft_ids)
    local_sum = jnp.sum(jnp.exp(logits - local_top[:, None]), axis=1)
    top_all, total_all, picked = merged((local_top, local_sum, picked_local), "heads", vocab_join)
    log_total = top_all + jnp.log(total_all)
    log_probs = logits - log_total[:, None]
    draft_logprob = picked - log_total
    return (new_hidden, log_probs, draft_logprob)


def solution(mesh):
    return jax.shard_map(
        body,
        mesh=mesh,
        in_specs=(
            P("batch", "seq"),
            P("batch"),
            P("batch"),
            P("seq"),
            P("seq", "heads"),
            P("seq", "heads", None),
            P("batch", "heads", "seq", None),
            P("heads", None, None),
            P("heads", None, None),
            P("heads", "seq"),
            P("seq"),
            P("seq", "heads"),
        ),
        out_specs=(P("batch", "seq"), P("batch", "heads"), P("batch")),
        check_vma=False,
    )
```

profile of v0, /device:TPU:0, one launch (start us, length us, event | category | flops | bytes accessed | tf_op | source)
XLA Modules:
  0.0 174.1 jit_solution(14055392007863681934)
XLA Ops:
  7.2 0.0 copy-start
  7.2 0.0 copy-start.2
  7.2 0.0 copy-start.5
  7.2 0.0 all-reduce.13.cloned.1.call-start
  7.3 1.7 fusion.26
  8.9 0.0 copy-start.7
  8.9 4.5 %fusion.40 = f32[12,1280]{1,0:T(8,128)} fusion(bf16[2560,1280]{1,0:T(8,128)(2,1)} %param.18, bf16[12,2560]{1,0:T(8,128)(2,1)} %param.14, f32[2560]{0:T(1024)} %param.17), kind=kOutput, calls=%fused_computation.52 | convolution fusion | flops 78735360 | bytes 6686720 | tf_op jit(solution)/shard_map/dot_general | solution.py:78
  13.5 0.0 copy-done
  13.5 0.0 copy-done.2
  13.5 0.0 copy-done.5
  13.5 1.2 fusion.7
  14.6 0.0 all-reduce.13.cloned.1.call-update
  14.7 0.0 all-reduce.9.cloned.1.call-start
  14.7 0.0 copy-done.7
  14.7 0.1 broadcast_compare_fusion
  14.8 1.6 copy.30
  16.4 0.0 copy-start.4
  16.4 6.4 %copy.33 = bf16[12,1,256,640]{2,3,0,1:T(8,128)(2,1)} copy(bf16[12,1,256,640]{3,2,1,0:T(8,128)(2,1)} %param.20) | data formatting | bytes 7864320 | tf_op args[6]
  22.7 0.0 copy-done.4
  22.7 0.6 copy.35
  23.4 15.8 %all-reduce.13.cloned.1.call-done = (f32[12,1280]{1,0:T(8,128)}, f32[12]{0:T(128)}, f32[12,640]{1,0:T(8,128)}) async-done(((f32[12,1280]{1,0:T(8,128)}, f32[12]{0:T(128)}, f32[12,640]{1,0:T(8,128)}), (f32[12,1280]{1,0:T(8,128)}, f32[12]{0:T(128)}, f32[12,640]{1,0:T(8,128)})) %all-reduce.13.cloned.1.call-update) | async-done | bytes 92224 | tf_op jit(solution)/shard_map/psum | solution.py:82
  39.2 0.0 copy-start.6
  39.2 0.7 add_rsqrt_fusion.1
  39.9 1.0 multiply_convert_fusion.2
  40.9 0.3 fusion.19
  41.2 2.0 %fusion.58 = (f32[12,10]{1,0:T(8,128)S(1)}, f32[12,10,256]{2,1,0:T(8,128)S(1)}) fusion(bf16[12,256,640]{1,2,0:T(8,128)(2,1)} %bitcast.84, bf16[12,10,320]{2,0,1:T(8,128)(2,1)S(1)} %fusion.19, pred[12,256]{1,0:T(8,128)(4,1)S(1)} %broadcast_compare_fusion), kind=kOutput, calls=%fused_computation.84 | convolution fusion | flops 19752840 | bytes 2169312 | tf_op jit(solution)/shard_map/bhr,btr->bht/dot_general | solution.py:96
  43.2 0.2 fusion.28
  43.4 2.2 %fusion.9 = f32[12,10,320]{2,1,0:T(8,128)S(1)} fusion(bf16[12,256,640]{1,2,0:T(8,128)(2,1)} %bitcast.85, f32[12,10,256]{2,1,0:T(8,128)S(1)} %get-tuple-element.245, f32[12,10]{1,0:T(8,128)S(1)} %get-tuple-element.244, pred[12,256]{1,0:T(8,128)(4,1)S(1)} %broadcast_compare_fusion), kind=kOutput, calls=%fused_computation.12 | convolution fusion | flops 19752960 | bytes 2246112 | tf_op jit(solution)/shard_map/bht,btr->bhr/dot_general | solution.py:110
  45.6 4.4 %all-gather.7 = f32[2,12,10]{2,1,0:T(8,128)S(1)} all-gather(f32[1,12,10]{2,1,0:T(8,128)S(1)} %bitcast.91), channel_id=4, replica_groups=mesh['batch'=4,'seq'=2,'heads'=4] {'seq'}, dimensions={0}, use_global_device_ids=true | all-gather | bytes 1440 | tf_op jit(solution)/shard_map/all_gather | solution.py:19
  50.0 4.3 %all-gather.6 = f32[2,12,10]{2,1,0:T(8,128)S(1)} all-gather(f32[1,12,10]{2,1,0:T(8,128)S(1)} %bitcast.90), channel_id=3, replica_groups=mesh['batch'=4,'seq'=2,'heads'=4] {'seq'}, dimensions={0}, use_global_device_ids=true | all-gather | bytes 1440 | tf_op jit(solution)/shard_map/all_gather | solution.py:19
  54.3 0.0 copy-done.6
  54.3 0.1 multiply_convert_fusion.3
  54.4 0.1 slice_convert_fusion
  54.5 0.2 fusion.30
  54.7 7.4 %all-gather = f32[24,10,320]{2,1,0:T(8,128)S(1)} all-gather(f32[12,10,320]{2,1,0:T(8,128)S(1)} %fusion.9), channel_id=2, replica_groups=mesh['batch'=4,'seq'=2,'heads'=4] {'seq'}, dimensions={0}, use_global_device_ids=true | all-gather | bytes 460800 | tf_op jit(solution)/shard_map/all_gather | solution.py:19
  62.1 0.2 fusion.24
  62.3 1.1 fusion.20
  63.4 0.0 copy-start.8
  63.5 4.5 %fusion.59 = f32[12,2560]{1,0:T(8,128)} fusion(bf16[12,1280]{1,0:T(8,128)(2,1)S(1)} %bitcast.89, bf16[1280,2560]{1,0:T(8,128)(2,1)} %param.23), kind=kOutput, calls=%fused_computation.85 | convolution fusion | flops 78643200 | bytes 6707200 | tf_op jit(solution)/shard_map/dot_general | solution.py:137
  68.0 0.0 all-reduce.9.cloned.1.call-update
  68.0 0.0 all-reduce.11.cloned.1.call-start
  68.1 0.0 copy-done.8
  68.1 0.6 dynamic-slice
  69.3 33.7 %all-reduce.9.cloned.1.call-done = f32[12,2560]{1,0:T(8,128)} async-done(((f32[12,2560]{1,0:T(8,128)}), f32[12,2560]{1,0:T(8,128)}) %all-reduce.9.cloned.1.call-update) | async-done | bytes 122896 | tf_op jit(solution)/shard_map/psum | solution.py:138
  103.0 0.0 copy-start.3
  103.1 18.3 %fusion.37 = f32[12,8000]{1,0:T(8,128)} fusion(bf16[2560,8000]{0,1:T(8,128)(2,1)} %param.25, f32[2560]{0:T(1024)} %param.24, f32[12,2560]{1,0:T(8,128)} %all-reduce.9.cloned.1.call-done, bf16[12,2560]{1,0:T(8,128)(2,1)S(1)} %copy-done.2), kind=kOutput, calls=%fused_computation.49 | convolution fusion | flops 491642880 | bytes 41538560 | tf_op jit(solution)/shard_map/dot_general | solution.py:141
  121.4 0.0 all-reduce.11.cloned.1.call-update
  121.4 0.0 copy-done.3
  121.4 1.3 multiply_reduce_fusion.1
  122.7 5.0 %psum.46 = f32[12]{0:T(128)S(1)} all-reduce(f32[12]{0:T(128)} %get-tuple-element.240), channel_id=1, replica_groups=mesh['batch'=4,'seq'=2,'heads'=4] {'seq'}, use_global_device_ids=true, to_apply=%region_8.9 | all-reduce | flops 12 | bytes 96 | tf_op jit(solution)/shard_map/psum | solution.py:147
  127.7 22.0 %all-reduce.11.cloned.1.call-done = f32[12,8000]{1,0:T(8,128)} async-done(((f32[12,8000]{1,0:T(8,128)}), f32[12,8000]{1,0:T(8,128)}) %all-reduce.11.cloned.1.call-update) | async-done | bytes 384016 | tf_op jit(solution)/shard_map/psum | solution.py:147
  149.7 1.3 multiply_reduce_fusion
  151.0 0.2 dynamic-update-slice
  151.2 1.4 select_reduce_fusion
  152.6 0.2 dynamic-update-slice.2
  152.8 0.2 dynamic-update-slice.1
  153.1 11.7 %all-reduce.3 = (f32[48]{0:T(128)S(1)}, f32[48]{0:T(128)S(1)}, f32[48]{0:T(128)S(1)}) all-reduce(f32[48]{0:T(128)S(1)} %dynamic-update-slice, f32[48]{0:T(128)S(1)} %dynamic-update-slice.1, f32[48]{0:T(128)S(1)} %dynamic-update-slice.2), channel_id=5, replica_groups=mesh['batch'=4,'seq'=2,'heads'=4] {'heads'}, use_global_device_ids=true, to_apply=%add | all-reduce | flops 144 | bytes 1152
  164.7 0.1 reshape.101
  164.8 0.1 reshape.102
  164.9 0.1 reshape.103
  165.0 0.1 while.12
  165.1 0.5 fusion.55
  165.6 1.9 %multiply_subtract_fusion = f32[12,8000]{1,0:T(8,128)} fusion(f32[12,8000]{1,0:T(8,128)} %all-reduce.11.cloned.1.call-done, f32[12]{0:T(128)S(1)} %get-tuple-element.233, f32[12]{0:T(128)S(1)} %add_rsqrt_fusion), kind=kLoop, calls=%fused_computation.24 | loop fusion | flops 192000 | bytes 768096 | tf_op jit(solution)/shard_map/sub | solution.py:154
  167.5 0.0 copy-done.1
  (15 shorter events, 0.2 us)
Async XLA Ops:
  7.2 6.3 %copy-start = (bf16[2560,1,640]{2,0,1:T(8,128)(2,1)S(1)}, bf16[2560,1,640]{2,0,1:T(8,128)(2,1)}, u32[]{:S(2)}) copy-start(bf16[2560,1,640]{2,0,1:T(8,128)(2,1)} %param.19) | copy-start | bytes 9830404
  7.2 6.3 %copy-start.2 = (bf16[12,2560]{1,0:T(8,128)(2,1)S(1)}, bf16[12,2560]{1,0:T(8,128)(2,1)}, u32[]{:S(2)}) copy-start(bf16[12,2560]{1,0:T(8,128)(2,1)} %param.14) | copy-start | bytes 184324
  7.2 6.3 %copy-start.5 = (f32[2560]{0:T(1024)S(1)}, f32[2560]{0:T(1024)}, u32[]{:S(2)}) copy-start(f32[2560]{0:T(1024)} %param.17) | copy-start | bytes 30724
  7.2 32.0 %all-reduce.13.cloned.1.call-start = ((), (), s32[]{:S(2)}) async-start(), calls=%async_computation.2 | async-start | bytes 246784 | tf_op jit(solution)/shard_map/psum | solution.py:82
  8.9 5.8 %copy-start.7 = (s32[12]{0:T(128)S(1)}, s32[12]{0:T(128)}, u32[]{:S(2)}) copy-start(s32[12]{0:T(128)} %param.15) | copy-start | bytes 148
  14.7 88.4 %all-reduce.9.cloned.1.call-start = ((), (), s32[]{:S(2)}) async-start(), calls=%async_computation | async-start | bytes 327680 | tf_op jit(solution)/shard_map/psum | solution.py:138
  16.4 6.4 %copy-start.4 = (bf16[1,320,1280]{2,1,0:T(8,128)(2,1)S(1)}, bf16[1,320,1280]{2,1,0:T(8,128)(2,1)}, u32[]{:S(2)}) copy-start(bf16[1,320,1280]{2,1,0:T(8,128)(2,1)} %param.22) | copy-start | bytes 2457604
  39.2 15.2 %copy-start.6 = (f32[12,640]{1,0:T(8,128)S(1)}, f32[12,640]{1,0:T(8,128)}, u32[]{:S(2)}) copy-start(f32[12,640]{1,0:T(8,128)} %get-tuple-element.229) | copy-start | bytes 92164
  63.4 4.7 %copy-start.8 = (u32[32]{0:T(128)S(1)}, u32[32]{0:T(128)}, u32[]{:S(2)}) copy-start(u32[32]{0:T(128)} %constant.107) | copy-start | bytes 388
  68.0 81.7 %all-reduce.11.cloned.1.call-start = ((), (), s32[]{:S(2)}) async-start(), calls=%async_computation.1 | async-start | bytes 1032192 | tf_op jit(solution)/shard_map/psum | solution.py:147
  103.0 18.3 %copy-start.3 = (f32[12,2560]{1,0:T(8,128)S(1)}, f32[12,2560]{1,0:T(8,128)}, u32[]{:S(2)}) copy-start(f32[12,2560]{1,0:T(8,128)} %all-reduce.9.cloned.1.call-done) | copy-start | bytes 368644
  103.0 64.5 %copy-start.1 = (bf16[2560,1,640]{2,0,1:T(8,128)(2,1)S(1)}, bf16[2560,1,640]{2,0,1:T(8,128)(2,1)}, u32[]{:S(2)}) copy-start(bf16[2560,1,640]{2,0,1:T(8,128)(2,1)} %param.19) | copy-start | bytes 9830404
Sparse Core Ops, SparseCore 0:
  14.8 24.3 all-reduce.12
  68.1 34.8 all-reduce.8
  121.5 28.1 all-reduce.10
where the time goes:
time: 175 us; the launch traced here: 174 us
  waiting for transfers between devices  71.6 us (41%)
  matrix products  34.3 us (20%)
  blocking collectives  32.8 us (19%)
  between operations  14.6 us (8%)
  other arithmetic  10.5 us (6%)
  local copies, waits for them, and re-layouts  10.2 us (6%)
    psum x1, waiting for transfers between devices, body(): attn_sum = lax.psum(attn_part, 'heads')  33.7 us
    psum x1, waiting for transfers between devices, body(): logit_sum, square_total = lax.psum((final_terms, final_squares), 'seq')  22 us
    dot_general x1, matrix products, body(): jnp.dot((updated * final_gain).astype(jnp.bfloat16), w_vocab, preferred_e...  18.3 us
    all_gather x3, blocking collectives, merged(): gathered = jax.tree.map(lambda a: lax.all_gather(a, axis), part)  16.1 us
    psum x1, waiting for transfers between devices, body(): lax.psum((query_part, latent_part, square_part), 'seq')  15.8 us
    unnamed x1, blocking collectives  11.7 us
    unnamed x30, local copies, waits for them, and re-layouts  9.88 us
    psum x1, blocking collectives, body(): logit_sum, square_total = lax.psum((final_terms, final_squares), 'seq')  5.04 us
  transfers between devices with their start and end apart: 3, of which 3 were waited for; matrix products, arithmetic and copies ran while one was open for 6% of the time, Pallas kernels for 0%

commit v1 on v0

v1 whole, which is shorter than its diff:
```python
import math

import jax
import jax.numpy as jnp
from jax import lax
from jax.experimental import pallas as pl
from jax.experimental.pallas import tpu as pltpu
from jax.sharding import PartitionSpec as P

HEAD_DIM = 128
LANES = 128
ROW_TILE = 16
EPSILON = 1e-05
NEGATIVE = -1e30
MIB = 1 << 20
ANY = pl.BlockSpec(memory_space=pl.ANY)
VMEM = pl.BlockSpec(memory_space=pltpu.VMEM)
SMEM = pl.BlockSpec(memory_space=pltpu.SMEM)
NT = (((1,), (1,)), ((), ()))


def resident(array):
    return pltpu.with_memory_space_constraint(array, pltpu.VMEM)


def stored(array):
    return pltpu.with_memory_space_constraint(array, pltpu.HBM)


def cost(micros):
    return pl.CostEstimate(flops=int(micros * 5e6), bytes_accessed=0, transcendentals=0)


def params(mib):
    return pltpu.CompilerParams(vmem_limit_bytes=int(mib * MIB))


def round_up(value, step):
    return -(-value // step) * step


def fold_of(rows, width):
    fold = 8 // math.gcd(rows, 8)
    return fold if width % (fold * LANES) == 0 else 1


def put_folded(ref, rows, fold, start, value):
    width = ref.shape[1]
    done = 0
    while done < value.shape[1]:
        piece, at = divmod(start + done, width)
        size = min(value.shape[1] - done, width - at)
        ref[piece * rows : (piece + 1) * rows, at : at + size] = value[:, done : done + size]
        done += size


def get_folded(refs, rows, start, size):
    width = refs[0].shape[1]
    pieces = []
    done = 0
    while done < size:
        piece, at = divmod(start + done, width)
        span = min(size - done, width - at)
        block = None
        for ref in refs:
            term = ref[piece * rows : (piece + 1) * rows, at : at + span]
            block = term if block is None else block + term
        pieces.append(block)
        done += span
    return pieces[0] if len(pieces) == 1 else jnp.concatenate(pieces, axis=1)


def swap(array, axis, mask):
    size = lax.axis_size(axis)
    return lax.ppermute(array, axis, [(i, i ^ mask) for i in range(size)])


def is_power(size):
    return size & (size - 1) == 0


def project(hidden, gain, w_query, w_latent):
    rows, depth = hidden.shape
    q_width, l_width = w_query.shape[1], w_latent.shape[1]
    width = q_width + l_width + LANES
    fold = fold_of(rows, width)
    chunks = 5 if depth % (5 * LANES) == 0 else 1
    step = depth // chunks

    def kernel(x_ref, gain_ref, wq_ref, wl_ref, out_ref, q_buf, l_buf, sems):
        copies = []
        for c in range(chunks):
            at = pl.ds(c * step, step)
            copies.append(
                (
                    pltpu.make_async_copy(wq_ref.at[at], q_buf.at[at], sems.at[0, c]),
                    pltpu.make_async_copy(wl_ref.at[at], l_buf.at[at], sems.at[1, c]),
                )
            )
        for pair in copies:
            for copy in pair:
                copy.start()
        states = x_ref[...].astype(jnp.float32)
        gained = (states * gain_ref[...]).astype(jnp.bfloat16)
        square = jnp.sum(states * states, axis=1, keepdims=True)
        acc_q = acc_l = None
        for c in range(chunks):
            for copy in copies[c]:
                copy.wait()
            x = gained[:, c * step : (c + 1) * step]
            part_q = jnp.dot(
                x, q_buf[c * step : (c + 1) * step, :], preferred_element_type=jnp.float32
            )
            part_l = jnp.dot(
                x, l_buf[c * step : (c + 1) * step, :], preferred_element_type=jnp.float32
            )
            acc_q = part_q if c == 0 else acc_q + part_q
            acc_l = part_l if c == 0 else acc_l + part_l
        put_folded(out_ref, rows, fold, 0, acc_q)
        put_folded(out_ref, rows, fold, q_width, acc_l)
        put_folded(
            out_ref, rows, fold, q_width + l_width, jnp.broadcast_to(square, (rows, LANES))
        )

    return pl.pallas_call(
        kernel,
        out_shape=jax.ShapeDtypeStruct((rows * fold, width // fold), jnp.float32),
        in_specs=[VMEM, VMEM, ANY, ANY],
        out_specs=VMEM,
        scratch_shapes=[
            pltpu.VMEM(w_query.shape, w_query.dtype),
            pltpu.VMEM(w_latent.shape, w_latent.dtype),
            pltpu.SemaphoreType.DMA((2, chunks)),
        ],
        compiler_params=params(14),
        cost_estimate=cost(5),
        name="project",
    )(hidden, gain, stored(w_query), stored(w_latent))


def fetch_rows(table, after, low, high, micros, pieces=4):
    step = round_up(-(-(high - low) // pieces), 16)
    bounds = [(at, min(at + step, high)) for at in range(low, high, step)]

    def kernel(table_ref, after_ref, out_ref, sems):
        copies = [
            pltpu.make_async_copy(
                table_ref.at[pl.ds(a, b - a)], out_ref.at[pl.ds(a - low, b - a)], sems.at[i]
            )
            for i, (a, b) in enumerate(bounds)
        ]
        for copy in copies:
            copy.start()
        for copy in copies:
            copy.wait()

    return pl.pallas_call(
        kernel,
        out_shape=pltpu.VMEM((high - low,) + table.shape[1:], table.dtype),
        in_specs=[ANY, ANY],
        out_specs=VMEM,
        scratch_shapes=[pltpu.SemaphoreType.DMA((len(bounds),))],
        compiler_params=params(1),
        cost_estimate=cost(micros),
        name="fetch_rows",
    )(stored(table), after)


def fetch_attention(cache, key_up, value_up, after, micros):
    rank, width = value_up.shape
    full = round_up(rank, LANES)

    def kernel(cache_ref, key_ref, value_ref, after_ref, cache_out, key_out, value_out, sems):
        requests = cache.shape[0]
        copies = [
            pltpu.make_async_copy(key_ref, key_out, sems.at[0]),
            pltpu.make_async_copy(value_ref, value_out.at[pl.ds(full - rank, rank)], sems.at[1]),
            pltpu.make_async_copy(cache_ref, cache_out, sems.at[2]),
        ]
        for copy in copies:
            copy.start()
        value_out[0 : full - rank, :] = jnp.zeros((full - rank, width), value_up.dtype)
        for copy in copies:
            copy.wait()

    return pl.pallas_call(
        kernel,
        out_shape=(
            pltpu.VMEM(cache.shape, cache.dtype),
            pltpu.VMEM(key_up.shape, key_up.dtype),
            pltpu.VMEM((full, width), value_up.dtype),
        ),
        in_specs=[ANY] * 4,
        out_specs=(VMEM,) * 3,
        scratch_shapes=[pltpu.SemaphoreType.DMA((3,))],
        compiler_params=params(1),
        cost_estimate=cost(micros),
        name="fetch_attention",
    )(stored(cache), stored(key_up), stored(value_up), after)


def attend(own, other, lengths, cache, key_up, value_pad, features):
    requests, span, width = cache.shape
    rank = width // 2
    full = value_pad.shape[0]
    low = width - full
    heads = key_up.shape[1] // HEAD_DIM
    slot = round_up(heads, 8)
    scaling = 1.0 / math.sqrt(HEAD_DIM)
    q_width = heads * HEAD_DIM
    send_width = q_width + 2 * LANES
    fold = fold_of(requests, send_width)

    def kernel(
        own_ref, other_ref, length_ref, cache_ref, key_ref, value_ref,
        send_ref, local_ref, score_own, top_buf, total_buf, latent_buf, stack, *tiles,
    ):
        absorbed, mixed = tiles[: full // LANES], tiles[full // LANES :]
        refs = (own_ref, other_ref)
        square = get_folded(refs, requests, q_width + width, LANES)
        inv = lax.rsqrt(square[:, 0:1] / features + EPSILON)
        query = (inv * get_folded(refs, requests, 0, q_width)).astype(jnp.bfloat16)
        latent = (inv * get_folded(refs, requests, q_width, width)).astype(jnp.bfloat16)
        latent_buf[...] = latent.astype(jnp.float32)
        for tile in absorbed:
            tile[...] = jnp.zeros(tile.shape, jnp.float32)
        for j in range(heads):
            at = slice(j * HEAD_DIM, (j + 1) * HEAD_DIM)
            row = lax.dot_general(
                query[:, at], key_ref[:, at], NT, preferred_element_type=jnp.float32
            )
            row = row.astype(jnp.bfloat16).astype(jnp.float32)
            for i, tile in enumerate(absorbed):
                piece = row[:, i * LANES : min((i + 1) * LANES, rank)]
                if piece.shape[1] < LANES:
                    edge = jnp.zeros((requests, LANES - piece.shape[1]), jnp.float32)
                    piece = jnp.concatenate([piece, edge], axis=1)
                tile[pl.ds(j, requests, stride=slot), :] = piece
        first = lax.axis_index("seq") * span
        positions = first + lax.broadcasted_iota(jnp.int32, (slot, span), 1)
        for b in range(requests):
            at = slice(b * slot, (b + 1) * slot)
            rows = jnp.concatenate([tile[at, :] for tile in absorbed], axis=1)
            score_own[at, :] = jnp.broadcast_to(
                jnp.sum(rows * latent_buf[b : b + 1, 0:full], axis=1, keepdims=True) * scaling,
                (slot, LANES),
            )
            scores = (
                lax.dot_general(
                    rows.astype(jnp.bfloat16),
                    cache_ref[b, :, 0:full],
                    NT,
                    preferred_element_type=jnp.float32,
                )
                * scaling
            )
            live = positions < length_ref[b]
            scores = jnp.where(live, scores, NEGATIVE)
            top = jnp.max(scores, axis=1, keepdims=True)
            weights = jnp.where(live, jnp.exp(scores - top), 0.0)
            top_buf[at, :] = jnp.broadcast_to(top, (slot, LANES))
            total_buf[at, :] = jnp.broadcast_to(
                jnp.sum(weights, axis=1, keepdims=True), (slot, LANES)
            )
            value = jnp.dot(
                weights.astype(jnp.bfloat16),
                cache_ref[b, :, low:width],
                preferred_element_type=jnp.float32,
            )
            for i, tile in enumerate(mixed):
                tile[at, :] = value[:, i * LANES : (i + 1) * LANES]
        lane = lax.broadcasted_iota(jnp.int32, (requests, LANES), 1)
        tops = jnp.full((requests, LANES), NEGATIVE, jnp.float32)
        owns = jnp.full((requests, LANES), NEGATIVE, jnp.float32)
        totals = jnp.zeros((requests, LANES), jnp.float32)
        second = ROW_TILE * -(-requests // ROW_TILE)
        stack[2 * second : 2 * second + requests, :] = latent[:, low:width]
        for j in range(heads):
            pick = pl.ds(j, requests, stride=slot)
            tops = jnp.where(lane == j, top_buf[pick, :], tops)
            totals = jnp.where(lane == j, total_buf[pick, :], totals)
            owns = jnp.where(lane == j, score_own[pick, :], owns)
            value = jnp.concatenate([tile[pick, :] for tile in mixed], axis=1)
            high = value.astype(jnp.bfloat16)
            stack[0:requests, :] = high
            stack[second : second + requests, :] = (value - high.astype(jnp.float32)).astype(
                jnp.bfloat16
            )
            at = slice(j * HEAD_DIM, (j + 1) * HEAD_DIM)
            lifted = jnp.dot(stack[...], value_ref[:, at], preferred_element_type=jnp.float32)
            put_folded(
                send_ref, requests, fold, j * HEAD_DIM,
                lifted[0:requests] + lifted[second : second + requests],
            )
            local_ref[:, at] = lifted[2 * second : 2 * second + requests]
        put_folded(send_ref, requests, fold, q_width, tops)
        put_folded(send_ref, requests, fold, q_width + LANES, totals)
        local_ref[:, q_width : q_width + LANES] = owns

    tall = requests * slot
    return pl.pallas_call(
        kernel,
        out_shape=(
            jax.ShapeDtypeStruct((requests * fold, send_width // fold), jnp.float32),
            jax.ShapeDtypeStruct((requests, q_width + LANES), jnp.float32),
        ),
        in_specs=[VMEM, VMEM, SMEM, VMEM, VMEM, VMEM],
        out_specs=(VMEM, VMEM),
        scratch_shapes=[
            pltpu.VMEM((tall, LANES), jnp.float32),
            pltpu.VMEM((tall, LANES), jnp.float32),
            pltpu.VMEM((tall, LANES), jnp.float32),
            pltpu.VMEM((requests, width), jnp.float32),
            pltpu.VMEM((3 * round_up(requests, ROW_TILE), full), jnp.bfloat16),
        ]
        + [pltpu.VMEM((tall, LANES), jnp.float32)] * (2 * full // LANES),
        compiler_params=params(5),
        cost_estimate=cost(5),
        name="attend",
    )(own, other, lengths, resident(cache), resident(key_up), resident(value_pad))


def merge_out(own, other, local, w_out, requests):
    q_width = local.shape[1] - LANES
    heads = q_width // HEAD_DIM
    width = w_out.shape[1]
    fold = fold_of(requests, width)
    step = 512 if width % 512 == 0 else width

    def kernel(own_ref, other_ref, local_ref, w_ref, out_ref, head_buf):
        top_a = get_folded((own_ref,), requests, q_width, LANES)
        top_b = get_folded((other_ref,), requests, q_width, LANES)
        total_a = get_folded((own_ref,), requests, q_width + LANES, LANES)
        total_b = get_folded((other_ref,), requests, q_width + LANES, LANES)
        own_score = local_ref[:, q_width : q_width + LANES]
        highest = jnp.maximum(jnp.maximum(top_a, top_b), own_score)
        scale_a = jnp.exp(top_a - highest)
        scale_b = jnp.exp(top_b - highest)
        own_weight = jnp.exp(own_score - highest)
        below = total_a * scale_a + total_b * scale_b + own_weight
        scale_a = scale_a / below
        scale_b = scale_b / below
        own_weight = own_weight / below
        for j in range(heads):
            at = slice(j * HEAD_DIM, (j + 1) * HEAD_DIM)
            value = (
                get_folded((own_ref,), requests, j * HEAD_DIM, HEAD_DIM) * scale_a[:, j : j + 1]
                + get_folded((other_ref,), requests, j * HEAD_DIM, HEAD_DIM)
                * scale_b[:, j : j + 1]
                + local_ref[:, at] * own_weight[:, j : j + 1]
            )
            head_buf[:, at] = value.astype(jnp.bfloat16)
        head_out = head_buf[...]
        for at in range(0, width, step):
            put_folded(
                out_ref, requests, fold, at,
                jnp.dot(head_out, w_ref[:, at : at + step], preferred_element_type=jnp.float32),
            )

    return pl.pallas_call(
        kernel,
        out_shape=jax.ShapeDtypeStruct((requests * fold, width // fold), jnp.float32),
        in_specs=[VMEM] * 4,
        out_specs=VMEM,
        scratch_shapes=[pltpu.VMEM((requests, q_width), jnp.bfloat16)],
        compiler_params=params(3),
        cost_estimate=cost(2),
        name="merge_out",
    )(own, other, local, resident(w_out))


def finish_states(own, other, hidden, gain):
    rows, width = hidden.shape

    def kernel(own_ref, other_ref, x_ref, gain_ref, new_ref, scaled_ref, square_ref):
        states = x_ref[...].astype(jnp.float32)
        updated = states + get_folded((own_ref, other_ref), rows, 0, width)
        new_ref[...] = updated.astype(jnp.bfloat16)
        scaled_ref[...] = (updated * gain_ref[...]).astype(jnp.bfloat16)
        square_ref[...] = jnp.broadcast_to(
            jnp.sum(updated * updated, axis=1, keepdims=True), (rows, LANES)
        )

    return pl.pallas_call(
        kernel,
        out_shape=(
            jax.ShapeDtypeStruct((rows, width), jnp.bfloat16),
            jax.ShapeDtypeStruct((rows, width), jnp.bfloat16),
            jax.ShapeDtypeStruct((rows, LANES), jnp.float32),
        ),
        in_specs=[VMEM] * 4,
        out_specs=(VMEM,) * 3,
        compiler_params=params(2),
        cost_estimate=cost(1),
        name="finish_states",
    )(own, other, hidden, gain)


def vocab_part(scaled, square, tables, first, last, width):
    rows = scaled.shape[0]
    fold = fold_of(rows, width)
    step = 512

    def kernel(x_ref, square_ref, *refs):
        tables_in, out_ref = refs[:-1], refs[-1]
        x = x_ref[...]
        base = 0
        for table in tables_in:
            low, high = max(first, base), min(last, base + table.shape[0])
            for at in range(low, high, step):
                end = min(at + step, high)
                put_folded(
                    out_ref, rows, fold, at - first,
                    lax.dot_general(
                        x, table[at - base : end - base, :], NT,
                        preferred_element_type=jnp.float32,
                    ),
                )
            base += table.shape[0]
        if last - first < width:
            put_folded(
                out_ref, rows, fold, last - first,
                jnp.broadcast_to(square_ref[:, 0:1], (rows, width - (last - first))),
            )

    return pl.pallas_call(
        kernel,
        out_shape=jax.ShapeDtypeStruct((rows * fold, width // fold), jnp.float32),
        in_specs=[VMEM] * (2 + len(tables)),
        out_specs=VMEM,
        compiler_params=params(3),
        cost_estimate=cost(6),
        name="vocab_part",
    )(scaled, square, *[resident(table) for table in tables])


def vocab_logits(parts, draft_ids, bounds, rows, features):
    columns = bounds[-1][1]
    count = len(bounds)
    flat = [array for pair in parts for array in pair]

    def kernel(id_ref, *refs):
        pairs = [refs[2 * i : 2 * i + 2] for i in range(count)]
        logit_ref, stat_ref = refs[2 * count :]
        full = pairs[-1][0].shape[0] * pairs[-1][0].shape[1] // rows
        square = get_folded(pairs[-1], rows, full - LANES, LANES)
        inv = lax.rsqrt(square[:, 0:1] / features + EPSILON)
        row = lax.broadcasted_iota(jnp.int32, (rows, 1), 0)
        wanted = jnp.zeros((rows, 1), jnp.int32)
        for r in range(rows):
            wanted = jnp.where(row == r, id_ref[r], wanted)
        wanted = wanted - lax.axis_index("heads") * columns
        top = jnp.full((rows, 1), NEGATIVE, jnp.float32)
        picked = jnp.zeros((rows, 1), jnp.float32)
        for pair, (first, last) in zip(pairs, bounds):
            logits = get_folded(pair, rows, 0, last - first) * inv
            logit_ref[:, first:last] = logits
            top = jnp.maximum(top, jnp.max(logits, axis=1, keepdims=True))
            column = first + lax.broadcasted_iota(jnp.int32, logits.shape, 1)
            picked = picked + jnp.sum(
                jnp.where(column == wanted, logits, 0.0), axis=1, keepdims=True
            )
        total = jnp.zeros((rows, 1), jnp.float32)
        for first, last in bounds:
            total = total + jnp.sum(
                jnp.exp(logit_ref[:, first:last] - top), axis=1, keepdims=True
            )
        lane = lax.broadcasted_iota(jnp.int32, (rows, LANES), 1)
        stat_ref[...] = jnp.where(
            lane == 0, top, jnp.where(lane == 1, total, jnp.where(lane == 2, picked, 0.0))
        )

    return pl.pallas_call(
        kernel,
        out_shape=(
            pltpu.VMEM((rows, columns), jnp.float32),
            jax.ShapeDtypeStruct((rows, LANES), jnp.float32),
        ),
        in_specs=[SMEM] + [VMEM] * len(flat),
        out_specs=(VMEM, VMEM),
        compiler_params=params(4),
        cost_estimate=cost(2),
        name="vocab_logits",
    )(draft_ids, *flat)


def vocab_finish(logits, stats):
    rows, columns = logits.shape
    count = len(stats)

    def kernel(logit_ref, *refs):
        stat_refs, out_ref, draft_ref = refs[:count], refs[count], refs[count + 1]
        state = [(ref[:, 0:1], ref[:, 1:2], ref[:, 2:3]) for ref in stat_refs]
        while len(state) > 1:
            joined = []
            for (top_a, sum_a, pick_a), (top_b, sum_b, pick_b) in zip(state[0::2], state[1::2]):
                top = jnp.maximum(top_a, top_b)
                joined.append(
                    (
                        top,
                        sum_a * jnp.exp(top_a - top) + sum_b * jnp.exp(top_b - top),
                        pick_a + pick_b,
                    )
                )
            state = joined
        top, total, picked = state[0]
        log_total = top + jnp.log(total)
        out_ref[...] = logit_ref[...] - log_total
        draft = picked - log_total
        row = lax.broadcasted_iota(jnp.int32, (rows, LANES), 0)
        lane = lax.broadcasted_iota(jnp.int32, (rows, LANES), 1)
        line = jnp.sum(jnp.where(row == lane, draft, 0.0), axis=0, keepdims=True)
        draft_ref[...] = line[:, 0:rows]

    return pl.pallas_call(
        kernel,
        out_shape=(
            jax.ShapeDtypeStruct((rows, columns), jnp.float32),
            jax.ShapeDtypeStruct((1, rows), jnp.float32),
        ),
        in_specs=[VMEM] * (1 + count),
        out_specs=(VMEM, VMEM),
        compiler_params=params(4),
        cost_estimate=cost(1),
        name="vocab_finish",
    )(resident(logits), *stats)


def pair_sum(array, axis):
    if lax.axis_size(axis) == 2:
        return array, swap(array, axis, 1)
    return lax.psum(array, axis), jnp.zeros_like(array)


def pair_softmax(array, axis, requests, q_width):
    if lax.axis_size(axis) == 2:
        return array, swap(array, axis, 1)
    fold = array.shape[0] // requests
    width = array.shape[1]
    flat = jnp.concatenate(
        [array[i * requests : (i + 1) * requests] for i in range(fold)], axis=1
    )
    every = lax.all_gather(flat, axis)
    tops = every[:, :, q_width : q_width + LANES]
    totals = every[:, :, q_width + LANES :]
    top = jnp.max(tops, axis=0)
    scale = jnp.exp(tops - top)
    heads = q_width // HEAD_DIM
    total = jnp.sum(totals * scale, axis=0)
    mixed = every[:, :, :q_width].reshape(every.shape[0], requests, heads, HEAD_DIM)
    mixed = jnp.sum(mixed * scale[:, :, :heads, None], axis=0).reshape(requests, q_width)
    flat = jnp.concatenate([mixed, top, total], axis=1)
    empty = jnp.concatenate(
        [jnp.zeros_like(mixed), jnp.full_like(top, NEGATIVE), jnp.zeros_like(total)], axis=1
    )

    def folded(value):
        return jnp.concatenate(
            [value[:, i * width : (i + 1) * width] for i in range(fold)], axis=0
        )

    return folded(flat), folded(empty)


def body(
    hidden_in,
    lengths,
    draft_ids,
    input_gain,
    w_query,
    w_latent,
    latent_cache,
    key_up,
    value_up,
    w_out,
    final_gain,
    w_vocab,
):
    rows, depth = hidden_in.shape
    features = depth * lax.axis_size("seq")
    columns = w_vocab.shape[1]
    table = w_vocab.T
    q_width = w_query.shape[1]

    sums = project(
        hidden_in,
        input_gain.reshape(1, depth),
        w_query,
        w_latent.reshape(depth, w_latent.shape[1] * w_latent.shape[2]),
    )
    own, other = pair_sum(sums, "seq")
    cache, keys, values = fetch_attention(
        latent_cache[:, 0], key_up[0], value_up[0], sums, 3
    )
    marks = [0]
    for share in (0.25, 0.55):
        marks.append(int(columns * share) // 512 * 512)
    marks.append(columns)

    packed, local = attend(own, other, lengths, cache, keys, values, features)
    own, other = pair_softmax(packed, "seq", rows, q_width)
    out_table = fetch_rows(w_out, packed, 0, w_out.shape[0], 3)
    part = merge_out(own, other, local, out_table, rows)

    heads = lax.axis_size("heads")
    tables = []
    if is_power(heads) and heads > 1:
        mask = 1
        level = 0
        while True:
            received = swap(part, "heads", mask)
            mask *= 2
            if mask >= heads:
                break
            tables.append(fetch_rows(table, part, marks[level], marks[level + 1], 3))
            level += 1
            part = part + received
    else:
        level = 0
        part, received = lax.psum(part, "heads"), jnp.zeros_like(part)
    tables.append(fetch_rows(table, part, marks[level], columns, 6, 8))

    new_hidden, scaled, square = finish_states(
        part, received, hidden_in, final_gain.reshape(1, depth)
    )
    chunk = round_up(-(-columns // 2), 512)
    bounds = [(0, min(chunk, columns)), (chunk, columns)]
    parts = []
    for first, last in bounds:
        width = round_up(last - first + (LANES if last == columns else 0), 2 * LANES)
        piece = vocab_part(scaled, square, tables, first, last, width)
        parts.append(pair_sum(piece, "seq"))
    logits, stats = vocab_logits(parts, draft_ids, bounds, rows, features)
    if is_power(heads):
        every = [stats] + [swap(stats, "heads", m) for m in range(1, heads)]
    else:
        gathered = lax.all_gather(stats, "heads")
        every = [gathered[i] for i in range(heads)]
        while not is_power(len(every)):
            every.append(jnp.concatenate([jnp.full_like(stats[:, :1], NEGATIVE), jnp.zeros_like(stats[:, 1:])], axis=1))
    log_probs, draft = vocab_finish(logits, every)
    return (new_hidden, log_probs, draft.reshape(rows))


def solution(mesh):
    return jax.shard_map(
        body,
        mesh=mesh,
        in_specs=(
            P("batch", "seq"),
            P("batch"),
            P("batch"),
            P("seq"),
            P("seq", "heads"),
            P("seq", "heads", None),
            P("batch", "heads", "seq", None),
            P("heads", None, None),
            P("heads", None, None),
            P("heads", "seq"),
            P("seq"),
            P("seq", "heads"),
        ),
        out_specs=(P("batch", "seq"), P("batch", "heads"), P("batch")),
        check_vma=False,
    )
```

time: 175 us -> 73.6 us (0.42)
  waiting for transfers between devices: 71.6 us -> 11.5 us
  Pallas kernels: 0 us -> 43.6 us
  matrix products: 34.3 us -> 0 us
  blocking collectives: 32.8 us -> 0 us
  starting transfers between devices: 0.12 us -> 15.8 us
  between operations: 14.6 us -> 0.74 us
  other arithmetic: 10.5 us -> 0.02 us
  local copies, waits for them, and re-layouts: 10.2 us -> 1.63 us
    psum x3 -> x0, waiting for transfers between devices: 71.5 us -> none  [the longest x1 33.7 us: body(): attn_sum = lax.psum(attn_part, 'heads')]
    pallas_call x0 -> x12, Pallas kernels: none -> 43.6 us  [the longest x3 16.9 us: fetch_rows(): pl.pallas_call(kernel, out_shape=pltpu.VMEM((high - low,) + table.shape[1...]
    dot_general x9 -> x0, matrix products: 34.3 us -> none  [the longest x1 18.3 us: body(): jnp.dot((updated * final_gain).astype(jnp.bfloat16), w_vocab, preferred_e...]
    all_gather x3 -> x0, blocking collectives: 16.1 us -> none  [merged(): gathered = jax.tree.map(lambda a: lax.all_gather(a, axis), part)]
    ppermute x0 -> x9, starting transfers between devices: none -> 15.8 us  [swap(): return lax.ppermute(array, axis, [(i, i ^ mask) for i in range(size)])]
    unnamed x1 -> x0, blocking collectives: 11.7 us -> none
    ppermute x0 -> x9, waiting for transfers between devices: none -> 11.5 us  [swap(): return lax.ppermute(array, axis, [(i, i ^ mask) for i in range(size)])]
    unnamed x30 -> x10, local copies, waits for them, and re-layouts: 9.88 us -> 0.91 us
  transfers between devices with their start and end apart: 3 -> 9, of which waited for: 3 -> 7; matrix products, arithmetic and copies ran while one was open for 6% -> 0% of each run, Pallas kernels for 0% -> 27%
where the time goes in v1:
time: 73.6 us; the launch traced here: 73.3 us
  Pallas kernels  43.6 us (59%)
  starting transfers between devices  15.8 us (21%)
  waiting for transfers between devices  11.5 us (16%)
  local copies, waits for them, and re-layouts  1.63 us (2%)
  between operations  0.74 us (1%)
    pallas_call x3, Pallas kernels, fetch_rows(): pl.pallas_call(kernel, out_shape=pltpu.VMEM((high - low,) + table.shape[1...  16.9 us
    ppermute x9, starting transfers between devices, swap(): return lax.ppermute(array, axis, [(i, i ^ mask) for i in range(size)])  15.8 us
    ppermute x9, waiting for transfers between devices, swap(): return lax.ppermute(array, axis, [(i, i ^ mask) for i in range(size)])  11.5 us
    pallas_call x2, Pallas kernels, vocab_part(): pl.pallas_call(kernel, out_shape=jax.ShapeDtypeStruct((rows * fold, width...  10.8 us
    pallas_call x1, Pallas kernels, attend(): pl.pallas_call(kernel, out_shape=(jax.ShapeDtypeStruct((requests * fold,...  5.26 us
    pallas_call x1, Pallas kernels, project(): pl.pallas_call(kernel, out_shape=jax.ShapeDtypeStruct((rows * fold, width...  4.27 us
    pallas_call x1, Pallas kernels, fetch_attention(): pl.pallas_call(kernel, out_shape=(pltpu.VMEM(cache.shape, cache.dtype), p...  2.65 us
  transfers between devices with their start and end apart: 9, of which 7 were waited for; matrix products, arithmetic and copies ran while one was open for 0% of the time, Pallas kernels for 27%

profile of v1, /device:TPU:0, one launch (start us, length us, event | category | flops | bytes accessed | tf_op | source)
XLA Modules:
  0.0 73.3 jit_solution(15437677493994692501)
XLA Ops:
  0.6 0.7 reshape.18.gain_ref
  1.3 0.0 copy-start
  1.4 0.9 %copy-done = bf16[12,2560]{1,0:T(8,128)(2,1)S(1)} copy-done((bf16[12,2560]{1,0:T(8,128)(2,1)S(1)}, bf16[12,2560]{1,0:T(8,128)(2,1)}, u32[]{:S(2)}) %copy-start) | copy-done | bytes 61464
  2.2 0.0 copy-start.2
  2.2 4.3 %project.1.after_ref.own_ref = f32[24,1024]{1,0:T(8,128)S(1)} custom-call(bf16[12,2560]{1,0:T(8,128)(2,1)S(1)} %copy-done, f32[1,2560]{1,0:T(1,128)S(1)} %reshape.18.gain_ref, bf16[2560,1280]{1,0:T(8,128)(2,1)} %wq_ref.1, bf16[2560,640]{1,0:T(8,128)(2,1)} %bitcast.9), custom_call_target="tpu_custom_call" | custom-call | flops 25000000 | tf_op jit(solution)/shard_map/project/pallas_call | solution.py:125
  6.5 3.1 %collective-permute-start = (f32[24,1024]{1,0:T(8,128)S(1)}, f32[24,1024]{1,0:T(8,128)S(1)}, u32[]{:S(2)}, u32[]{:S(2)}) collective-permute-start(f32[24,1024]{1,0:T(8,128)S(1)} %project.1.after_ref.own_ref), channel_id=1, source_target_pairs={{0,4},{4,0},{1,5},{5,1},{2,6},{6,2},{3,7},{7,3},{8,12},{12,8},{9,1... | collective-permute-start | bytes 294920 | tf_op jit(solution)/shard_map/ppermute | solution.py:75
  9.6 2.6 %fetch_attention.1 = (bf16[12,256,640]{2,1,0:T(8,128)(2,1)S(1)}, bf16[320,1280]{1,0:T(8,128)(2,1)S(1)}, bf16[384,1280]{1,0:T(8,128)(2,1)S(1)}) custom-call(bf16[12,256,640]{2,1,0:T(8,128)(2,1)} %bitcast.8, bf16[320,1280]{1,0:T(8,128)(2,1)} %bitcast.10, bf16[320,1280]{1,0:T(8,128)(2,1)} %bitcast.11, f32[24,1024]{1,0:T(8,128)S(1)} %project.1.after_ref.own_ref), custom_call_target="tpu_custom_call" | custom-call | flops 15000000 | tf_op jit(solution)/shard_map/fetch_attention/pallas_call | solution.py:186
  12.2 0.1 collective-permute-done.other_ref
  12.4 0.0 copy-done.2
  12.4 5.3 %attend.1 = (f32[24,768]{1,0:T(8,128)S(1)}, f32[12,1408]{1,0:T(8,128)S(1)}) custom-call(f32[24,1024]{1,0:T(8,128)S(1)} %project.1.after_ref.own_ref, f32[24,1024]{1,0:T(8,128)S(1)} %collective-permute-done.other_ref, s32[12]{0:T(128)S(1)} %copy-done.2, bf16[12,256,640]{2,1,0:T(8,128)(2,1)S(1)} %get-tuple-element.15.cache_ref, ...), custom_call_target="tpu_custom_call" | custom-call | flops 25000000 | tf_op jit(solution)/shard_map/attend/pallas_call | solution.py:301
  17.6 1.9 %collective-permute-start.1 = (f32[24,768]{1,0:T(8,128)S(1)}, f32[24,768]{1,0:T(8,128)S(1)}, u32[]{:S(2)}, u32[]{:S(2)}) collective-permute-start(f32[24,768]{1,0:T(8,128)S(1)} %get-tuple-element.18.after_ref.own_ref), channel_id=1, source_target_pairs={{0,4},{4,0},{1,5},{5,1},{2,6},{6,2},{3,7},{7,3},{8,12},{12,8},{9,1... | collective-permute-start | bytes 221192 | tf_op jit(solution)/shard_map/ppermute | solution.py:75
  19.5 2.9 %fetch_rows.3.w_ref = bf16[1280,2560]{1,0:T(8,128)(2,1)S(1)} custom-call(bf16[1280,2560]{1,0:T(8,128)(2,1)} %table_ref.1, f32[24,768]{1,0:T(8,128)S(1)} %get-tuple-element.18.after_ref.own_ref), custom_call_target="tpu_custom_call" | custom-call | flops 15000000 | tf_op jit(solution)/shard_map/fetch_rows/pallas_call | solution.py:157
  22.5 0.0 copy-start.4
  22.5 0.0 collective-permute-done.1.other_ref
  22.5 1.1 %merge_out.1.after_ref = f32[24,1280]{1,0:T(8,128)S(1)} custom-call(f32[24,768]{1,0:T(8,128)S(1)} %get-tuple-element.18.after_ref.own_ref, f32[24,768]{1,0:T(8,128)S(1)} %collective-permute-done.1.other_ref, f32[12,1408]{1,0:T(8,128)S(1)} %get-tuple-element.19.local_ref, bf16[1280,2560]{1,0:T(8,128)(2,1)S(1)} %fetch_rows.3.w_ref), custom_call_target="tpu_custom_call" | custom-call | flops 10000000 | tf_op jit(solution)/shard_map/merge_out/pallas_call | solution.py:360
  23.6 1.6 %collective-permute-start.2 = (f32[24,1280]{1,0:T(8,128)S(1)}, f32[24,1280]{1,0:T(8,128)S(1)}, u32[]{:S(2)}, u32[]{:S(2)}) collective-permute-start(f32[24,1280]{1,0:T(8,128)S(1)} %merge_out.1.after_ref), channel_id=1, source_target_pairs={{0,1},{1,0},{2,3},{3,2},{4,5},{5,4},{6,7},{7,6},{8,9},{9,8},{10,11... | collective-permute-start | bytes 368648 | tf_op jit(solution)/shard_map/ppermute | solution.py:75
  25.1 3.3 %collective-permute-done.2 = f32[24,1280]{1,0:T(8,128)S(1)} collective-permute-done((f32[24,1280]{1,0:T(8,128)S(1)}, f32[24,1280]{1,0:T(8,128)S(1)}, u32[]{:S(2)}, u32[]{:S(2)}) %collective-permute-start.2) | collective-permute-done | bytes 122912 | tf_op jit(solution)/shard_map/ppermute | solution.py:75
  28.5 2.8 %collective-permute-start.3 = (f32[24,1280]{1,0:T(8,128)S(1)}, f32[24,1280]{1,0:T(8,128)S(1)}, u32[]{:S(2)}, u32[]{:S(2)}) collective-permute-start(f32[24,1280]{1,0:T(8,128)S(1)} %add.3.own_ref.after_ref), channel_id=1, source_target_pairs={{0,2},{1,3},{2,0},{3,1},{4,6},{5,7},{6,4},{7,5},{8,10},{9,11},{10,... | collective-permute-start | bytes 368648 | tf_op jit(solution)/shard_map/ppermute | solution.py:75
  31.3 0.0 copy-done.4
  31.3 3.3 %fetch_rows.4.refs_0_ = bf16[1536,2560]{1,0:T(8,128)(2,1)S(1)} custom-call(bf16[8000,2560]{1,0:T(8,128)(2,1)} %bitcast.6, f32[24,1280]{1,0:T(8,128)S(1)} %merge_out.1.after_ref), custom_call_target="tpu_custom_call" | custom-call | flops 15000000 | tf_op jit(solution)/shard_map/fetch_rows/pallas_call | solution.py:157
  34.7 0.0 copy-start.1
  34.7 10.6 %fetch_rows.5.refs_1_ = bf16[6464,2560]{1,0:T(8,128)(2,1)S(1)} custom-call(bf16[8000,2560]{1,0:T(8,128)(2,1)} %bitcast.7, f32[24,1280]{1,0:T(8,128)S(1)} %add.3.own_ref.after_ref), custom_call_target="tpu_custom_call" | custom-call | flops 30000000 | tf_op jit(solution)/shard_map/fetch_rows/pallas_call | solution.py:157
  45.3 0.0 collective-permute-done.3.other_ref
  45.3 0.0 copy-done.1
  45.3 0.7 finish_states.1
  46.0 5.3 %vocab_part.3.refs_2_ = f32[24,2048]{1,0:T(8,128)S(1)} custom-call(bf16[12,2560]{1,0:T(8,128)(2,1)S(1)} %get-tuple-element.21.x_ref, f32[12,128]{1,0:T(8,128)S(1)} %get-tuple-element.22.square_ref, bf16[1536,2560]{1,0:T(8,128)(2,1)S(1)} %fetch_rows.4.refs_0_, bf16[6464,2560]{1,0:T(8,128)(2,1)S(1)} %fetch_rows.5.refs_1_), custom_call_target="tpu_custom_call" | custom-call | flops 30000000 | tf_op jit(solution)/shard_map/vocab_part/pallas_call | solution.py:426
  51.2 0.0 copy-start.3
  51.3 5.5 %vocab_part.2.refs_0_ = f32[24,2048]{1,0:T(8,128)S(1)} custom-call(bf16[12,2560]{1,0:T(8,128)(2,1)S(1)} %get-tuple-element.21.x_ref, f32[12,128]{1,0:T(8,128)S(1)} %get-tuple-element.22.square_ref, bf16[1536,2560]{1,0:T(8,128)(2,1)S(1)} %fetch_rows.4.refs_0_, bf16[6464,2560]{1,0:T(8,128)(2,1)S(1)} %fetch_rows.5.refs_1_), custom_call_target="tpu_custom_call" | custom-call | flops 30000000 | tf_op jit(solution)/shard_map/vocab_part/pallas_call | solution.py:426
  56.8 1.8 %collective-permute-start.4 = (f32[24,2048]{1,0:T(8,128)S(1)}, f32[24,2048]{1,0:T(8,128)S(1)}, u32[]{:S(2)}, u32[]{:S(2)}) collective-permute-start(f32[24,2048]{1,0:T(8,128)S(1)} %vocab_part.2.refs_0_), channel_id=1, source_target_pairs={{0,4},{4,0},{1,5},{5,1},{2,6},{6,2},{3,7},{7,3},{8,12},{12,8},{9,1... | collective-permute-start | bytes 589832 | tf_op jit(solution)/shard_map/ppermute | solution.py:75
  58.6 0.2 collective-permute-start.5
  58.8 3.7 %collective-permute-done.4.refs_1_ = f32[24,2048]{1,0:T(8,128)S(1)} collective-permute-done((f32[24,2048]{1,0:T(8,128)S(1)}, f32[24,2048]{1,0:T(8,128)S(1)}, u32[]{:S(2)}, u32[]{:S(2)}) %collective-permute-start.4) | collective-permute-done | bytes 196640 | tf_op jit(solution)/shard_map/ppermute | solution.py:75
  62.5 2.1 %collective-permute-done.5.refs_3_ = f32[24,2048]{1,0:T(8,128)S(1)} collective-permute-done((f32[24,2048]{1,0:T(8,128)S(1)}, f32[24,2048]{1,0:T(8,128)S(1)}, u32[]{:S(2)}, u32[]{:S(2)}) %collective-permute-start.5) | collective-permute-done | bytes 196640 | tf_op jit(solution)/shard_map/ppermute | solution.py:75
  64.6 0.0 copy-done.3
  64.6 0.9 %vocab_logits.1 = (f32[12,8000]{1,0:T(8,128)S(1)}, f32[12,128]{1,0:T(8,128)S(1)}) custom-call(s32[12]{0:T(128)S(1)} %copy-done.3, f32[24,2048]{1,0:T(8,128)S(1)} %vocab_part.2.refs_0_, f32[24,2048]{1,0:T(8,128)S(1)} %collective-permute-done.4.refs_1_, f32[24,2048]{1,0:T(8,128)S(1)} %vocab_part.3.refs_2_, f32[24,2048]{1,0:T(8,128)S(1)} %collective-permute-done.5.refs_3_), custom_call_target="tpu_custom_call" | custom-call | flops 10000000 | tf_op jit(solution)/shard_map/vocab_logits/pallas_call | solution.py:473
  65.5 1.4 %collective-permute-start.8 = (f32[12,128]{1,0:T(8,128)S(1)}, f32[12,128]{1,0:T(8,128)S(1)}, u32[]{:S(2)}, u32[]{:S(2)}) collective-permute-start(f32[12,128]{1,0:T(8,128)S(1)} %get-tuple-element.24.refs_0_), channel_id=1, source_target_pairs={{0,3},{1,2},{2,1},{3,0},{4,7},{5,6},{6,5},{7,4},{8,11},{9,10},{10,... | collective-permute-start | bytes 18440 | tf_op jit(solution)/shard_map/ppermute | solution.py:75
  66.9 1.7 %collective-permute-start.7 = (f32[12,128]{1,0:T(8,128)S(1)}, f32[12,128]{1,0:T(8,128)S(1)}, u32[]{:S(2)}, u32[]{:S(2)}) collective-permute-start(f32[12,128]{1,0:T(8,128)S(1)} %get-tuple-element.24.refs_0_), channel_id=1, source_target_pairs={{0,2},{1,3},{2,0},{3,1},{4,6},{5,7},{6,4},{7,5},{8,10},{9,11},{10,... | collective-permute-start | bytes 18440 | tf_op jit(solution)/shard_map/ppermute | solution.py:75
  68.6 1.3 %collective-permute-start.6 = (f32[12,128]{1,0:T(8,128)S(1)}, f32[12,128]{1,0:T(8,128)S(1)}, u32[]{:S(2)}, u32[]{:S(2)}) collective-permute-start(f32[12,128]{1,0:T(8,128)S(1)} %get-tuple-element.24.refs_0_), channel_id=1, source_target_pairs={{0,1},{1,0},{2,3},{3,2},{4,5},{5,4},{6,7},{7,6},{8,9},{9,8},{10,11... | collective-permute-start | bytes 18440 | tf_op jit(solution)/shard_map/ppermute | solution.py:75
  69.9 1.1 %collective-permute-done.8.refs_3_ = f32[12,128]{1,0:T(8,128)S(1)} collective-permute-done((f32[12,128]{1,0:T(8,128)S(1)}, f32[12,128]{1,0:T(8,128)S(1)}, u32[]{:S(2)}, u32[]{:S(2)}) %collective-permute-start.8) | collective-permute-done | bytes 6176 | tf_op jit(solution)/shard_map/ppermute | solution.py:75
  71.0 0.4 collective-permute-done.7.refs_2_
  71.4 0.8 %collective-permute-done.6.refs_1_ = f32[12,128]{1,0:T(8,128)S(1)} collective-permute-done((f32[12,128]{1,0:T(8,128)S(1)}, f32[12,128]{1,0:T(8,128)S(1)}, u32[]{:S(2)}, u32[]{:S(2)}) %collective-permute-start.6) | collective-permute-done | bytes 6176 | tf_op jit(solution)/shard_map/ppermute | solution.py:75
  72.2 1.1 %vocab_finish.1 = (f32[12,8000]{1,0:T(8,128)}, f32[1,12]{1,0:T(1,128)}) custom-call(f32[12,8000]{1,0:T(8,128)S(1)} %get-tuple-element.23.logit_ref, f32[12,128]{1,0:T(8,128)S(1)} %get-tuple-element.24.refs_0_, f32[12,128]{1,0:T(8,128)S(1)} %collective-permute-done.6.refs_1_, f32[12,128]{1,0:T(8,128)S(1)} %collective-permute-done.7.refs_2_, ...), custom_call_target="tpu_custom_call" | custom-call | flops 5000000 | tf_op jit(solution)/shard_map/vocab_finish/pallas_call | solution.py:515
  (2 shorter events, 0.0 us)
Async XLA Ops:
  1.3 0.9 %copy-start = (bf16[12,2560]{1,0:T(8,128)(2,1)S(1)}, bf16[12,2560]{1,0:T(8,128)(2,1)}, u32[]{:S(2)}) copy-start(bf16[12,2560]{1,0:T(8,128)(2,1)} %x_ref.3) | copy-start | bytes 184324
  2.2 10.1 %copy-start.2 = (s32[12]{0:T(128)S(1)}, s32[12]{0:T(128)}, u32[]{:S(2)}) copy-start(s32[12]{0:T(128)} %length_ref.1) | copy-start | bytes 148
  6.5 5.9 %collective-permute-start = (f32[24,1024]{1,0:T(8,128)S(1)}, f32[24,1024]{1,0:T(8,128)S(1)}, u32[]{:S(2)}, u32[]{:S(2)}) collective-permute-start(f32[24,1024]{1,0:T(8,128)S(1)} %project.1.after_ref.own_ref), channel_id=1, source_target_pairs={{0,4},{4,0},{1,5},{5,1},{2,6},{6,2},{3,7},{7,3},{8,12},{12,8},{9,1... | collective-permute-start | bytes 294920 | tf_op jit(solution)/shard_map/ppermute | solution.py:75
  17.6 4.9 %collective-permute-start.1 = (f32[24,768]{1,0:T(8,128)S(1)}, f32[24,768]{1,0:T(8,128)S(1)}, u32[]{:S(2)}, u32[]{:S(2)}) collective-permute-start(f32[24,768]{1,0:T(8,128)S(1)} %get-tuple-element.18.after_ref.own_ref), channel_id=1, source_target_pairs={{0,4},{4,0},{1,5},{5,1},{2,6},{6,2},{3,7},{7,3},{8,12},{12,8},{9,1... | collective-permute-start | bytes 221192 | tf_op jit(solution)/shard_map/ppermute | solution.py:75
  22.5 8.8 %copy-start.4 = (f32[2560]{0:T(1024)S(1)}, f32[2560]{0:T(1024)}, u32[]{:S(2)}) copy-start(f32[2560]{0:T(1024)} %param.22) | copy-start | bytes 30724
  23.6 4.9 %collective-permute-start.2 = (f32[24,1280]{1,0:T(8,128)S(1)}, f32[24,1280]{1,0:T(8,128)S(1)}, u32[]{:S(2)}, u32[]{:S(2)}) collective-permute-start(f32[24,1280]{1,0:T(8,128)S(1)} %merge_out.1.after_ref), channel_id=1, source_target_pairs={{0,1},{1,0},{2,3},{3,2},{4,5},{5,4},{6,7},{7,6},{8,9},{9,8},{10,11... | collective-permute-start | bytes 368648 | tf_op jit(solution)/shard_map/ppermute | solution.py:75
  28.5 16.8 %collective-permute-start.3 = (f32[24,1280]{1,0:T(8,128)S(1)}, f32[24,1280]{1,0:T(8,128)S(1)}, u32[]{:S(2)}, u32[]{:S(2)}) collective-permute-start(f32[24,1280]{1,0:T(8,128)S(1)} %add.3.own_ref.after_ref), channel_id=1, source_target_pairs={{0,2},{1,3},{2,0},{3,1},{4,6},{5,7},{6,4},{7,5},{8,10},{9,11},{10,... | collective-permute-start | bytes 368648 | tf_op jit(solution)/shard_map/ppermute | solution.py:75
  34.7 10.6 %copy-start.1 = (bf16[12,2560]{1,0:T(8,128)(2,1)S(1)}, bf16[12,2560]{1,0:T(8,128)(2,1)}, u32[]{:S(2)}) copy-start(bf16[12,2560]{1,0:T(8,128)(2,1)} %x_ref.3) | copy-start | bytes 184324
  51.2 13.4 %copy-start.3 = (s32[12]{0:T(128)S(1)}, s32[12]{0:T(128)}, u32[]{:S(2)}) copy-start(s32[12]{0:T(128)} %id_ref.1) | copy-start | bytes 148
  56.8 5.7 %collective-permute-start.4 = (f32[24,2048]{1,0:T(8,128)S(1)}, f32[24,2048]{1,0:T(8,128)S(1)}, u32[]{:S(2)}, u32[]{:S(2)}) collective-permute-start(f32[24,2048]{1,0:T(8,128)S(1)} %vocab_part.2.refs_0_), channel_id=1, source_target_pairs={{0,4},{4,0},{1,5},{5,1},{2,6},{6,2},{3,7},{7,3},{8,12},{12,8},{9,1... | collective-permute-start | bytes 589832 | tf_op jit(solution)/shard_map/ppermute | solution.py:75
  58.6 6.0 %collective-permute-start.5 = (f32[24,2048]{1,0:T(8,128)S(1)}, f32[24,2048]{1,0:T(8,128)S(1)}, u32[]{:S(2)}, u32[]{:S(2)}) collective-permute-start(f32[24,2048]{1,0:T(8,128)S(1)} %vocab_part.3.refs_2_), channel_id=1, source_target_pairs={{0,4},{4,0},{1,5},{5,1},{2,6},{6,2},{3,7},{7,3},{8,12},{12,8},{9,1... | collective-permute-start | bytes 589832 | tf_op jit(solution)/shard_map/ppermute | solution.py:75
  65.5 5.5 %collective-permute-start.8 = (f32[12,128]{1,0:T(8,128)S(1)}, f32[12,128]{1,0:T(8,128)S(1)}, u32[]{:S(2)}, u32[]{:S(2)}) collective-permute-start(f32[12,128]{1,0:T(8,128)S(1)} %get-tuple-element.24.refs_0_), channel_id=1, source_target_pairs={{0,3},{1,2},{2,1},{3,0},{4,7},{5,6},{6,5},{7,4},{8,11},{9,10},{10,... | collective-permute-start | bytes 18440 | tf_op jit(solution)/shard_map/ppermute | solution.py:75
  66.9 4.5 %collective-permute-start.7 = (f32[12,128]{1,0:T(8,128)S(1)}, f32[12,128]{1,0:T(8,128)S(1)}, u32[]{:S(2)}, u32[]{:S(2)}) collective-permute-start(f32[12,128]{1,0:T(8,128)S(1)} %get-tuple-element.24.refs_0_), channel_id=1, source_target_pairs={{0,2},{1,3},{2,0},{3,1},{4,6},{5,7},{6,4},{7,5},{8,10},{9,11},{10,... | collective-permute-start | bytes 18440 | tf_op jit(solution)/shard_map/ppermute | solution.py:75
  68.6 3.7 %collective-permute-start.6 = (f32[12,128]{1,0:T(8,128)S(1)}, f32[12,128]{1,0:T(8,128)S(1)}, u32[]{:S(2)}, u32[]{:S(2)}) collective-permute-start(f32[12,128]{1,0:T(8,128)S(1)} %get-tuple-element.24.refs_0_), channel_id=1, source_target_pairs={{0,1},{1,0},{2,3},{3,2},{4,5},{5,4},{6,7},{7,6},{8,9},{9,8},{10,11... | collective-permute-start | bytes 18440 | tf_op jit(solution)/shard_map/ppermute | solution.py:75

commit v2 on v1

--- a/solution.py
+++ b/solution.py
@@ -7,9 +7,11 @@
 from jax.experimental.pallas import tpu as pltpu
 from jax.sharding import PartitionSpec as P
 
+
 HEAD_DIM = 128
 LANES = 128
 ROW_TILE = 16
+BLOCK = 256
 EPSILON = 1e-05
 NEGATIVE = -1e30
 MIB = 1 << 20
@@ -44,7 +46,7 @@
     return fold if width % (fold * LANES) == 0 else 1
 
 
-def put_folded(ref, rows, fold, start, value):
+def put_folded(ref, rows, start, value):
     width = ref.shape[1]
     done = 0
     while done < value.shape[1]:
@@ -87,7 +89,13 @@
     chunks = 5 if depth % (5 * LANES) == 0 else 1
     step = depth // chunks
 
-    def kernel(x_ref, gain_ref, wq_ref, wl_ref, out_ref, q_buf, l_buf, sems):
+    def kernel(x_hbm, gain_hbm, wq_ref, wl_ref, out_ref, x_ref, gain_ref, q_buf, l_buf, sems, ends):
+        small = [
+            pltpu.make_async_copy(x_hbm, x_ref, ends.at[0]),
+            pltpu.make_async_copy(gain_hbm, gain_ref, ends.at[1]),
+        ]
+        for copy in small:
+            copy.start()
         copies = []
         for c in range(chunks):
             at = pl.ds(c * step, step)
@@ -100,8 +108,10 @@
         for pair in copies:
             for copy in pair:
                 copy.start()
+        for copy in small:
+            copy.wait()
         states = x_ref[...].astype(jnp.float32)
-        gained = (states * gain_ref[...]).astype(jnp.bfloat16)
+        gained = (states * gain_ref[...].reshape(1, depth)).astype(jnp.bfloat16)
         square = jnp.sum(states * states, axis=1, keepdims=True)
         acc_q = acc_l = None
         for c in range(chunks):
@@ -116,53 +126,66 @@
             )
             acc_q = part_q if c == 0 else acc_q + part_q
             acc_l = part_l if c == 0 else acc_l + part_l
-        put_folded(out_ref, rows, fold, 0, acc_q)
-        put_folded(out_ref, rows, fold, q_width, acc_l)
-        put_folded(
-            out_ref, rows, fold, q_width + l_width, jnp.broadcast_to(square, (rows, LANES))
-        )
+        put_folded(out_ref, rows, 0, acc_q)
+        put_folded(out_ref, rows, q_width, acc_l)
+        put_folded(out_ref, rows, q_width + l_width, jnp.broadcast_to(square, (rows, LANES)))
 
     return pl.pallas_call(
         kernel,
         out_shape=jax.ShapeDtypeStruct((rows * fold, width // fold), jnp.float32),
-        in_specs=[VMEM, VMEM, ANY, ANY],
+        in_specs=[ANY] * 4,
         out_specs=VMEM,
         scratch_shapes=[
+            pltpu.VMEM(hidden.shape, hidden.dtype),
+            pltpu.VMEM(gain.shape, gain.dtype),
             pltpu.VMEM(w_query.shape, w_query.dtype),
             pltpu.VMEM(w_latent.shape, w_latent.dtype),
             pltpu.SemaphoreType.DMA((2, chunks)),
+            pltpu.SemaphoreType.DMA((2,)),
         ],
         compiler_params=params(14),
         cost_estimate=cost(5),
         name="project",
-    )(hidden, gain, stored(w_query), stored(w_latent))
-
-
-def fetch_rows(table, after, low, high, micros, pieces=4):
-    step = round_up(-(-(high - low) // pieces), 16)
+    )(stored(hidden), stored(gain), stored(w_query), stored(w_latent))
+
+
+def row_copies(table_ref, out_ref, sems, low, high, step):
     bounds = [(at, min(at + step, high)) for at in range(low, high, step)]
-
-    def kernel(table_ref, after_ref, out_ref, sems):
-        copies = [
-            pltpu.make_async_copy(
-                table_ref.at[pl.ds(a, b - a)], out_ref.at[pl.ds(a - low, b - a)], sems.at[i]
-            )
-            for i, (a, b) in enumerate(bounds)
-        ]
+    return [
+        pltpu.make_async_copy(
+            table_ref.at[pl.ds(a, b - a)], out_ref.at[pl.ds(a - low, b - a)], sems.at[i]
+        )
+        for i, (a, b) in enumerate(bounds)
+    ]
+
+
+def fetch_turned(table, after, low, high, micros):
+    depth = table.shape[1]
+    count = high - low
+
+    def kernel(table_ref, after_ref, out_ref, held, sems):
+        copies = row_copies(table_ref, held, sems, low, high, BLOCK)
         for copy in copies:
             copy.start()
-        for copy in copies:
+        for i, copy in enumerate(copies):
             copy.wait()
-
-    return pl.pallas_call(
-        kernel,
-        out_shape=pltpu.VMEM((high - low,) + table.shape[1:], table.dtype),
+            a, b = i * BLOCK, min((i + 1) * BLOCK, count)
+            for k in range(0, depth, BLOCK):
+                end = min(k + BLOCK, depth)
+                out_ref[k:end, a:b] = held[a:b, k:end].T
+
+    return pl.pallas_call(
+        kernel,
+        out_shape=pltpu.VMEM((depth, count), table.dtype),
         in_specs=[ANY, ANY],
         out_specs=VMEM,
-        scratch_shapes=[pltpu.SemaphoreType.DMA((len(bounds),))],
-        compiler_params=params(1),
+        scratch_shapes=[
+            pltpu.VMEM((count, depth), table.dtype),
+            pltpu.SemaphoreType.DMA((-(-count // BLOCK),)),
+        ],
+        compiler_params=params(1 + count * round_up(depth, LANES) * 2 / MIB),
         cost_estimate=cost(micros),
-        name="fetch_rows",
+        name="fetch_turned",
     )(stored(table), after)
 
 
@@ -171,7 +194,6 @@
     full = round_up(rank, LANES)
 
     def kernel(cache_ref, key_ref, value_ref, after_ref, cache_out, key_out, value_out, sems):
-        requests = cache.shape[0]
         copies = [
             pltpu.make_async_copy(key_ref, key_out, sems.at[0]),
             pltpu.make_async_copy(value_ref, value_out.at[pl.ds(full - rank, rank)], sems.at[1]),
@@ -199,7 +221,7 @@
     )(stored(cache), stored(key_up), stored(value_up), after)
 
 
-def attend(own, other, lengths, cache, key_up, value_pad, features):
+def attend(own, other, lengths, cache, key_up, value_pad, features, w_out, table, low_row, high_row):
     requests, span, width = cache.shape
     rank = width // 2
     full = value_pad.shape[0]
@@ -210,12 +232,17 @@
     q_width = heads * HEAD_DIM
     send_width = q_width + 2 * LANES
     fold = fold_of(requests, send_width)
+    tall_step = round_up(-(-(high_row - low_row) // 2), ROW_TILE)
 
     def kernel(
-        own_ref, other_ref, length_ref, cache_ref, key_ref, value_ref,
-        send_ref, local_ref, score_own, top_buf, total_buf, latent_buf, stack, *tiles,
+        own_ref, other_ref, length_ref, cache_ref, key_ref, value_ref, w_ref, table_ref,
+        send_ref, local_ref, w_held, table_held, sems, score_own, top_buf, total_buf, latent_buf, stack, *tiles,
     ):
         absorbed, mixed = tiles[: full // LANES], tiles[full // LANES :]
+        copies = row_copies(w_ref, w_held, sems.at[0], 0, w_out.shape[0], w_out.shape[0] // 2)
+        copies += row_copies(table_ref, table_held, sems.at[1], low_row, high_row, tall_step)
+        for copy in copies:
+            copy.start()
         refs = (own_ref, other_ref)
         square = get_folded(refs, requests, q_width + width, LANES)
         inv = lax.rsqrt(square[:, 0:1] / features + EPSILON)
@@ -289,13 +316,15 @@
             at = slice(j * HEAD_DIM, (j + 1) * HEAD_DIM)
             lifted = jnp.dot(stack[...], value_ref[:, at], preferred_element_type=jnp.float32)
             put_folded(
-                send_ref, requests, fold, j * HEAD_DIM,
+                send_ref, requests, j * HEAD_DIM,
                 lifted[0:requests] + lifted[second : second + requests],
             )
             local_ref[:, at] = lifted[2 * second : 2 * second + requests]
-        put_folded(send_ref, requests, fold, q_width, tops)
-        put_folded(send_ref, requests, fold, q_width + LANES, totals)
+        put_folded(send_ref, requests, q_width, tops)
+        put_folded(send_ref, requests, q_width + LANES, totals)
         local_ref[:, q_width : q_width + LANES] = owns
+        for copy in copies:
+            copy.wait()
 
     tall = requests * slot
     return pl.pallas_call(
@@ -303,10 +332,13 @@
         out_shape=(
             jax.ShapeDtypeStruct((requests * fold, send_width // fold), jnp.float32),
             jax.ShapeDtypeStruct((requests, q_width + LANES), jnp.float32),
+            pltpu.VMEM(w_out.shape, w_out.dtype),
+            pltpu.VMEM((high_row - low_row, table.shape[1]), table.dtype),
         ),
-        in_specs=[VMEM, VMEM, SMEM, VMEM, VMEM, VMEM],
-        out_specs=(VMEM, VMEM),
+        in_specs=[VMEM, VMEM, SMEM, VMEM, VMEM, VMEM, ANY, ANY],
+        out_specs=(VMEM,) * 4,
         scratch_shapes=[
+            pltpu.SemaphoreType.DMA((2, 2)),
             pltpu.VMEM((tall, LANES), jnp.float32),
             pltpu.VMEM((tall, LANES), jnp.float32),
             pltpu.VMEM((tall, LANES), jnp.float32),
@@ -317,7 +349,10 @@
         compiler_params=params(5),
         cost_estimate=cost(5),
         name="attend",
-    )(own, other, lengths, resident(cache), resident(key_up), resident(value_pad))
+    )(
+        own, other, lengths, resident(cache), resident(key_up), resident(value_pad),
+        stored(w_out), stored(table),
+    )
 
 
 def merge_out(own, other, local, w_out, requests):
@@ -353,7 +388,7 @@
         head_out = head_buf[...]
         for at in range(0, width, step):
             put_folded(
-                out_ref, requests, fold, at,
+                out_ref, requests, at,
                 jnp.dot(head_out, w_ref[:, at : at + step], preferred_element_type=jnp.float32),
             )
 
@@ -369,59 +404,89 @@
     )(own, other, local, resident(w_out))
 
 
-def finish_states(own, other, hidden, gain):
-    rows, width = hidden.shape
-
-    def kernel(own_ref, other_ref, x_ref, gain_ref, new_ref, scaled_ref, square_ref):
+def put_terms(out_ref, rows, start, x, table_ref, turned):
+    count = table_ref.shape[1] if turned else table_ref.shape[0]
+    depth = x.shape[1]
+    half = depth // 2 if depth % (2 * LANES) == 0 else depth
+    for at in range(0, count, 2 * BLOCK):
+        end = min(at + 2 * BLOCK, count)
+        total = None
+        for k in range(0, depth, half):
+            piece = x[:, k : k + half]
+            if turned:
+                term = jnp.dot(
+                    piece, table_ref[k : k + half, at:end], preferred_element_type=jnp.float32
+                )
+            else:
+                term = lax.dot_general(
+                    piece, table_ref[at:end, k : k + half], NT, preferred_element_type=jnp.float32
+                )
+            total = term if total is None else total + term
+        put_folded(out_ref, rows, start + at, total)
+
+
+def vocab_head(own, other, hidden, gain, turned, table, low_row, high_row, width):
+    rows, depth = hidden.shape
+    fold = fold_of(rows, width)
+    count = len(turned)
+    pieces = 4
+    step = round_up(-(-(high_row - low_row) // pieces), ROW_TILE)
+
+    def kernel(own_ref, other_ref, x_ref, gain_ref, *refs):
+        table_ref = refs[count]
+        new_ref, scaled_ref, square_ref, out_ref, held, sems = refs[count + 1 :]
+        copies = row_copies(table_ref, held, sems, low_row, high_row, step)
+        for copy in copies:
+            copy.start()
         states = x_ref[...].astype(jnp.float32)
-        updated = states + get_folded((own_ref, other_ref), rows, 0, width)
+        updated = states + get_folded((own_ref, other_ref), rows, 0, depth)
         new_ref[...] = updated.astype(jnp.bfloat16)
-        scaled_ref[...] = (updated * gain_ref[...]).astype(jnp.bfloat16)
+        scaled = (updated * gain_ref[...].reshape(1, depth)).astype(jnp.bfloat16)
+        scaled_ref[...] = scaled
         square_ref[...] = jnp.broadcast_to(
             jnp.sum(updated * updated, axis=1, keepdims=True), (rows, LANES)
         )
+        start = 0
+        for turned_ref in refs[:count]:
+            put_terms(out_ref, rows, start, scaled, turned_ref, True)
+            start += turned_ref.shape[1]
+        for copy in copies:
+            copy.wait()
 
     return pl.pallas_call(
         kernel,
         out_shape=(
-            jax.ShapeDtypeStruct((rows, width), jnp.bfloat16),
-            jax.ShapeDtypeStruct((rows, width), jnp.bfloat16),
+            jax.ShapeDtypeStruct((rows, depth), jnp.bfloat16),
+            jax.ShapeDtypeStruct((rows, depth), jnp.bfloat16),
             jax.ShapeDtypeStruct((rows, LANES), jnp.float32),
+            jax.ShapeDtypeStruct((rows * fold, width // fold), jnp.float32),
+            pltpu.VMEM((high_row - low_row, depth), table.dtype),
         ),
-        in_specs=[VMEM] * 4,
-        out_specs=(VMEM,) * 3,
-        compiler_params=params(2),
-        cost_estimate=cost(1),
-        name="finish_states",
-    )(own, other, hidden, gain)
-
-
-def vocab_part(scaled, square, tables, first, last, width):
+        in_specs=[VMEM] * (4 + count) + [ANY],
+        out_specs=(VMEM,) * 5,
+        scratch_shapes=[pltpu.SemaphoreType.DMA((pieces,))],
+        compiler_params=params(3),
+        cost_estimate=cost(4),
+        name="vocab_head",
+    )(own, other, hidden, gain, *[resident(part) for part in turned], stored(table))
+
+
+def vocab_tail(scaled, square, tables, width):
     rows = scaled.shape[0]
     fold = fold_of(rows, width)
-    step = 512
+    used = sum(table.shape[0] for table in tables)
 
     def kernel(x_ref, square_ref, *refs):
-        tables_in, out_ref = refs[:-1], refs[-1]
+        out_ref = refs[-1]
         x = x_ref[...]
-        base = 0
-        for table in tables_in:
-            low, high = max(first, base), min(last, base + table.shape[0])
-            for at in range(low, high, step):
-                end = min(at + step, high)
-                put_folded(
-                    out_ref, rows, fold, at - first,
-                    lax.dot_general(
-                        x, table[at - base : end - base, :], NT,
-                        preferred_element_type=jnp.float32,
-                    ),
-                )
-            base += table.shape[0]
-        if last - first < width:
-            put_folded(
-                out_ref, rows, fold, last - first,
-                jnp.broadcast_to(square_ref[:, 0:1], (rows, width - (last - first))),
-            )
+        start = 0
+        for table_ref in refs[:-1]:
+            put_terms(out_ref, rows, start, x, table_ref, False)
+            start += table_ref.shape[0]
+        put_folded(
+            out_ref, rows, used,
+            jnp.broadcast_to(square_ref[:, 0:1], (rows, width - used)),
+        )
 
     return pl.pallas_call(
         kernel,
@@ -430,7 +495,7 @@
         out_specs=VMEM,
         compiler_params=params(3),
         cost_estimate=cost(6),
-        name="vocab_part",
+        name="vocab_tail",
     )(scaled, square, *[resident(table) for table in tables])
 
 
@@ -582,9 +647,14 @@
     table = w_vocab.T
     q_width = w_query.shape[1]
 
+    def mark(share):
+        return int(columns * share) // BLOCK * BLOCK
+
+    marks = [0, mark(0.16), mark(0.336), mark(0.64), mark(0.82), columns]
+
     sums = project(
         hidden_in,
-        input_gain.reshape(1, depth),
+        input_gain,
         w_query,
         w_latent.reshape(depth, w_latent.shape[1] * w_latent.shape[2]),
     )
@@ -592,44 +662,36 @@
     cache, keys, values = fetch_attention(
         latent_cache[:, 0], key_up[0], value_up[0], sums, 3
     )
-    marks = [0]
-    for share in (0.25, 0.55):
-        marks.append(int(columns * share) // 512 * 512)
-    marks.append(columns)
-
-    packed, local = attend(own, other, lengths, cache, keys, values, features)
+    packed, local, out_table, stored_part = attend(
+        own, other, lengths, cache, keys, values, features, w_out, table, marks[3], marks[4]
+    )
     own, other = pair_softmax(packed, "seq", rows, q_width)
-    out_table = fetch_rows(w_out, packed, 0, w_out.shape[0], 3)
+    turned = [fetch_turned(table, packed, marks[0], marks[1], 3)]
     part = merge_out(own, other, local, out_table, rows)
 
     heads = lax.axis_size("heads")
-    tables = []
+    first = part
     if is_power(heads) and heads > 1:
         mask = 1
-        level = 0
         while True:
             received = swap(part, "heads", mask)
             mask *= 2
             if mask >= heads:
                 break
-            tables.append(fetch_rows(table, part, marks[level], marks[level + 1], 3))
-            level += 1
             part = part + received
     else:
-        level = 0
         part, received = lax.psum(part, "heads"), jnp.zeros_like(part)
-    tables.append(fetch_rows(table, part, marks[level], columns, 6, 8))
-
-    new_hidden, scaled, square = finish_states(
-        part, received, hidden_in, final_gain.reshape(1, depth)
+    turned.append(fetch_turned(table, first, marks[1], marks[2], 3))
+    turned.append(fetch_turned(table, part, marks[2], marks[3], 6))
+
+    bounds = [(0, marks[3]), (marks[3], columns)]
+    tail_width = round_up(columns - marks[3] + LANES, 2 * LANES)
+    new_hidden, scaled, square, piece, late_part = vocab_head(
+        part, received, hidden_in, final_gain, turned, table, marks[4], columns, marks[3]
     )
-    chunk = round_up(-(-columns // 2), 512)
-    bounds = [(0, min(chunk, columns)), (chunk, columns)]
-    parts = []
-    for first, last in bounds:
-        width = round_up(last - first + (LANES if last == columns else 0), 2 * LANES)
-        piece = vocab_part(scaled, square, tables, first, last, width)
-        parts.append(pair_sum(piece, "seq"))
+    parts = [pair_sum(piece, "seq")]
+    piece = vocab_tail(scaled, square, [stored_part, late_part], tail_width)
+    parts.append(pair_sum(piece, "seq"))
     logits, stats = vocab_logits(parts, draft_ids, bounds, rows, features)
     if is_power(heads):
         every = [stats] + [swap(stats, "heads", m) for m in range(1, heads)]

time: 73.6 us -> 70.4 us (0.957)
  Pallas kernels: 43.6 us -> 40.1 us
  local copies, waits for them, and re-layouts: 1.63 us -> 0.02 us
  starting transfers between devices: 15.8 us -> 17 us
  waiting for transfers between devices: 11.5 us -> 12.4 us
    pallas_call x6 -> x5, Pallas kernels: 28.3 us -> 21.8 us  [the longest x3 12 us: fetch_turned(): pl.pallas_call(kernel, out_shape=pltpu.VMEM((depth, count), table.dtype),...]
    pallas_call x1, Pallas kernels: 5.26 us -> 7.09 us  [attend(): pl.pallas_call(kernel, out_shape=(jax.ShapeDtypeStruct((requests * fold,...]
    pallas_call x1, Pallas kernels: 4.27 us -> 5.54 us  [project(): pl.pallas_call(kernel, out_shape=jax.ShapeDtypeStruct((rows * fold, width...]
    ppermute x9, starting transfers between devices: 15.8 us -> 17 us  [swap(): return lax.ppermute(array, axis, [(i, i ^ mask) for i in range(size)])]
    unnamed x10 -> x8, local copies, waits for them, and re-layouts: 0.91 us -> 0.02 us
    ppermute x9, waiting for transfers between devices: 11.5 us -> 12.4 us  [swap(): return lax.ppermute(array, axis, [(i, i ^ mask) for i in range(size)])]
  transfers between devices with their start and end apart: 9 -> 9, of which waited for: 7 -> 6; matrix products, arithmetic and copies ran while one was open for 0% -> 0% of each run, Pallas kernels for 27% -> 26%
where the time goes in v2:
time: 70.4 us; the launch traced here: 70.3 us
  Pallas kernels  40.1 us (57%)
  starting transfers between devices  17 us (24%)
  waiting for transfers between devices  12.4 us (18%)
  between operations  0.75 us (1%)
    ppermute x9, starting transfers between devices, swap(): return lax.ppermute(array, axis, [(i, i ^ mask) for i in range(size)])  17 us
    ppermute x9, waiting for transfers between devices, swap(): return lax.ppermute(array, axis, [(i, i ^ mask) for i in range(size)])  12.4 us
    pallas_call x3, Pallas kernels, fetch_turned(): pl.pallas_call(kernel, out_shape=pltpu.VMEM((depth, count), table.dtype),...  12 us
    pallas_call x1, Pallas kernels, attend(): pl.pallas_call(kernel, out_shape=(jax.ShapeDtypeStruct((requests * fold,...  7.09 us
    pallas_call x1, Pallas kernels, vocab_head(): pl.pallas_call(kernel, out_shape=(jax.ShapeDtypeStruct((rows, depth), jnp...  5.85 us
    pallas_call x1, Pallas kernels, project(): pl.pallas_call(kernel, out_shape=jax.ShapeDtypeStruct((rows * fold, width...  5.54 us
    pallas_call x1, Pallas kernels, vocab_tail(): pl.pallas_call(kernel, out_shape=jax.ShapeDtypeStruct((rows * fold, width...  3.9 us
    pallas_call x1, Pallas kernels, fetch_attention(): pl.pallas_call(kernel, out_shape=(pltpu.VMEM(cache.shape, cache.dtype), p...  2.65 us
  transfers between devices with their start and end apart: 9, of which 6 were waited for; matrix products, arithmetic and copies ran while one was open for 0% of the time, Pallas kernels for 26%

profile of v2, /device:TPU:0, one launch (start us, length us, event | category | flops | bytes accessed | tf_op | source)
XLA Modules:
  0.0 70.3 jit_solution(14560937690572938472)
XLA Ops:
  0.6 0.0 copy-start.2
  0.6 5.5 %project.1.after_ref.own_ref = f32[24,1024]{1,0:T(8,128)S(1)} custom-call(bf16[12,2560]{1,0:T(8,128)(2,1)} %x_ref.1, f32[2560]{0:T(1024)} %gain_hbm.1, bf16[2560,1280]{1,0:T(8,128)(2,1)} %wq_ref.1, bf16[2560,640]{1,0:T(8,128)(2,1)} %bitcast.12), custom_call_target="tpu_custom_call" | custom-call | flops 25000000 | tf_op jit(solution)/shard_map/project/pallas_call | solution.py:133
  6.2 3.1 %collective-permute-start = (f32[24,1024]{1,0:T(8,128)S(1)}, f32[24,1024]{1,0:T(8,128)S(1)}, u32[]{:S(2)}, u32[]{:S(2)}) collective-permute-start(f32[24,1024]{1,0:T(8,128)S(1)} %project.1.after_ref.own_ref), channel_id=1, source_target_pairs={{0,4},{4,0},{1,5},{5,1},{2,6},{6,2},{3,7},{7,3},{8,12},{12,8},{9,1... | collective-permute-start | bytes 294920 | tf_op jit(solution)/shard_map/ppermute | solution.py:77
  9.3 2.6 %fetch_attention.1 = (bf16[12,256,640]{2,1,0:T(8,128)(2,1)S(1)}, bf16[320,1280]{1,0:T(8,128)(2,1)S(1)}, bf16[384,1280]{1,0:T(8,128)(2,1)S(1)}) custom-call(bf16[12,256,640]{2,1,0:T(8,128)(2,1)} %bitcast.11, bf16[320,1280]{1,0:T(8,128)(2,1)} %bitcast.13, bf16[320,1280]{1,0:T(8,128)(2,1)} %bitcast.14, f32[24,1024]{1,0:T(8,128)S(1)} %project.1.after_ref.own_ref), custom_call_target="tpu_custom_call" | custom-call | flops 15000000 | tf_op jit(solution)/shard_map/fetch_attention/pallas_call | solution.py:208
  11.9 0.1 collective-permute-done.other_ref
  12.0 0.0 copy-done.2
  12.1 7.1 %attend.1 = (f32[24,768]{1,0:T(8,128)S(1)}, f32[12,1408]{1,0:T(8,128)S(1)}, bf16[1280,2560]{1,0:T(8,128)(2,1)S(1)}, bf16[1280,2560]{1,0:T(8,128)(2,1)S(1)}) custom-call(f32[24,1024]{1,0:T(8,128)S(1)} %project.1.after_ref.own_ref, f32[24,1024]{1,0:T(8,128)S(1)} %collective-permute-done.other_ref, s32[12]{0:T(128)S(1)} %copy-done.2, ...), custom_call_target="tpu_custom_call" | custom-call | flops 25000000 | tf_op jit(solution)/shard_map/attend/pallas_call | solution.py:330
  19.2 1.9 %collective-permute-start.1 = (f32[24,768]{1,0:T(8,128)S(1)}, f32[24,768]{1,0:T(8,128)S(1)}, u32[]{:S(2)}, u32[]{:S(2)}) collective-permute-start(f32[24,768]{1,0:T(8,128)S(1)} %get-tuple-element.22.own_ref.after_ref), channel_id=1, source_target_pairs={{0,4},{4,0},{1,5},{5,1},{2,6},{6,2},{3,7},{7,3},{8,12},{12,8},{9,1... | collective-permute-start | bytes 221192 | tf_op jit(solution)/shard_map/ppermute | solution.py:77
  21.0 2.5 %collective-permute-done.1.other_ref = f32[24,768]{1,0:T(8,128)S(1)} collective-permute-done((f32[24,768]{1,0:T(8,128)S(1)}, f32[24,768]{1,0:T(8,128)S(1)}, u32[]{:S(2)}, u32[]{:S(2)}) %collective-permute-start.1) | collective-permute-done | bytes 73760 | tf_op jit(solution)/shard_map/ppermute | solution.py:77
  23.6 1.1 %merge_out.1.after_ref = f32[24,1280]{1,0:T(8,128)S(1)} custom-call(f32[24,768]{1,0:T(8,128)S(1)} %get-tuple-element.22.own_ref.after_ref, f32[24,768]{1,0:T(8,128)S(1)} %collective-permute-done.1.other_ref, f32[12,1408]{1,0:T(8,128)S(1)} %get-tuple-element.23.local_ref, bf16[1280,2560]{1,0:T(8,128)(2,1)S(1)} %get-tuple-element.24.w_ref), custom_call_target="tpu_custom_call" | custom-call | flops 10000000 | tf_op jit(solution)/shard_map/merge_out/pallas_call | solution.py:395
  24.6 1.9 %collective-permute-start.2 = (f32[24,1280]{1,0:T(8,128)S(1)}, f32[24,1280]{1,0:T(8,128)S(1)}, u32[]{:S(2)}, u32[]{:S(2)}) collective-permute-start(f32[24,1280]{1,0:T(8,128)S(1)} %merge_out.1.after_ref), channel_id=1, source_target_pairs={{0,1},{1,0},{2,3},{3,2},{4,5},{5,4},{6,7},{7,6},{8,9},{9,8},{10,11... | collective-permute-start | bytes 368648 | tf_op jit(solution)/shard_map/ppermute | solution.py:77
  26.5 3.0 %collective-permute-done.2 = f32[24,1280]{1,0:T(8,128)S(1)} collective-permute-done((f32[24,1280]{1,0:T(8,128)S(1)}, f32[24,1280]{1,0:T(8,128)S(1)}, u32[]{:S(2)}, u32[]{:S(2)}) %collective-permute-start.2) | collective-permute-done | bytes 122912 | tf_op jit(solution)/shard_map/ppermute | solution.py:77
  29.5 3.6 %collective-permute-start.3 = (f32[24,1280]{1,0:T(8,128)S(1)}, f32[24,1280]{1,0:T(8,128)S(1)}, u32[]{:S(2)}, u32[]{:S(2)}) collective-permute-start(f32[24,1280]{1,0:T(8,128)S(1)} %add.3.after_ref.own_ref), channel_id=1, source_target_pairs={{0,2},{1,3},{2,0},{3,1},{4,6},{5,7},{6,4},{7,5},{8,10},{9,11},{10,... | collective-permute-start | bytes 368648 | tf_op jit(solution)/shard_map/ppermute | solution.py:77
  33.1 3.3 %fetch_turned.3.refs_0_ = bf16[2560,1280]{1,0:T(8,128)(2,1)S(1)} custom-call(bf16[8000,2560]{1,0:T(8,128)(2,1)} %bitcast.7, f32[24,768]{1,0:T(8,128)S(1)} %get-tuple-element.22.own_ref.after_ref), custom_call_target="tpu_custom_call" | custom-call | flops 15000000 | tf_op jit(solution)/shard_map/fetch_turned/pallas_call | solution.py:177
  36.4 3.3 %fetch_turned.4.refs_1_ = bf16[2560,1280]{1,0:T(8,128)(2,1)S(1)} custom-call(bf16[8000,2560]{1,0:T(8,128)(2,1)} %bitcast.8, f32[24,1280]{1,0:T(8,128)S(1)} %merge_out.1.after_ref), custom_call_target="tpu_custom_call" | custom-call | flops 15000000 | tf_op jit(solution)/shard_map/fetch_turned/pallas_call | solution.py:177
  39.8 0.0 copy-start
  39.8 0.0 copy-start.1
  39.8 5.4 %fetch_turned.5.refs_2_ = bf16[2560,2560]{1,0:T(8,128)(2,1)S(1)} custom-call(bf16[8000,2560]{1,0:T(8,128)(2,1)} %bitcast.9, f32[24,1280]{1,0:T(8,128)S(1)} %add.3.after_ref.own_ref), custom_call_target="tpu_custom_call" | custom-call | flops 30000000 | tf_op jit(solution)/shard_map/fetch_turned/pallas_call | solution.py:177
  45.2 0.0 collective-permute-done.3.other_ref
  45.2 0.0 copy-done
  45.2 0.0 copy-done.1
  45.2 5.9 %vocab_head.1 = (bf16[12,2560]{1,0:T(8,128)(2,1)}, bf16[12,2560]{1,0:T(8,128)(2,1)S(1)}, f32[12,128]{1,0:T(8,128)S(1)}, f32[24,2560]{1,0:T(8,128)S(1)}, bf16[1600,2560]{1,0:T(8,128)(2,1)S(1)}) custom-call(f32[24,1280]{1,0:T(8,128)S(1)} %add.3.after_ref.own_ref, f32[24,1280]{1,0:T(8,128)S(1)} %collective-permute-done.3.other_ref, ...), custom_call_target="tpu_custom_call" | custom-call | flops 20000000 | tf_op jit(solution)/shard_map/vocab_head/pallas_call | solution.py:456
  51.1 2.0 %collective-permute-start.4 = (f32[24,2560]{1,0:T(8,128)S(1)}, f32[24,2560]{1,0:T(8,128)S(1)}, u32[]{:S(2)}, u32[]{:S(2)}) collective-permute-start(f32[24,2560]{1,0:T(8,128)S(1)} %get-tuple-element.26.refs_0_), channel_id=1, source_target_pairs={{0,4},{4,0},{1,5},{5,1},{2,6},{6,2},{3,7},{7,3},{8,12},{12,8},{9,1... | collective-permute-start | bytes 737288 | tf_op jit(solution)/shard_map/ppermute | solution.py:77
  53.1 0.0 copy-start.3
  53.1 3.9 %vocab_tail.1.refs_2_ = f32[24,1536]{1,0:T(8,128)S(1)} custom-call(bf16[12,2560]{1,0:T(8,128)(2,1)S(1)} %get-tuple-element.27.x_ref, f32[12,128]{1,0:T(8,128)S(1)} %get-tuple-element.28.square_ref, bf16[1280,2560]{1,0:T(8,128)(2,1)S(1)} %get-tuple-element.29.refs_0_, bf16[1600,2560]{1,0:T(8,128)(2,1)S(1)} %get-tuple-element.30.refs_1_), custom_call_target="tpu_custom_call" | custom-call | flops 30000000 | tf_op jit(solution)/shard_map/vocab_tail/pallas_call | solution.py:491
  57.0 0.1 collective-permute-start.5
  57.1 5.1 %collective-permute-done.5.refs_3_ = f32[24,1536]{1,0:T(8,128)S(1)} collective-permute-done((f32[24,1536]{1,0:T(8,128)S(1)}, f32[24,1536]{1,0:T(8,128)S(1)}, u32[]{:S(2)}, u32[]{:S(2)}) %collective-permute-start.5) | collective-permute-done | bytes 147488 | tf_op jit(solution)/shard_map/ppermute | solution.py:77
  62.2 0.0 collective-permute-done.4.refs_1_
  62.2 0.0 copy-done.3
  62.2 0.9 %vocab_logits.1 = (f32[12,8000]{1,0:T(8,128)S(1)}, f32[12,128]{1,0:T(8,128)S(1)}) custom-call(s32[12]{0:T(128)S(1)} %copy-done.3, f32[24,2560]{1,0:T(8,128)S(1)} %get-tuple-element.26.refs_0_, f32[24,2560]{1,0:T(8,128)S(1)} %collective-permute-done.4.refs_1_, f32[24,1536]{1,0:T(8,128)S(1)} %vocab_tail.1.refs_2_, f32[24,1536]{1,0:T(8,128)S(1)} %collective-permute-done.5.refs_3_), custom_call_target="tpu_custom_call" | custom-call | flops 10000000 | tf_op jit(solution)/shard_map/vocab_logits/pallas_call | solution.py:538
  63.1 0.3 collective-permute-start.8
  63.4 1.7 %collective-permute-start.7 = (f32[12,128]{1,0:T(8,128)S(1)}, f32[12,128]{1,0:T(8,128)S(1)}, u32[]{:S(2)}, u32[]{:S(2)}) collective-permute-start(f32[12,128]{1,0:T(8,128)S(1)} %get-tuple-element.32.refs_0_), channel_id=1, source_target_pairs={{0,2},{1,3},{2,0},{3,1},{4,6},{5,7},{6,4},{7,5},{8,10},{9,11},{10,... | collective-permute-start | bytes 18440 | tf_op jit(solution)/shard_map/ppermute | solution.py:77
  65.1 2.4 %collective-permute-start.6 = (f32[12,128]{1,0:T(8,128)S(1)}, f32[12,128]{1,0:T(8,128)S(1)}, u32[]{:S(2)}, u32[]{:S(2)}) collective-permute-start(f32[12,128]{1,0:T(8,128)S(1)} %get-tuple-element.32.refs_0_), channel_id=1, source_target_pairs={{0,1},{1,0},{2,3},{3,2},{4,5},{5,4},{6,7},{7,6},{8,9},{9,8},{10,11... | collective-permute-start | bytes 18440 | tf_op jit(solution)/shard_map/ppermute | solution.py:77
  67.5 1.1 %collective-permute-done.8.refs_3_ = f32[12,128]{1,0:T(8,128)S(1)} collective-permute-done((f32[12,128]{1,0:T(8,128)S(1)}, f32[12,128]{1,0:T(8,128)S(1)}, u32[]{:S(2)}, u32[]{:S(2)}) %collective-permute-start.8) | collective-permute-done | bytes 6176 | tf_op jit(solution)/shard_map/ppermute | solution.py:77
  68.6 0.0 collective-permute-done.7.refs_2_
  68.6 0.6 collective-permute-done.6.refs_1_
  69.1 1.1 %vocab_finish.1 = (f32[12,8000]{1,0:T(8,128)}, f32[1,12]{1,0:T(1,128)}) custom-call(f32[12,8000]{1,0:T(8,128)S(1)} %get-tuple-element.31.logit_ref, f32[12,128]{1,0:T(8,128)S(1)} %get-tuple-element.32.refs_0_, f32[12,128]{1,0:T(8,128)S(1)} %collective-permute-done.6.refs_1_, f32[12,128]{1,0:T(8,128)S(1)} %collective-permute-done.7.refs_2_, ...), custom_call_target="tpu_custom_call" | custom-call | flops 5000000 | tf_op jit(solution)/shard_map/vocab_finish/pallas_call | solution.py:580
  (1 shorter events, 0.0 us)
Async XLA Ops:
  0.6 11.4 %copy-start.2 = (s32[12]{0:T(128)S(1)}, s32[12]{0:T(128)}, u32[]{:S(2)}) copy-start(s32[12]{0:T(128)} %length_ref.1) | copy-start | bytes 148
  6.2 5.9 %collective-permute-start = (f32[24,1024]{1,0:T(8,128)S(1)}, f32[24,1024]{1,0:T(8,128)S(1)}, u32[]{:S(2)}, u32[]{:S(2)}) collective-permute-start(f32[24,1024]{1,0:T(8,128)S(1)} %project.1.after_ref.own_ref), channel_id=1, source_target_pairs={{0,4},{4,0},{1,5},{5,1},{2,6},{6,2},{3,7},{7,3},{8,12},{12,8},{9,1... | collective-permute-start | bytes 294920 | tf_op jit(solution)/shard_map/ppermute | solution.py:77
  19.2 4.4 %collective-permute-start.1 = (f32[24,768]{1,0:T(8,128)S(1)}, f32[24,768]{1,0:T(8,128)S(1)}, u32[]{:S(2)}, u32[]{:S(2)}) collective-permute-start(f32[24,768]{1,0:T(8,128)S(1)} %get-tuple-element.22.own_ref.after_ref), channel_id=1, source_target_pairs={{0,4},{4,0},{1,5},{5,1},{2,6},{6,2},{3,7},{7,3},{8,12},{12,8},{9,1... | collective-permute-start | bytes 221192 | tf_op jit(solution)/shard_map/ppermute | solution.py:77
  24.6 4.9 %collective-permute-start.2 = (f32[24,1280]{1,0:T(8,128)S(1)}, f32[24,1280]{1,0:T(8,128)S(1)}, u32[]{:S(2)}, u32[]{:S(2)}) collective-permute-start(f32[24,1280]{1,0:T(8,128)S(1)} %merge_out.1.after_ref), channel_id=1, source_target_pairs={{0,1},{1,0},{2,3},{3,2},{4,5},{5,4},{6,7},{7,6},{8,9},{9,8},{10,11... | collective-permute-start | bytes 368648 | tf_op jit(solution)/shard_map/ppermute | solution.py:77
  29.5 15.6 %collective-permute-start.3 = (f32[24,1280]{1,0:T(8,128)S(1)}, f32[24,1280]{1,0:T(8,128)S(1)}, u32[]{:S(2)}, u32[]{:S(2)}) collective-permute-start(f32[24,1280]{1,0:T(8,128)S(1)} %add.3.after_ref.own_ref), channel_id=1, source_target_pairs={{0,2},{1,3},{2,0},{3,1},{4,6},{5,7},{6,4},{7,5},{8,10},{9,11},{10,... | collective-permute-start | bytes 368648 | tf_op jit(solution)/shard_map/ppermute | solution.py:77
  39.8 5.4 %copy-start = (bf16[12,2560]{1,0:T(8,128)(2,1)S(1)}, bf16[12,2560]{1,0:T(8,128)(2,1)}, u32[]{:S(2)}) copy-start(bf16[12,2560]{1,0:T(8,128)(2,1)} %x_ref.1) | copy-start | bytes 184324
  39.8 5.4 %copy-start.1 = (f32[2560]{0:T(1024)S(1)}, f32[2560]{0:T(1024)}, u32[]{:S(2)}) copy-start(f32[2560]{0:T(1024)} %gain_ref.1) | copy-start | bytes 30724
  51.1 11.2 %collective-permute-start.4 = (f32[24,2560]{1,0:T(8,128)S(1)}, f32[24,2560]{1,0:T(8,128)S(1)}, u32[]{:S(2)}, u32[]{:S(2)}) collective-permute-start(f32[24,2560]{1,0:T(8,128)S(1)} %get-tuple-element.26.refs_0_), channel_id=1, source_target_pairs={{0,4},{4,0},{1,5},{5,1},{2,6},{6,2},{3,7},{7,3},{8,12},{12,8},{9,1... | collective-permute-start | bytes 737288 | tf_op jit(solution)/shard_map/ppermute | solution.py:77
  53.1 9.1 %copy-start.3 = (s32[12]{0:T(128)S(1)}, s32[12]{0:T(128)}, u32[]{:S(2)}) copy-start(s32[12]{0:T(128)} %id_ref.1) | copy-start | bytes 148
  57.0 5.2 %collective-permute-start.5 = (f32[24,1536]{1,0:T(8,128)S(1)}, f32[24,1536]{1,0:T(8,128)S(1)}, u32[]{:S(2)}, u32[]{:S(2)}) collective-permute-start(f32[24,1536]{1,0:T(8,128)S(1)} %vocab_tail.1.refs_2_), channel_id=1, source_target_pairs={{0,4},{4,0},{1,5},{5,1},{2,6},{6,2},{3,7},{7,3},{8,12},{12,8},{9,1... | collective-permute-start | bytes 442376 | tf_op jit(solution)/shard_map/ppermute | solution.py:77
  63.1 5.5 %collective-permute-start.8 = (f32[12,128]{1,0:T(8,128)S(1)}, f32[12,128]{1,0:T(8,128)S(1)}, u32[]{:S(2)}, u32[]{:S(2)}) collective-permute-start(f32[12,128]{1,0:T(8,128)S(1)} %get-tuple-element.32.refs_0_), channel_id=1, source_target_pairs={{0,3},{1,2},{2,1},{3,0},{4,7},{5,6},{6,5},{7,4},{8,11},{9,10},{10,... | collective-permute-start | bytes 18440 | tf_op jit(solution)/shard_map/ppermute | solution.py:77
  63.4 5.2 %collective-permute-start.7 = (f32[12,128]{1,0:T(8,128)S(1)}, f32[12,128]{1,0:T(8,128)S(1)}, u32[]{:S(2)}, u32[]{:S(2)}) collective-permute-start(f32[12,128]{1,0:T(8,128)S(1)} %get-tuple-element.32.refs_0_), channel_id=1, source_target_pairs={{0,2},{1,3},{2,0},{3,1},{4,6},{5,7},{6,4},{7,5},{8,10},{9,11},{10,... | collective-permute-start | bytes 18440 | tf_op jit(solution)/shard_map/ppermute | solution.py:77
  65.1 4.0 %collective-permute-start.6 = (f32[12,128]{1,0:T(8,128)S(1)}, f32[12,128]{1,0:T(8,128)S(1)}, u32[]{:S(2)}, u32[]{:S(2)}) collective-permute-start(f32[12,128]{1,0:T(8,128)S(1)} %get-tuple-element.32.refs_0_), channel_id=1, source_target_pairs={{0,1},{1,0},{2,3},{3,2},{4,5},{5,4},{6,7},{7,6},{8,9},{9,8},{10,11... | collective-permute-start | bytes 18440 | tf_op jit(solution)/shard_map/ppermute | solution.py:77

commit v3 on v2

--- a/solution.py
+++ b/solution.py
@@ -77,6 +77,11 @@
     return lax.ppermute(array, axis, [(i, i ^ mask) for i in range(size)])
 
 
+def fence(sem):
+    pl.semaphore_signal(sem, 1)
+    pl.semaphore_wait(sem, 1)
+
+
 def is_power(size):
     return size & (size - 1) == 0
 
@@ -89,13 +94,14 @@
     chunks = 5 if depth % (5 * LANES) == 0 else 1
     step = depth // chunks
 
-    def kernel(x_hbm, gain_hbm, wq_ref, wl_ref, out_ref, x_ref, gain_ref, q_buf, l_buf, sems, ends):
+    def kernel(x_hbm, gain_hbm, wq_ref, wl_ref, out_ref, x_ref, gain_ref, q_buf, l_buf, sems, ends, gate):
         small = [
             pltpu.make_async_copy(x_hbm, x_ref, ends.at[0]),
             pltpu.make_async_copy(gain_hbm, gain_ref, ends.at[1]),
         ]
         for copy in small:
             copy.start()
+        fence(gate)
         copies = []
         for c in range(chunks):
             at = pl.ds(c * step, step)
@@ -142,6 +148,7 @@
             pltpu.VMEM(w_latent.shape, w_latent.dtype),
             pltpu.SemaphoreType.DMA((2, chunks)),
             pltpu.SemaphoreType.DMA((2,)),
+            pltpu.SemaphoreType.REGULAR,
         ],
         compiler_params=params(14),
         cost_estimate=cost(5),
@@ -221,28 +228,28 @@
     )(stored(cache), stored(key_up), stored(value_up), after)
 
 
-def attend(own, other, lengths, cache, key_up, value_pad, features, w_out, table, low_row, high_row):
+def attend(own, other, lengths, cache, key_up, value_pad, features, w_out):
     requests, span, width = cache.shape
     rank = width // 2
     full = value_pad.shape[0]
     low = width - full
     heads = key_up.shape[1] // HEAD_DIM
-    slot = round_up(heads, 8)
+    slot = round_up(heads, ROW_TILE)
     scaling = 1.0 / math.sqrt(HEAD_DIM)
     q_width = heads * HEAD_DIM
     send_width = q_width + 2 * LANES
     fold = fold_of(requests, send_width)
-    tall_step = round_up(-(-(high_row - low_row) // 2), ROW_TILE)
 
     def kernel(
-        own_ref, other_ref, length_ref, cache_ref, key_ref, value_ref, w_ref, table_ref,
-        send_ref, local_ref, w_held, table_held, sems, score_own, top_buf, total_buf, latent_buf, stack, *tiles,
+        own_ref, other_ref, length_ref, cache_ref, key_ref, value_ref, w_ref,
+        send_ref, local_ref, w_held, sems, gate, score_own, top_buf, total_buf, latent_buf, stack,
+        score_buf, weight_buf, *tiles,
     ):
         absorbed, mixed = tiles[: full // LANES], tiles[full // LANES :]
-        copies = row_copies(w_ref, w_held, sems.at[0], 0, w_out.shape[0], w_out.shape[0] // 2)
-        copies += row_copies(table_ref, table_held, sems.at[1], low_row, high_row, tall_step)
+        copies = row_copies(w_ref, w_held, sems, 0, w_out.shape[0], w_out.shape[0] // 2)
         for copy in copies:
             copy.start()
+        fence(gate)
         refs = (own_ref, other_ref)
         square = get_folded(refs, requests, q_width + width, LANES)
         inv = lax.rsqrt(square[:, 0:1] / features + EPSILON)
@@ -265,34 +272,32 @@
                 tile[pl.ds(j, requests, stride=slot), :] = piece
         first = lax.axis_index("seq") * span
         positions = first + lax.broadcasted_iota(jnp.int32, (slot, span), 1)
-        for b in range(requests):
-            at = slice(b * slot, (b + 1) * slot)
+        spans = [slice(b * slot, (b + 1) * slot) for b in range(requests)]
+        for b, at in enumerate(spans):
             rows = jnp.concatenate([tile[at, :] for tile in absorbed], axis=1)
+            score_buf[at, :] = lax.dot_general(
+                rows.astype(jnp.bfloat16),
+                cache_ref[b, :, 0:full],
+                NT,
+                preferred_element_type=jnp.float32,
+            )
             score_own[at, :] = jnp.broadcast_to(
                 jnp.sum(rows * latent_buf[b : b + 1, 0:full], axis=1, keepdims=True) * scaling,
                 (slot, LANES),
             )
-            scores = (
-                lax.dot_general(
-                    rows.astype(jnp.bfloat16),
-                    cache_ref[b, :, 0:full],
-                    NT,
-                    preferred_element_type=jnp.float32,
-                )
-                * scaling
-            )
+        for b, at in enumerate(spans):
             live = positions < length_ref[b]
-            scores = jnp.where(live, scores, NEGATIVE)
+            scores = jnp.where(live, score_buf[at, :] * scaling, NEGATIVE)
             top = jnp.max(scores, axis=1, keepdims=True)
             weights = jnp.where(live, jnp.exp(scores - top), 0.0)
             top_buf[at, :] = jnp.broadcast_to(top, (slot, LANES))
             total_buf[at, :] = jnp.broadcast_to(
                 jnp.sum(weights, axis=1, keepdims=True), (slot, LANES)
             )
+            weight_buf[at, :] = weights.astype(jnp.bfloat16)
+        for b, at in enumerate(spans):
             value = jnp.dot(
-                weights.astype(jnp.bfloat16),
-                cache_ref[b, :, low:width],
-                preferred_element_type=jnp.float32,
+                weight_buf[at, :], cache_ref[b, :, low:width], preferred_element_type=jnp.float32
             )
             for i, tile in enumerate(mixed):
                 tile[at, :] = value[:, i * LANES : (i + 1) * LANES]
@@ -333,17 +338,19 @@
             jax.ShapeDtypeStruct((requests * fold, send_width // fold), jnp.float32),
             jax.ShapeDtypeStruct((requests, q_width + LANES), jnp.float32),
             pltpu.VMEM(w_out.shape, w_out.dtype),
-            pltpu.VMEM((high_row - low_row, table.shape[1]), table.dtype),
         ),
-        in_specs=[VMEM, VMEM, SMEM, VMEM, VMEM, VMEM, ANY, ANY],
-        out_specs=(VMEM,) * 4,
+        in_specs=[VMEM, VMEM, SMEM, VMEM, VMEM, VMEM, ANY],
+        out_specs=(VMEM,) * 3,
         scratch_shapes=[
-            pltpu.SemaphoreType.DMA((2, 2)),
+            pltpu.SemaphoreType.DMA((2,)),
+            pltpu.SemaphoreType.REGULAR,
             pltpu.VMEM((tall, LANES), jnp.float32),
             pltpu.VMEM((tall, LANES), jnp.float32),
             pltpu.VMEM((tall, LANES), jnp.float32),
             pltpu.VMEM((requests, width), jnp.float32),
             pltpu.VMEM((3 * round_up(requests, ROW_TILE), full), jnp.bfloat16),
+            pltpu.VMEM((tall, span), jnp.float32),
+            pltpu.VMEM((tall, span), jnp.bfloat16),
         ]
         + [pltpu.VMEM((tall, LANES), jnp.float32)] * (2 * full // LANES),
         compiler_params=params(5),
@@ -351,7 +358,7 @@
         name="attend",
     )(
         own, other, lengths, resident(cache), resident(key_up), resident(value_pad),
-        stored(w_out), stored(table),
+        stored(w_out),
     )
 
 
@@ -434,10 +441,11 @@
 
     def kernel(own_ref, other_ref, x_ref, gain_ref, *refs):
         table_ref = refs[count]
-        new_ref, scaled_ref, square_ref, out_ref, held, sems = refs[count + 1 :]
+        new_ref, scaled_ref, square_ref, out_ref, held, sems, gate = refs[count + 1 :]
         copies = row_copies(table_ref, held, sems, low_row, high_row, step)
         for copy in copies:
             copy.start()
+        fence(gate)
         states = x_ref[...].astype(jnp.float32)
         updated = states + get_folded((own_ref, other_ref), rows, 0, depth)
         new_ref[...] = updated.astype(jnp.bfloat16)
@@ -464,25 +472,33 @@
         ),
         in_specs=[VMEM] * (4 + count) + [ANY],
         out_specs=(VMEM,) * 5,
-        scratch_shapes=[pltpu.SemaphoreType.DMA((pieces,))],
+        scratch_shapes=[pltpu.SemaphoreType.DMA((pieces,)), pltpu.SemaphoreType.REGULAR],
         compiler_params=params(3),
         cost_estimate=cost(4),
         name="vocab_head",
     )(own, other, hidden, gain, *[resident(part) for part in turned], stored(table))
 
 
-def vocab_tail(scaled, square, tables, width):
-    rows = scaled.shape[0]
+def vocab_tail(scaled, square, held_part, table, low_row, high_row, width):
+    rows, depth = scaled.shape
     fold = fold_of(rows, width)
-    used = sum(table.shape[0] for table in tables)
-
-    def kernel(x_ref, square_ref, *refs):
-        out_ref = refs[-1]
+    count = high_row - low_row
+    used = held_part.shape[0] + count
+    step = round_up(-(-count // 2), 2 * BLOCK)
+    pieces = -(-count // step)
+
+    def kernel(x_ref, square_ref, held_ref, table_ref, out_ref, late, sems, gate):
+        copies = row_copies(table_ref, late, sems, low_row, high_row, step)
+        for copy in copies:
+            copy.start()
+        fence(gate)
         x = x_ref[...]
-        start = 0
-        for table_ref in refs[:-1]:
-            put_terms(out_ref, rows, start, x, table_ref, False)
-            start += table_ref.shape[0]
+        put_terms(out_ref, rows, 0, x, held_ref, False)
+        start = held_part.shape[0]
+        for i, copy in enumerate(copies):
+            copy.wait()
+            a, b = i * step, min((i + 1) * step, count)
+            put_terms(out_ref, rows, start + a, x, late.at[a:b], False)
         put_folded(
             out_ref, rows, used,
             jnp.broadcast_to(square_ref[:, 0:1], (rows, width - used)),
@@ -491,12 +507,17 @@
     return pl.pallas_call(
         kernel,
         out_shape=jax.ShapeDtypeStruct((rows * fold, width // fold), jnp.float32),
-        in_specs=[VMEM] * (2 + len(tables)),
+        in_specs=[VMEM, VMEM, VMEM, ANY],
         out_specs=VMEM,
-        compiler_params=params(3),
+        scratch_shapes=[
+            pltpu.VMEM((count, depth), table.dtype),
+            pltpu.SemaphoreType.DMA((pieces,)),
+            pltpu.SemaphoreType.REGULAR,
+        ],
+        compiler_params=params(3 + count * round_up(depth, LANES) * 2 / MIB),
         cost_estimate=cost(6),
         name="vocab_tail",
-    )(scaled, square, *[resident(table) for table in tables])
+    )(scaled, square, resident(held_part), stored(table))
 
 
 def vocab_logits(parts, draft_ids, bounds, rows, features):
@@ -650,7 +671,7 @@
     def mark(share):
         return int(columns * share) // BLOCK * BLOCK
 
-    marks = [0, mark(0.16), mark(0.336), mark(0.64), mark(0.82), columns]
+    marks = [0, mark(0.16), mark(0.32), mark(0.64), mark(0.832), columns]
 
     sums = project(
         hidden_in,
@@ -662,8 +683,8 @@
     cache, keys, values = fetch_attention(
         latent_cache[:, 0], key_up[0], value_up[0], sums, 3
     )
-    packed, local, out_table, stored_part = attend(
-        own, other, lengths, cache, keys, values, features, w_out, table, marks[3], marks[4]
+    packed, local, out_table = attend(
+        own, other, lengths, cache, keys, values, features, w_out
     )
     own, other = pair_softmax(packed, "seq", rows, q_width)
     turned = [fetch_turned(table, packed, marks[0], marks[1], 3)]
@@ -687,10 +708,10 @@
     bounds = [(0, marks[3]), (marks[3], columns)]
     tail_width = round_up(columns - marks[3] + LANES, 2 * LANES)
     new_hidden, scaled, square, piece, late_part = vocab_head(
-        part, received, hidden_in, final_gain, turned, table, marks[4], columns, marks[3]
+        part, received, hidden_in, final_gain, turned, table, marks[3], marks[4], marks[3]
     )
     parts = [pair_sum(piece, "seq")]
-    piece = vocab_tail(scaled, square, [stored_part, late_part], tail_width)
+    piece = vocab_tail(scaled, square, late_part, table, marks[4], columns, tail_width)
     parts.append(pair_sum(piece, "seq"))
     logits, stats = vocab_logits(parts, draft_ids, bounds, rows, features)
     if is_power(heads):

time: 70.4 us -> 65 us (0.923)
  Pallas kernels: 40.1 us -> 34.8 us
    pallas_call x1, Pallas kernels: 7.09 us -> 3.49 us  [attend(): pl.pallas_call(kernel, out_shape=(jax.ShapeDtypeStruct((requests * fold,...]
    pallas_call x1, Pallas kernels: 5.85 us -> 4.38 us  [vocab_head(): pl.pallas_call(kernel, out_shape=(jax.ShapeDtypeStruct((rows, depth), jnp...]
    pallas_call x1, Pallas kernels: 5.54 us -> 4.35 us  [project(): pl.pallas_call(kernel, out_shape=jax.ShapeDtypeStruct((rows * fold, width...]
    pallas_call x1, Pallas kernels: 3.9 us -> 4.8 us  [vocab_tail(): pl.pallas_call(kernel, out_shape=jax.ShapeDtypeStruct((rows * fold, width...]
  transfers between devices with their start and end apart: 9 -> 9, of which waited for: 6 -> 6; matrix products, arithmetic and copies ran while one was open for 0% -> 0% of each run, Pallas kernels for 26% -> 30%
where the time goes in v3:
time: 65 us; the launch traced here: 64.9 us
  Pallas kernels  34.8 us (54%)
  starting transfers between devices  17 us (26%)
  waiting for transfers between devices  12.4 us (19%)
  between operations  0.75 us (1%)
    ppermute x9, starting transfers between devices, swap(): return lax.ppermute(array, axis, [(i, i ^ mask) for i in range(size)])  17 us
    ppermute x9, waiting for transfers between devices, swap(): return lax.ppermute(array, axis, [(i, i ^ mask) for i in range(size)])  12.4 us
    pallas_call x3, Pallas kernels, fetch_turned(): pl.pallas_call(kernel, out_shape=pltpu.VMEM((depth, count), table.dtype),...  12 us
    pallas_call x1, Pallas kernels, vocab_tail(): pl.pallas_call(kernel, out_shape=jax.ShapeDtypeStruct((rows * fold, width...  4.8 us
    pallas_call x1, Pallas kernels, vocab_head(): pl.pallas_call(kernel, out_shape=(jax.ShapeDtypeStruct((rows, depth), jnp...  4.38 us
    pallas_call x1, Pallas kernels, project(): pl.pallas_call(kernel, out_shape=jax.ShapeDtypeStruct((rows * fold, width...  4.35 us
    pallas_call x1, Pallas kernels, attend(): pl.pallas_call(kernel, out_shape=(jax.ShapeDtypeStruct((requests * fold,...  3.49 us
    pallas_call x1, Pallas kernels, fetch_attention(): pl.pallas_call(kernel, out_shape=(pltpu.VMEM(cache.shape, cache.dtype), p...  2.65 us
  transfers between devices with their start and end apart: 9, of which 6 were waited for; matrix products, arithmetic and copies ran while one was open for 0% of the time, Pallas kernels for 30%

profile of v3, /device:TPU:0, one launch (start us, length us, event | category | flops | bytes accessed | tf_op | source)
XLA Modules:
  0.0 64.9 jit_solution(3925286071067014830)
XLA Ops:
  0.6 0.0 copy-start.2
  0.6 4.4 %project.1.after_ref.own_ref = f32[24,1024]{1,0:T(8,128)S(1)} custom-call(bf16[12,2560]{1,0:T(8,128)(2,1)} %x_ref.1, f32[2560]{0:T(1024)} %gain_hbm.1, bf16[2560,1280]{1,0:T(8,128)(2,1)} %wq_ref.1, bf16[2560,640]{1,0:T(8,128)(2,1)} %bitcast.12), custom_call_target="tpu_custom_call" | custom-call | flops 25000000 | tf_op jit(solution)/shard_map/project/pallas_call | solution.py:139
  5.0 3.1 %collective-permute-start = (f32[24,1024]{1,0:T(8,128)S(1)}, f32[24,1024]{1,0:T(8,128)S(1)}, u32[]{:S(2)}, u32[]{:S(2)}) collective-permute-start(f32[24,1024]{1,0:T(8,128)S(1)} %project.1.after_ref.own_ref), channel_id=1, source_target_pairs={{0,4},{4,0},{1,5},{5,1},{2,6},{6,2},{3,7},{7,3},{8,12},{12,8},{9,1... | collective-permute-start | bytes 294920 | tf_op jit(solution)/shard_map/ppermute | solution.py:77
  8.1 2.6 %fetch_attention.1 = (bf16[12,256,640]{2,1,0:T(8,128)(2,1)S(1)}, bf16[320,1280]{1,0:T(8,128)(2,1)S(1)}, bf16[384,1280]{1,0:T(8,128)(2,1)S(1)}) custom-call(bf16[12,256,640]{2,1,0:T(8,128)(2,1)} %bitcast.11, bf16[320,1280]{1,0:T(8,128)(2,1)} %bitcast.13, bf16[320,1280]{1,0:T(8,128)(2,1)} %bitcast.14, f32[24,1024]{1,0:T(8,128)S(1)} %project.1.after_ref.own_ref), custom_call_target="tpu_custom_call" | custom-call | flops 15000000 | tf_op jit(solution)/shard_map/fetch_attention/pallas_call | solution.py:215
  10.7 0.1 collective-permute-done.other_ref
  10.9 0.0 copy-done.2
  10.9 3.5 %attend.1 = (f32[24,768]{1,0:T(8,128)S(1)}, f32[12,1408]{1,0:T(8,128)S(1)}, bf16[1280,2560]{1,0:T(8,128)(2,1)S(1)}) custom-call(f32[24,1024]{1,0:T(8,128)S(1)} %project.1.after_ref.own_ref, f32[24,1024]{1,0:T(8,128)S(1)} %collective-permute-done.other_ref, s32[12]{0:T(128)S(1)} %copy-done.2, bf16[12,256,640]{2,1,0:T(8,128)(2,1)S(1)} %get-tuple-element.18.cache_ref, ...), custom_call_target="tpu_custom_call" | custom-call | flops 25000000 | tf_op jit(solution)/shard_map/attend/pallas_call | solution.py:335
  14.4 1.9 %collective-permute-start.1 = (f32[24,768]{1,0:T(8,128)S(1)}, f32[24,768]{1,0:T(8,128)S(1)}, u32[]{:S(2)}, u32[]{:S(2)}) collective-permute-start(f32[24,768]{1,0:T(8,128)S(1)} %get-tuple-element.21.own_ref.after_ref), channel_id=1, source_target_pairs={{0,4},{4,0},{1,5},{5,1},{2,6},{6,2},{3,7},{7,3},{8,12},{12,8},{9,1... | collective-permute-start | bytes 221192 | tf_op jit(solution)/shard_map/ppermute | solution.py:77
  16.2 2.5 %collective-permute-done.1.other_ref = f32[24,768]{1,0:T(8,128)S(1)} collective-permute-done((f32[24,768]{1,0:T(8,128)S(1)}, f32[24,768]{1,0:T(8,128)S(1)}, u32[]{:S(2)}, u32[]{:S(2)}) %collective-permute-start.1) | collective-permute-done | bytes 73760 | tf_op jit(solution)/shard_map/ppermute | solution.py:77
  18.8 1.1 %merge_out.1.after_ref = f32[24,1280]{1,0:T(8,128)S(1)} custom-call(f32[24,768]{1,0:T(8,128)S(1)} %get-tuple-element.21.own_ref.after_ref, f32[24,768]{1,0:T(8,128)S(1)} %collective-permute-done.1.other_ref, f32[12,1408]{1,0:T(8,128)S(1)} %get-tuple-element.22.local_ref, bf16[1280,2560]{1,0:T(8,128)(2,1)S(1)} %get-tuple-element.23.w_ref), custom_call_target="tpu_custom_call" | custom-call | flops 10000000 | tf_op jit(solution)/shard_map/merge_out/pallas_call | solution.py:402
  19.8 1.9 %collective-permute-start.2 = (f32[24,1280]{1,0:T(8,128)S(1)}, f32[24,1280]{1,0:T(8,128)S(1)}, u32[]{:S(2)}, u32[]{:S(2)}) collective-permute-start(f32[24,1280]{1,0:T(8,128)S(1)} %merge_out.1.after_ref), channel_id=1, source_target_pairs={{0,1},{1,0},{2,3},{3,2},{4,5},{5,4},{6,7},{7,6},{8,9},{9,8},{10,11... | collective-permute-start | bytes 368648 | tf_op jit(solution)/shard_map/ppermute | solution.py:77
  21.7 3.0 %collective-permute-done.2 = f32[24,1280]{1,0:T(8,128)S(1)} collective-permute-done((f32[24,1280]{1,0:T(8,128)S(1)}, f32[24,1280]{1,0:T(8,128)S(1)}, u32[]{:S(2)}, u32[]{:S(2)}) %collective-permute-start.2) | collective-permute-done | bytes 122912 | tf_op jit(solution)/shard_map/ppermute | solution.py:77
  24.7 3.6 %collective-permute-start.3 = (f32[24,1280]{1,0:T(8,128)S(1)}, f32[24,1280]{1,0:T(8,128)S(1)}, u32[]{:S(2)}, u32[]{:S(2)}) collective-permute-start(f32[24,1280]{1,0:T(8,128)S(1)} %add.3.after_ref.own_ref), channel_id=1, source_target_pairs={{0,2},{1,3},{2,0},{3,1},{4,6},{5,7},{6,4},{7,5},{8,10},{9,11},{10,... | collective-permute-start | bytes 368648 | tf_op jit(solution)/shard_map/ppermute | solution.py:77
  28.3 3.3 %fetch_turned.3.refs_0_ = bf16[2560,1280]{1,0:T(8,128)(2,1)S(1)} custom-call(bf16[8000,2560]{1,0:T(8,128)(2,1)} %bitcast.6, f32[24,768]{1,0:T(8,128)S(1)} %get-tuple-element.21.own_ref.after_ref), custom_call_target="tpu_custom_call" | custom-call | flops 15000000 | tf_op jit(solution)/shard_map/fetch_turned/pallas_call | solution.py:184
  31.6 3.3 %fetch_turned.4.refs_1_ = bf16[2560,1280]{1,0:T(8,128)(2,1)S(1)} custom-call(bf16[8000,2560]{1,0:T(8,128)(2,1)} %bitcast.7, f32[24,1280]{1,0:T(8,128)S(1)} %merge_out.1.after_ref), custom_call_target="tpu_custom_call" | custom-call | flops 15000000 | tf_op jit(solution)/shard_map/fetch_turned/pallas_call | solution.py:184
  35.0 0.0 copy-start
  35.0 0.0 copy-start.1
  35.0 5.4 %fetch_turned.5.refs_2_ = bf16[2560,2560]{1,0:T(8,128)(2,1)S(1)} custom-call(bf16[8000,2560]{1,0:T(8,128)(2,1)} %bitcast.8, f32[24,1280]{1,0:T(8,128)S(1)} %add.3.after_ref.own_ref), custom_call_target="tpu_custom_call" | custom-call | flops 30000000 | tf_op jit(solution)/shard_map/fetch_turned/pallas_call | solution.py:184
  40.4 0.0 collective-permute-done.3.other_ref
  40.4 0.0 copy-done
  40.4 0.0 copy-done.1
  40.4 4.4 %vocab_head.1 = (bf16[12,2560]{1,0:T(8,128)(2,1)}, bf16[12,2560]{1,0:T(8,128)(2,1)S(1)}, f32[12,128]{1,0:T(8,128)S(1)}, f32[24,2560]{1,0:T(8,128)S(1)}, bf16[1536,2560]{1,0:T(8,128)(2,1)S(1)}) custom-call(f32[24,1280]{1,0:T(8,128)S(1)} %add.3.after_ref.own_ref, f32[24,1280]{1,0:T(8,128)S(1)} %collective-permute-done.3.other_ref, ...), custom_call_target="tpu_custom_call" | custom-call | flops 20000000 | tf_op jit(solution)/shard_map/vocab_head/pallas_call | solution.py:464
  44.8 2.0 %collective-permute-start.4 = (f32[24,2560]{1,0:T(8,128)S(1)}, f32[24,2560]{1,0:T(8,128)S(1)}, u32[]{:S(2)}, u32[]{:S(2)}) collective-permute-start(f32[24,2560]{1,0:T(8,128)S(1)} %get-tuple-element.25.refs_0_), channel_id=1, source_target_pairs={{0,4},{4,0},{1,5},{5,1},{2,6},{6,2},{3,7},{7,3},{8,12},{12,8},{9,1... | collective-permute-start | bytes 737288 | tf_op jit(solution)/shard_map/ppermute | solution.py:77
  46.8 0.0 copy-start.3
  46.8 4.8 %vocab_tail.1.refs_2_ = f32[24,1536]{1,0:T(8,128)S(1)} custom-call(bf16[12,2560]{1,0:T(8,128)(2,1)S(1)} %get-tuple-element.26.x_ref, f32[12,128]{1,0:T(8,128)S(1)} %get-tuple-element.27.square_ref, bf16[1536,2560]{1,0:T(8,128)(2,1)S(1)} %get-tuple-element.28.held_ref, bf16[8000,2560]{1,0:T(8,128)(2,1)} %bitcast.10), custom_call_target="tpu_custom_call" | custom-call | flops 30000000 | tf_op jit(solution)/shard_map/vocab_tail/pallas_call | solution.py:507
  51.6 0.1 collective-permute-start.5
  51.8 5.1 %collective-permute-done.5.refs_3_ = f32[24,1536]{1,0:T(8,128)S(1)} collective-permute-done((f32[24,1536]{1,0:T(8,128)S(1)}, f32[24,1536]{1,0:T(8,128)S(1)}, u32[]{:S(2)}, u32[]{:S(2)}) %collective-permute-start.5) | collective-permute-done | bytes 147488 | tf_op jit(solution)/shard_map/ppermute | solution.py:77
  56.8 0.0 collective-permute-done.4.refs_1_
  56.9 0.0 copy-done.3
  56.9 0.9 %vocab_logits.1 = (f32[12,8000]{1,0:T(8,128)S(1)}, f32[12,128]{1,0:T(8,128)S(1)}) custom-call(s32[12]{0:T(128)S(1)} %copy-done.3, f32[24,2560]{1,0:T(8,128)S(1)} %get-tuple-element.25.refs_0_, f32[24,2560]{1,0:T(8,128)S(1)} %collective-permute-done.4.refs_1_, f32[24,1536]{1,0:T(8,128)S(1)} %vocab_tail.1.refs_2_, f32[24,1536]{1,0:T(8,128)S(1)} %collective-permute-done.5.refs_3_), custom_call_target="tpu_custom_call" | custom-call | flops 10000000 | tf_op jit(solution)/shard_map/vocab_logits/pallas_call | solution.py:559
  57.7 0.3 collective-permute-start.8
  58.1 1.7 %collective-permute-start.7 = (f32[12,128]{1,0:T(8,128)S(1)}, f32[12,128]{1,0:T(8,128)S(1)}, u32[]{:S(2)}, u32[]{:S(2)}) collective-permute-start(f32[12,128]{1,0:T(8,128)S(1)} %get-tuple-element.30.refs_0_), channel_id=1, source_target_pairs={{0,2},{1,3},{2,0},{3,1},{4,6},{5,7},{6,4},{7,5},{8,10},{9,11},{10,... | collective-permute-start | bytes 18440 | tf_op jit(solution)/shard_map/ppermute | solution.py:77
  59.8 2.4 %collective-permute-start.6 = (f32[12,128]{1,0:T(8,128)S(1)}, f32[12,128]{1,0:T(8,128)S(1)}, u32[]{:S(2)}, u32[]{:S(2)}) collective-permute-start(f32[12,128]{1,0:T(8,128)S(1)} %get-tuple-element.30.refs_0_), channel_id=1, source_target_pairs={{0,1},{1,0},{2,3},{3,2},{4,5},{5,4},{6,7},{7,6},{8,9},{9,8},{10,11... | collective-permute-start | bytes 18440 | tf_op jit(solution)/shard_map/ppermute | solution.py:77
  62.1 1.1 %collective-permute-done.8.refs_3_ = f32[12,128]{1,0:T(8,128)S(1)} collective-permute-done((f32[12,128]{1,0:T(8,128)S(1)}, f32[12,128]{1,0:T(8,128)S(1)}, u32[]{:S(2)}, u32[]{:S(2)}) %collective-permute-start.8) | collective-permute-done | bytes 6176 | tf_op jit(solution)/shard_map/ppermute | solution.py:77
  63.2 0.0 collective-permute-done.7.refs_2_
  63.2 0.6 collective-permute-done.6.refs_1_
  63.8 1.1 %vocab_finish.1 = (f32[12,8000]{1,0:T(8,128)}, f32[1,12]{1,0:T(1,128)}) custom-call(f32[12,8000]{1,0:T(8,128)S(1)} %get-tuple-element.29.logit_ref, f32[12,128]{1,0:T(8,128)S(1)} %get-tuple-element.30.refs_0_, f32[12,128]{1,0:T(8,128)S(1)} %collective-permute-done.6.refs_1_, f32[12,128]{1,0:T(8,128)S(1)} %collective-permute-done.7.refs_2_, ...), custom_call_target="tpu_custom_call" | custom-call | flops 5000000 | tf_op jit(solution)/shard_map/vocab_finish/pallas_call | solution.py:601
  (1 shorter events, 0.0 us)
Async XLA Ops:
  0.6 10.2 %copy-start.2 = (s32[12]{0:T(128)S(1)}, s32[12]{0:T(128)}, u32[]{:S(2)}) copy-start(s32[12]{0:T(128)} %length_ref.1) | copy-start | bytes 148
  5.0 5.9 %collective-permute-start = (f32[24,1024]{1,0:T(8,128)S(1)}, f32[24,1024]{1,0:T(8,128)S(1)}, u32[]{:S(2)}, u32[]{:S(2)}) collective-permute-start(f32[24,1024]{1,0:T(8,128)S(1)} %project.1.after_ref.own_ref), channel_id=1, source_target_pairs={{0,4},{4,0},{1,5},{5,1},{2,6},{6,2},{3,7},{7,3},{8,12},{12,8},{9,1... | collective-permute-start | bytes 294920 | tf_op jit(solution)/shard_map/ppermute | solution.py:77
  14.4 4.4 %collective-permute-start.1 = (f32[24,768]{1,0:T(8,128)S(1)}, f32[24,768]{1,0:T(8,128)S(1)}, u32[]{:S(2)}, u32[]{:S(2)}) collective-permute-start(f32[24,768]{1,0:T(8,128)S(1)} %get-tuple-element.21.own_ref.after_ref), channel_id=1, source_target_pairs={{0,4},{4,0},{1,5},{5,1},{2,6},{6,2},{3,7},{7,3},{8,12},{12,8},{9,1... | collective-permute-start | bytes 221192 | tf_op jit(solution)/shard_map/ppermute | solution.py:77
  19.8 4.9 %collective-permute-start.2 = (f32[24,1280]{1,0:T(8,128)S(1)}, f32[24,1280]{1,0:T(8,128)S(1)}, u32[]{:S(2)}, u32[]{:S(2)}) collective-permute-start(f32[24,1280]{1,0:T(8,128)S(1)} %merge_out.1.after_ref), channel_id=1, source_target_pairs={{0,1},{1,0},{2,3},{3,2},{4,5},{5,4},{6,7},{7,6},{8,9},{9,8},{10,11... | collective-permute-start | bytes 368648 | tf_op jit(solution)/shard_map/ppermute | solution.py:77
  24.7 15.6 %collective-permute-start.3 = (f32[24,1280]{1,0:T(8,128)S(1)}, f32[24,1280]{1,0:T(8,128)S(1)}, u32[]{:S(2)}, u32[]{:S(2)}) collective-permute-start(f32[24,1280]{1,0:T(8,128)S(1)} %add.3.after_ref.own_ref), channel_id=1, source_target_pairs={{0,2},{1,3},{2,0},{3,1},{4,6},{5,7},{6,4},{7,5},{8,10},{9,11},{10,... | collective-permute-start | bytes 368648 | tf_op jit(solution)/shard_map/ppermute | solution.py:77
  35.0 5.4 %copy-start = (bf16[12,2560]{1,0:T(8,128)(2,1)S(1)}, bf16[12,2560]{1,0:T(8,128)(2,1)}, u32[]{:S(2)}) copy-start(bf16[12,2560]{1,0:T(8,128)(2,1)} %x_ref.1) | copy-start | bytes 184324
  35.0 5.4 %copy-start.1 = (f32[2560]{0:T(1024)S(1)}, f32[2560]{0:T(1024)}, u32[]{:S(2)}) copy-start(f32[2560]{0:T(1024)} %gain_ref.1) | copy-start | bytes 30724
  44.8 12.1 %collective-permute-start.4 = (f32[24,2560]{1,0:T(8,128)S(1)}, f32[24,2560]{1,0:T(8,128)S(1)}, u32[]{:S(2)}, u32[]{:S(2)}) collective-permute-start(f32[24,2560]{1,0:T(8,128)S(1)} %get-tuple-element.25.refs_0_), channel_id=1, source_target_pairs={{0,4},{4,0},{1,5},{5,1},{2,6},{6,2},{3,7},{7,3},{8,12},{12,8},{9,1... | collective-permute-start | bytes 737288 | tf_op jit(solution)/shard_map/ppermute | solution.py:77
  46.8 10.0 %copy-start.3 = (s32[12]{0:T(128)S(1)}, s32[12]{0:T(128)}, u32[]{:S(2)}) copy-start(s32[12]{0:T(128)} %id_ref.1) | copy-start | bytes 148
  51.6 5.2 %collective-permute-start.5 = (f32[24,1536]{1,0:T(8,128)S(1)}, f32[24,1536]{1,0:T(8,128)S(1)}, u32[]{:S(2)}, u32[]{:S(2)}) collective-permute-start(f32[24,1536]{1,0:T(8,128)S(1)} %vocab_tail.1.refs_2_), channel_id=1, source_target_pairs={{0,4},{4,0},{1,5},{5,1},{2,6},{6,2},{3,7},{7,3},{8,12},{12,8},{9,1... | collective-permute-start | bytes 442376 | tf_op jit(solution)/shard_map/ppermute | solution.py:77
  57.7 5.5 %collective-permute-start.8 = (f32[12,128]{1,0:T(8,128)S(1)}, f32[12,128]{1,0:T(8,128)S(1)}, u32[]{:S(2)}, u32[]{:S(2)}) collective-permute-start(f32[12,128]{1,0:T(8,128)S(1)} %get-tuple-element.30.refs_0_), channel_id=1, source_target_pairs={{0,3},{1,2},{2,1},{3,0},{4,7},{5,6},{6,5},{7,4},{8,11},{9,10},{10,... | collective-permute-start | bytes 18440 | tf_op jit(solution)/shard_map/ppermute | solution.py:77
  58.1 5.2 %collective-permute-start.7 = (f32[12,128]{1,0:T(8,128)S(1)}, f32[12,128]{1,0:T(8,128)S(1)}, u32[]{:S(2)}, u32[]{:S(2)}) collective-permute-start(f32[12,128]{1,0:T(8,128)S(1)} %get-tuple-element.30.refs_0_), channel_id=1, source_target_pairs={{0,2},{1,3},{2,0},{3,1},{4,6},{5,7},{6,4},{7,5},{8,10},{9,11},{10,... | collective-permute-start | bytes 18440 | tf_op jit(solution)/shard_map/ppermute | solution.py:77
  59.8 4.0 %collective-permute-start.6 = (f32[12,128]{1,0:T(8,128)S(1)}, f32[12,128]{1,0:T(8,128)S(1)}, u32[]{:S(2)}, u32[]{:S(2)}) collective-permute-start(f32[12,128]{1,0:T(8,128)S(1)} %get-tuple-element.30.refs_0_), channel_id=1, source_target_pairs={{0,1},{1,0},{2,3},{3,2},{4,5},{5,4},{6,7},{7,6},{8,9},{9,8},{10,11... | collective-permute-start | bytes 18440 | tf_op jit(solution)/shard_map/ppermute | solution.py:77

commit v4 on v3

--- a/solution.py
+++ b/solution.py
@@ -12,6 +12,7 @@
 LANES = 128
 ROW_TILE = 16
 BLOCK = 256
+RING = 6
 EPSILON = 1e-05
 NEGATIVE = -1e30
 MIB = 1 << 20
@@ -166,49 +167,87 @@
     ]
 
 
+def turn_copies(table_ref, held_ref, sems, low, high):
+    slots = held_ref.shape[0]
+    copies = []
+    for i, at in enumerate(range(low, high, BLOCK)):
+        size = min(BLOCK, high - at)
+        copies.append(
+            pltpu.make_async_copy(
+                table_ref.at[pl.ds(at, size)],
+                held_ref.at[i % slots, pl.ds(0, size)],
+                sems.at[i % slots],
+            )
+        )
+    return copies
+
+
+def turn_rows(copies, held_ref, out_ref):
+    slots, _, depth = held_ref.shape
+    count = out_ref.shape[1]
+    for i, copy in enumerate(copies):
+        copy.wait()
+        a, b = i * BLOCK, min((i + 1) * BLOCK, count)
+        for k in range(0, depth, BLOCK):
+            end = min(k + BLOCK, depth)
+            out_ref[k:end, a:b] = held_ref[i % slots, 0 : b - a, k:end].T
+        if i + slots < len(copies):
+            copies[i + slots].start()
+
+
+def turn_slots(count):
+    return min(RING, -(-count // BLOCK))
+
+
+def turn_scratch(table, count):
+    return [
+        pltpu.VMEM((turn_slots(count), BLOCK, table.shape[1]), table.dtype),
+        pltpu.SemaphoreType.DMA((turn_slots(count),)),
+    ]
+
+
+def turn_params(table, count):
+    size = turn_slots(count) * BLOCK * round_up(table.shape[1], LANES) * 2
+    return params(1 + size / MIB)
+
+
 def fetch_turned(table, after, low, high, micros):
-    depth = table.shape[1]
-    count = high - low
-
     def kernel(table_ref, after_ref, out_ref, held, sems):
-        copies = row_copies(table_ref, held, sems, low, high, BLOCK)
-        for copy in copies:
+        copies = turn_copies(table_ref, held, sems, low, high)
+        for copy in copies[: held.shape[0]]:
             copy.start()
-        for i, copy in enumerate(copies):
-            copy.wait()
-            a, b = i * BLOCK, min((i + 1) * BLOCK, count)
-            for k in range(0, depth, BLOCK):
-                end = min(k + BLOCK, depth)
-                out_ref[k:end, a:b] = held[a:b, k:end].T
-
-    return pl.pallas_call(
-        kernel,
-        out_shape=pltpu.VMEM((depth, count), table.dtype),
+        turn_rows(copies, held, out_ref)
+
+    return pl.pallas_call(
+        kernel,
+        out_shape=pltpu.VMEM((table.shape[1], high - low), table.dtype),
         in_specs=[ANY, ANY],
         out_specs=VMEM,
-        scratch_shapes=[
-            pltpu.VMEM((count, depth), table.dtype),
-            pltpu.SemaphoreType.DMA((-(-count // BLOCK),)),
-        ],
-        compiler_params=params(1 + count * round_up(depth, LANES) * 2 / MIB),
+        scratch_shapes=turn_scratch(table, high - low),
+        compiler_params=turn_params(table, high - low),
         cost_estimate=cost(micros),
         name="fetch_turned",
     )(stored(table), after)
 
 
-def fetch_attention(cache, key_up, value_up, after, micros):
+def fetch_attention(cache, key_up, value_up, table, after, low, high, micros):
     rank, width = value_up.shape
     full = round_up(rank, LANES)
 
-    def kernel(cache_ref, key_ref, value_ref, after_ref, cache_out, key_out, value_out, sems):
+    def kernel(
+        cache_ref, key_ref, value_ref, table_ref, after_ref,
+        cache_out, key_out, value_out, turned_out, sems, held, row_sems,
+    ):
         copies = [
             pltpu.make_async_copy(key_ref, key_out, sems.at[0]),
             pltpu.make_async_copy(value_ref, value_out.at[pl.ds(full - rank, rank)], sems.at[1]),
             pltpu.make_async_copy(cache_ref, cache_out, sems.at[2]),
         ]
-        for copy in copies:
+        rows = turn_copies(table_ref, held, row_sems, low, high)
+        for copy in rows[: held.shape[0]] + copies:
             copy.start()
         value_out[0 : full - rank, :] = jnp.zeros((full - rank, width), value_up.dtype)
+        turn_rows(rows, held, turned_out)
         for copy in copies:
             copy.wait()
 
@@ -218,14 +257,15 @@
             pltpu.VMEM(cache.shape, cache.dtype),
             pltpu.VMEM(key_up.shape, key_up.dtype),
             pltpu.VMEM((full, width), value_up.dtype),
+            pltpu.VMEM((table.shape[1], high - low), table.dtype),
         ),
-        in_specs=[ANY] * 4,
-        out_specs=(VMEM,) * 3,
-        scratch_shapes=[pltpu.SemaphoreType.DMA((3,))],
-        compiler_params=params(1),
+        in_specs=[ANY] * 5,
+        out_specs=(VMEM,) * 4,
+        scratch_shapes=[pltpu.SemaphoreType.DMA((3,))] + turn_scratch(table, high - low),
+        compiler_params=turn_params(table, high - low),
         cost_estimate=cost(micros),
         name="fetch_attention",
-    )(stored(cache), stored(key_up), stored(value_up), after)
+    )(stored(cache), stored(key_up), stored(value_up), stored(table), after)
 
 
 def attend(own, other, lengths, cache, key_up, value_pad, features, w_out):
@@ -411,37 +451,41 @@
     )(own, other, local, resident(w_out))
 
 
-def put_terms(out_ref, rows, start, x, table_ref, turned):
-    count = table_ref.shape[1] if turned else table_ref.shape[0]
+def put_terms(out_ref, rows, x, parts, low, high):
     depth = x.shape[1]
     half = depth // 2 if depth % (2 * LANES) == 0 else depth
-    for at in range(0, count, 2 * BLOCK):
-        end = min(at + 2 * BLOCK, count)
-        total = None
-        for k in range(0, depth, half):
-            piece = x[:, k : k + half]
-            if turned:
-                term = jnp.dot(
-                    piece, table_ref[k : k + half, at:end], preferred_element_type=jnp.float32
-                )
-            else:
-                term = lax.dot_general(
-                    piece, table_ref[at:end, k : k + half], NT, preferred_element_type=jnp.float32
-                )
-            total = term if total is None else total + term
-        put_folded(out_ref, rows, start + at, total)
-
-
-def vocab_head(own, other, hidden, gain, turned, table, low_row, high_row, width):
+    base = 0
+    for ref, turned in parts:
+        count = ref.shape[1] if turned else ref.shape[0]
+        first, last = max(low, base), min(high, base + count)
+        for at in range(first, last, 2 * BLOCK):
+            a, b = at - base, min(at + 2 * BLOCK, last) - base
+            total = None
+            for k in range(0, depth, half):
+                piece = x[:, k : k + half]
+                if turned:
+                    term = jnp.dot(
+                        piece, ref[k : k + half, a:b], preferred_element_type=jnp.float32
+                    )
+                else:
+                    term = lax.dot_general(
+                        piece, ref[a:b, k : k + half], NT, preferred_element_type=jnp.float32
+                    )
+                total = term if total is None else total + term
+            put_folded(out_ref, rows, at - low, total)
+        base += count
+
+
+def vocab_head(own, other, hidden, gain, turned, split, table, low_row, high_row, width):
     rows, depth = hidden.shape
     fold = fold_of(rows, width)
     count = len(turned)
-    pieces = 4
+    pieces = 2
     step = round_up(-(-(high_row - low_row) // pieces), ROW_TILE)
 
     def kernel(own_ref, other_ref, x_ref, gain_ref, *refs):
         table_ref = refs[count]
-        new_ref, scaled_ref, square_ref, out_ref, held, sems, gate = refs[count + 1 :]
+        new_ref, scaled_ref, out_ref, held, sems, gate = refs[count + 1 :]
         copies = row_copies(table_ref, held, sems, low_row, high_row, step)
         for copy in copies:
             copy.start()
@@ -451,13 +495,9 @@
         new_ref[...] = updated.astype(jnp.bfloat16)
         scaled = (updated * gain_ref[...].reshape(1, depth)).astype(jnp.bfloat16)
         scaled_ref[...] = scaled
-        square_ref[...] = jnp.broadcast_to(
-            jnp.sum(updated * updated, axis=1, keepdims=True), (rows, LANES)
-        )
-        start = 0
-        for turned_ref in refs[:count]:
-            put_terms(out_ref, rows, start, scaled, turned_ref, True)
-            start += turned_ref.shape[1]
+        square = jnp.sum(updated * updated, axis=1, keepdims=True)
+        put_folded(out_ref, rows, split, jnp.broadcast_to(square, (rows, width - split)))
+        put_terms(out_ref, rows, scaled, [(ref, True) for ref in refs[:count]], 0, split)
         for copy in copies:
             copy.wait()
 
@@ -466,12 +506,11 @@
         out_shape=(
             jax.ShapeDtypeStruct((rows, depth), jnp.bfloat16),
             jax.ShapeDtypeStruct((rows, depth), jnp.bfloat16),
-            jax.ShapeDtypeStruct((rows, LANES), jnp.float32),
             jax.ShapeDtypeStruct((rows * fold, width // fold), jnp.float32),
             pltpu.VMEM((high_row - low_row, depth), table.dtype),
         ),
         in_specs=[VMEM] * (4 + count) + [ANY],
-        out_specs=(VMEM,) * 5,
+        out_specs=(VMEM,) * 4,
         scratch_shapes=[pltpu.SemaphoreType.DMA((pieces,)), pltpu.SemaphoreType.REGULAR],
         compiler_params=params(3),
         cost_estimate=cost(4),
@@ -479,78 +518,85 @@
     )(own, other, hidden, gain, *[resident(part) for part in turned], stored(table))
 
 
-def vocab_tail(scaled, square, held_part, table, low_row, high_row, width):
-    rows, depth = scaled.shape
+def vocab_tail(scaled, turned, late_part, split, columns, width):
+    rows = scaled.shape[0]
     fold = fold_of(rows, width)
-    count = high_row - low_row
-    used = held_part.shape[0] + count
-    step = round_up(-(-count // 2), 2 * BLOCK)
-    pieces = -(-count // step)
-
-    def kernel(x_ref, square_ref, held_ref, table_ref, out_ref, late, sems, gate):
-        copies = row_copies(table_ref, late, sems, low_row, high_row, step)
-        for copy in copies:
-            copy.start()
-        fence(gate)
-        x = x_ref[...]
-        put_terms(out_ref, rows, 0, x, held_ref, False)
-        start = held_part.shape[0]
-        for i, copy in enumerate(copies):
-            copy.wait()
-            a, b = i * step, min((i + 1) * step, count)
-            put_terms(out_ref, rows, start + a, x, late.at[a:b], False)
-        put_folded(
-            out_ref, rows, used,
-            jnp.broadcast_to(square_ref[:, 0:1], (rows, width - used)),
-        )
+    count = len(turned)
+
+    def kernel(x_ref, *refs):
+        late_ref, out_ref = refs[count:]
+        used = columns - split
+        if used < width:
+            put_folded(out_ref, rows, used, jnp.zeros((rows, width - used), jnp.float32))
+        parts = [(ref, True) for ref in refs[:count]] + [(late_ref, False)]
+        put_terms(out_ref, rows, x_ref[...], parts, split, columns)
 
     return pl.pallas_call(
         kernel,
         out_shape=jax.ShapeDtypeStruct((rows * fold, width // fold), jnp.float32),
-        in_specs=[VMEM, VMEM, VMEM, ANY],
+        in_specs=[VMEM] * (2 + count),
         out_specs=VMEM,
-        scratch_shapes=[
-            pltpu.VMEM((count, depth), table.dtype),
-            pltpu.SemaphoreType.DMA((pieces,)),
-            pltpu.SemaphoreType.REGULAR,
-        ],
-        compiler_params=params(3 + count * round_up(depth, LANES) * 2 / MIB),
+        compiler_params=params(3),
         cost_estimate=cost(6),
         name="vocab_tail",
-    )(scaled, square, resident(held_part), stored(table))
-
-
-def vocab_logits(parts, draft_ids, bounds, rows, features):
-    columns = bounds[-1][1]
-    count = len(bounds)
-    flat = [array for pair in parts for array in pair]
-
-    def kernel(id_ref, *refs):
-        pairs = [refs[2 * i : 2 * i + 2] for i in range(count)]
-        logit_ref, stat_ref = refs[2 * count :]
-        full = pairs[-1][0].shape[0] * pairs[-1][0].shape[1] // rows
-        square = get_folded(pairs[-1], rows, full - LANES, LANES)
+    )(scaled, *[resident(part) for part in turned], resident(late_part))
+
+
+def vocab_front(own, other, draft_ids, last, columns, features):
+    rows = draft_ids.shape[0]
+    width = own.shape[0] * own.shape[1] // rows
+
+    def kernel(id_ref, own_ref, other_ref, logit_ref, stat_ref):
+        pair = (own_ref, other_ref)
+        square = get_folded(pair, rows, width - LANES, LANES)
         inv = lax.rsqrt(square[:, 0:1] / features + EPSILON)
         row = lax.broadcasted_iota(jnp.int32, (rows, 1), 0)
         wanted = jnp.zeros((rows, 1), jnp.int32)
         for r in range(rows):
             wanted = jnp.where(row == r, id_ref[r], wanted)
         wanted = wanted - lax.axis_index("heads") * columns
-        top = jnp.full((rows, 1), NEGATIVE, jnp.float32)
-        picked = jnp.zeros((rows, 1), jnp.float32)
-        for pair, (first, last) in zip(pairs, bounds):
-            logits = get_folded(pair, rows, 0, last - first) * inv
-            logit_ref[:, first:last] = logits
-            top = jnp.maximum(top, jnp.max(logits, axis=1, keepdims=True))
-            column = first + lax.broadcasted_iota(jnp.int32, logits.shape, 1)
-            picked = picked + jnp.sum(
-                jnp.where(column == wanted, logits, 0.0), axis=1, keepdims=True
-            )
-        total = jnp.zeros((rows, 1), jnp.float32)
-        for first, last in bounds:
-            total = total + jnp.sum(
-                jnp.exp(logit_ref[:, first:last] - top), axis=1, keepdims=True
-            )
+        logits = get_folded(pair, rows, 0, last) * inv
+        logit_ref[...] = logits
+        column = lax.broadcasted_iota(jnp.int32, logits.shape, 1)
+        picked = jnp.sum(jnp.where(column == wanted, logits, 0.0), axis=1, keepdims=True)
+        top = jnp.max(logits, axis=1, keepdims=True)
+        total = jnp.sum(jnp.exp(logits - top), axis=1, keepdims=True)
+        lane = lax.broadcasted_iota(jnp.int32, (rows, LANES), 1)
+        stats = jnp.where(lane == 1, total, jnp.where(lane == 2, picked, inv))
+        stat_ref[0:rows, :] = jnp.where(lane == 0, top, stats)
+        stat_ref[rows : 2 * rows, :] = jnp.broadcast_to(wanted, (rows, LANES)).astype(jnp.float32)
+
+    return pl.pallas_call(
+        kernel,
+        out_shape=(
+            pltpu.VMEM((rows, last), jnp.float32),
+            jax.ShapeDtypeStruct((2 * rows, LANES), jnp.float32),
+        ),
+        in_specs=[SMEM, VMEM, VMEM],
+        out_specs=(VMEM, VMEM),
+        compiler_params=params(4),
+        cost_estimate=cost(1),
+        name="vocab_front",
+    )(draft_ids, own, other)
+
+
+def vocab_back(own, other, front_stats, first, count):
+    rows = front_stats.shape[0] // 2
+
+    def kernel(front_ref, own_ref, other_ref, logit_ref, stat_ref):
+        top_front, total_front = front_ref[0:rows, 0:1], front_ref[0:rows, 1:2]
+        picked_front, inv = front_ref[0:rows, 2:3], front_ref[0:rows, 3:4]
+        wanted = front_ref[rows : 2 * rows, 0:1].astype(jnp.int32)
+        logits = get_folded((own_ref, other_ref), rows, 0, count) * inv
+        logit_ref[...] = logits
+        column = first + lax.broadcasted_iota(jnp.int32, logits.shape, 1)
+        picked = picked_front + jnp.sum(
+            jnp.where(column == wanted, logits, 0.0), axis=1, keepdims=True
+        )
+        top = jnp.maximum(top_front, jnp.max(logits, axis=1, keepdims=True))
+        total = total_front * jnp.exp(top_front - top) + jnp.sum(
+            jnp.exp(logits - top), axis=1, keepdims=True
+        )
         lane = lax.broadcasted_iota(jnp.int32, (rows, LANES), 1)
         stat_ref[...] = jnp.where(
             lane == 0, top, jnp.where(lane == 1, total, jnp.where(lane == 2, picked, 0.0))
@@ -559,22 +605,23 @@
     return pl.pallas_call(
         kernel,
         out_shape=(
-            pltpu.VMEM((rows, columns), jnp.float32),
+            pltpu.VMEM((rows, count), jnp.float32),
             jax.ShapeDtypeStruct((rows, LANES), jnp.float32),
         ),
-        in_specs=[SMEM] + [VMEM] * len(flat),
+        in_specs=[VMEM] * 3,
         out_specs=(VMEM, VMEM),
         compiler_params=params(4),
-        cost_estimate=cost(2),
-        name="vocab_logits",
-    )(draft_ids, *flat)
-
-
-def vocab_finish(logits, stats):
-    rows, columns = logits.shape
+        cost_estimate=cost(1),
+        name="vocab_back",
+    )(front_stats, own, other)
+
+
+def vocab_finish(front, back, stats):
+    rows, split = front.shape
+    columns = split + back.shape[1]
     count = len(stats)
 
-    def kernel(logit_ref, *refs):
+    def kernel(front_ref, back_ref, *refs):
         stat_refs, out_ref, draft_ref = refs[:count], refs[count], refs[count + 1]
         state = [(ref[:, 0:1], ref[:, 1:2], ref[:, 2:3]) for ref in stat_refs]
         while len(state) > 1:
@@ -591,7 +638,8 @@
             state = joined
         top, total, picked = state[0]
         log_total = top + jnp.log(total)
-        out_ref[...] = logit_ref[...] - log_total
+        out_ref[:, 0:split] = front_ref[...] - log_total
+        out_ref[:, split:columns] = back_ref[...] - log_total
         draft = picked - log_total
         row = lax.broadcasted_iota(jnp.int32, (rows, LANES), 0)
         lane = lax.broadcasted_iota(jnp.int32, (rows, LANES), 1)
@@ -604,12 +652,12 @@
             jax.ShapeDtypeStruct((rows, columns), jnp.float32),
             jax.ShapeDtypeStruct((1, rows), jnp.float32),
         ),
-        in_specs=[VMEM] * (1 + count),
+        in_specs=[VMEM] * (2 + count),
         out_specs=(VMEM, VMEM),
         compiler_params=params(4),
         cost_estimate=cost(1),
         name="vocab_finish",
-    )(resident(logits), *stats)
+    )(resident(front), resident(back), *stats)
 
 
 def pair_sum(array, axis):
@@ -671,7 +719,8 @@
     def mark(share):
         return int(columns * share) // BLOCK * BLOCK
 
-    marks = [0, mark(0.16), mark(0.32), mark(0.64), mark(0.832), columns]
+    marks = [0, mark(0.096), mark(0.288), mark(0.512), mark(0.896), columns]
+    split = mark(0.448)
 
     sums = project(
         hidden_in,
@@ -680,14 +729,15 @@
         w_latent.reshape(depth, w_latent.shape[1] * w_latent.shape[2]),
     )
     own, other = pair_sum(sums, "seq")
-    cache, keys, values = fetch_attention(
-        latent_cache[:, 0], key_up[0], value_up[0], sums, 3
+    cache, keys, values, turned = fetch_attention(
+        latent_cache[:, 0], key_up[0], value_up[0], table, sums, marks[0], marks[1], 3
     )
+    turned = [turned]
     packed, local, out_table = attend(
         own, other, lengths, cache, keys, values, features, w_out
     )
     own, other = pair_softmax(packed, "seq", rows, q_width)
-    turned = [fetch_turned(table, packed, marks[0], marks[1], 3)]
+    turned.append(fetch_turned(table, packed, marks[1], marks[2], 3))
     part = merge_out(own, other, local, out_table, rows)
 
     heads = lax.axis_size("heads")
@@ -702,18 +752,21 @@
             part = part + received
     else:
         part, received = lax.psum(part, "heads"), jnp.zeros_like(part)
-    turned.append(fetch_turned(table, first, marks[1], marks[2], 3))
-    turned.append(fetch_turned(table, part, marks[2], marks[3], 6))
-
-    bounds = [(0, marks[3]), (marks[3], columns)]
-    tail_width = round_up(columns - marks[3] + LANES, 2 * LANES)
-    new_hidden, scaled, square, piece, late_part = vocab_head(
-        part, received, hidden_in, final_gain, turned, table, marks[3], marks[4], marks[3]
+    turned.append(fetch_turned(table, first, marks[2], marks[3], 3))
+    turned.append(fetch_turned(table, part, marks[3], marks[4], 6))
+
+    new_hidden, scaled, piece, late_part = vocab_head(
+        part, received, hidden_in, final_gain,
+        turned, split,
+        table, marks[4], columns, round_up(split + LANES, 2 * LANES),
     )
-    parts = [pair_sum(piece, "seq")]
-    piece = vocab_tail(scaled, square, late_part, table, marks[4], columns, tail_width)
-    parts.append(pair_sum(piece, "seq"))
-    logits, stats = vocab_logits(parts, draft_ids, bounds, rows, features)
+    own, other = pair_sum(piece, "seq")
+    piece = vocab_tail(
+        scaled, turned, late_part, split, columns, round_up(columns - split, 2 * LANES)
+    )
+    front, front_stats = vocab_front(own, other, draft_ids, split, columns, features)
+    own, other = pair_sum(piece, "seq")
+    back, stats = vocab_back(own, other, front_stats, split, columns - split)
     if is_power(heads):
         every = [stats] + [swap(stats, "heads", m) for m in range(1, heads)]
     else:
@@ -721,7 +774,7 @@
         every = [gathered[i] for i in range(heads)]
         while not is_power(len(every)):
             every.append(jnp.concatenate([jnp.full_like(stats[:, :1], NEGATIVE), jnp.zeros_like(stats[:, 1:])], axis=1))
-    log_probs, draft = vocab_finish(logits, every)
+    log_probs, draft = vocab_finish(front, back, every)
     return (new_hidden, log_probs, draft.reshape(rows))
 
 

time: 65 us -> 67.6 us (1.040)
  waiting for transfers between devices: 12.4 us -> 15.3 us
  starting transfers between devices: 17 us -> 14.7 us
  Pallas kernels: 34.8 us -> 36.7 us
    pallas_call x4 -> x5, Pallas kernels: 12.9 us -> 15.8 us  [the longest x3 14.5 us: fetch_turned(): pl.pallas_call(kernel, out_shape=pltpu.VMEM((table.shape[1], high - low),...]
    ppermute x9, waiting for transfers between devices: 12.4 us -> 15.3 us  [swap(): return lax.ppermute(array, axis, [(i, i ^ mask) for i in range(size)])]
    ppermute x9, starting transfers between devices: 17 us -> 14.7 us  [swap(): return lax.ppermute(array, axis, [(i, i ^ mask) for i in range(size)])]
    pallas_call x1, Pallas kernels: 4.8 us -> 3.58 us  [vocab_tail(): pl.pallas_call(kernel, out_shape=jax.ShapeDtypeStruct((rows * fold, width...]
    pallas_call x1, Pallas kernels: 2.65 us -> 3.86 us  [fetch_attention(): pl.pallas_call(kernel, out_shape=(pltpu.VMEM(cache.shape, cache.dtype), p...]
    pallas_call x1, Pallas kernels: 4.38 us -> 3.35 us  [vocab_head(): pl.pallas_call(kernel, out_shape=(jax.ShapeDtypeStruct((rows, depth), jnp...]
  transfers between devices with their start and end apart: 9 -> 9, of which waited for: 6 -> 6; matrix products, arithmetic and copies ran while one was open for 0% -> 0% of each run, Pallas kernels for 30% -> 28%
where the time goes in v4:
time: 67.6 us; the launch traced here: 67.5 us
  Pallas kernels  36.7 us (54%)
  waiting for transfers between devices  15.3 us (23%)
  starting transfers between devices  14.7 us (22%)
  between operations  0.76 us (1%)
    ppermute x9, waiting for transfers between devices, swap(): return lax.ppermute(array, axis, [(i, i ^ mask) for i in range(size)])  15.3 us
    ppermute x9, starting transfers between devices, swap(): return lax.ppermute(array, axis, [(i, i ^ mask) for i in range(size)])  14.7 us
    pallas_call x3, Pallas kernels, fetch_turned(): pl.pallas_call(kernel, out_shape=pltpu.VMEM((table.shape[1], high - low),...  14.5 us
    pallas_call x1, Pallas kernels, project(): pl.pallas_call(kernel, out_shape=jax.ShapeDtypeStruct((rows * fold, width...  4.35 us
    pallas_call x1, Pallas kernels, fetch_attention(): pl.pallas_call(kernel, out_shape=(pltpu.VMEM(cache.shape, cache.dtype), p...  3.86 us
    pallas_call x1, Pallas kernels, vocab_tail(): pl.pallas_call(kernel, out_shape=jax.ShapeDtypeStruct((rows * fold, width...  3.58 us
    pallas_call x1, Pallas kernels, attend(): pl.pallas_call(kernel, out_shape=(jax.ShapeDtypeStruct((requests * fold,...  3.49 us
    pallas_call x1, Pallas kernels, vocab_head(): pl.pallas_call(kernel, out_shape=(jax.ShapeDtypeStruct((rows, depth), jnp...  3.35 us
  transfers between devices with their start and end apart: 9, of which 6 were waited for; matrix products, arithmetic and copies ran while one was open for 0% of the time, Pallas kernels for 28%

profile of v4, /device:TPU:0, one launch (start us, length us, event | category | flops | bytes accessed | tf_op | source)
XLA Modules:
  0.0 67.5 jit_solution(13945805176812195731)
XLA Ops:
  0.6 4.3 %project.1.after_ref.own_ref = f32[24,1024]{1,0:T(8,128)S(1)} custom-call(bf16[12,2560]{1,0:T(8,128)(2,1)} %x_ref.1, f32[2560]{0:T(1024)} %gain_hbm.1, bf16[2560,1280]{1,0:T(8,128)(2,1)} %wq_ref.1, bf16[2560,640]{1,0:T(8,128)(2,1)} %bitcast.12), custom_call_target="tpu_custom_call" | custom-call | flops 25000000 | tf_op jit(solution)/shard_map/project/pallas_call | solution.py:140
  5.0 3.1 %collective-permute-start = (f32[24,1024]{1,0:T(8,128)S(1)}, f32[24,1024]{1,0:T(8,128)S(1)}, u32[]{:S(2)}, u32[]{:S(2)}) collective-permute-start(f32[24,1024]{1,0:T(8,128)S(1)} %project.1.after_ref.own_ref), channel_id=1, source_target_pairs={{0,4},{4,0},{1,5},{5,1},{2,6},{6,2},{3,7},{7,3},{8,12},{12,8},{9,1... | collective-permute-start | bytes 294920 | tf_op jit(solution)/shard_map/ppermute | solution.py:78
  8.0 0.0 copy-start.2
  8.1 3.9 %fetch_attention.1 = (bf16[12,256,640]{2,1,0:T(8,128)(2,1)S(1)}, bf16[320,1280]{1,0:T(8,128)(2,1)S(1)}, bf16[384,1280]{1,0:T(8,128)(2,1)S(1)}, bf16[2560,768]{1,0:T(8,128)(2,1)S(1)}) custom-call(bf16[12,256,640]{2,1,0:T(8,128)(2,1)} %bitcast.11, bf16[320,1280]{1,0:T(8,128)(2,1)} %bitcast.13, bf16[320,1280]{1,0:T(8,128)(2,1)} %bitcast.14, ...), custom_call_target="tpu_custom_call" | custom-call | flops 15000000 | tf_op jit(solution)/shard_map/fetch_attention/pallas_call | solution.py:254
  11.9 0.0 collective-permute-done.other_ref
  11.9 0.0 copy-done.2
  11.9 3.5 %attend.1 = (f32[24,768]{1,0:T(8,128)S(1)}, f32[12,1408]{1,0:T(8,128)S(1)}, bf16[1280,2560]{1,0:T(8,128)(2,1)S(1)}) custom-call(f32[24,1024]{1,0:T(8,128)S(1)} %project.1.after_ref.own_ref, f32[24,1024]{1,0:T(8,128)S(1)} %collective-permute-done.other_ref, s32[12]{0:T(128)S(1)} %copy-done.2, bf16[12,256,640]{2,1,0:T(8,128)(2,1)S(1)} %get-tuple-element.20.cache_ref, ...), custom_call_target="tpu_custom_call" | custom-call | flops 25000000 | tf_op jit(solution)/shard_map/attend/pallas_call | solution.py:375
  15.4 0.8 %collective-permute-start.1 = (f32[24,768]{1,0:T(8,128)S(1)}, f32[24,768]{1,0:T(8,128)S(1)}, u32[]{:S(2)}, u32[]{:S(2)}) collective-permute-start(f32[24,768]{1,0:T(8,128)S(1)} %get-tuple-element.23.own_ref.after_ref), channel_id=1, source_target_pairs={{0,4},{4,0},{1,5},{5,1},{2,6},{6,2},{3,7},{7,3},{8,12},{12,8},{9,1... | collective-permute-start | bytes 221192 | tf_op jit(solution)/shard_map/ppermute | solution.py:78
  16.2 3.6 %collective-permute-done.1.other_ref = f32[24,768]{1,0:T(8,128)S(1)} collective-permute-done((f32[24,768]{1,0:T(8,128)S(1)}, f32[24,768]{1,0:T(8,128)S(1)}, u32[]{:S(2)}, u32[]{:S(2)}) %collective-permute-start.1) | collective-permute-done | bytes 73760 | tf_op jit(solution)/shard_map/ppermute | solution.py:78
  19.9 1.1 %merge_out.1.after_ref = f32[24,1280]{1,0:T(8,128)S(1)} custom-call(f32[24,768]{1,0:T(8,128)S(1)} %get-tuple-element.23.own_ref.after_ref, f32[24,768]{1,0:T(8,128)S(1)} %collective-permute-done.1.other_ref, f32[12,1408]{1,0:T(8,128)S(1)} %get-tuple-element.24.local_ref, bf16[1280,2560]{1,0:T(8,128)(2,1)S(1)} %get-tuple-element.25.w_ref), custom_call_target="tpu_custom_call" | custom-call | flops 10000000 | tf_op jit(solution)/shard_map/merge_out/pallas_call | solution.py:442
  20.9 1.6 %collective-permute-start.2 = (f32[24,1280]{1,0:T(8,128)S(1)}, f32[24,1280]{1,0:T(8,128)S(1)}, u32[]{:S(2)}, u32[]{:S(2)}) collective-permute-start(f32[24,1280]{1,0:T(8,128)S(1)} %merge_out.1.after_ref), channel_id=1, source_target_pairs={{0,1},{1,0},{2,3},{3,2},{4,5},{5,4},{6,7},{7,6},{8,9},{9,8},{10,11... | collective-permute-start | bytes 368648 | tf_op jit(solution)/shard_map/ppermute | solution.py:78
  22.5 3.3 %collective-permute-done.2 = f32[24,1280]{1,0:T(8,128)S(1)} collective-permute-done((f32[24,1280]{1,0:T(8,128)S(1)}, f32[24,1280]{1,0:T(8,128)S(1)}, u32[]{:S(2)}, u32[]{:S(2)}) %collective-permute-start.2) | collective-permute-done | bytes 122912 | tf_op jit(solution)/shard_map/ppermute | solution.py:78
  25.8 2.8 %collective-permute-start.3 = (f32[24,1280]{1,0:T(8,128)S(1)}, f32[24,1280]{1,0:T(8,128)S(1)}, u32[]{:S(2)}, u32[]{:S(2)}) collective-permute-start(f32[24,1280]{1,0:T(8,128)S(1)} %add.3.after_ref.own_ref), channel_id=1, source_target_pairs={{0,2},{1,3},{2,0},{3,1},{4,6},{5,7},{6,4},{7,5},{8,10},{9,11},{10,... | collective-permute-start | bytes 368648 | tf_op jit(solution)/shard_map/ppermute | solution.py:78
  28.7 3.7 %fetch_turned.3.refs_1_ = bf16[2560,1536]{1,0:T(8,128)(2,1)S(1)} custom-call(bf16[8000,2560]{1,0:T(8,128)(2,1)} %bitcast.7, f32[24,768]{1,0:T(8,128)S(1)} %get-tuple-element.23.own_ref.after_ref), custom_call_target="tpu_custom_call" | custom-call | flops 15000000 | tf_op jit(solution)/shard_map/fetch_turned/pallas_call | solution.py:221
  32.4 4.3 %fetch_turned.4.refs_2_ = bf16[2560,1792]{1,0:T(8,128)(2,1)S(1)} custom-call(bf16[8000,2560]{1,0:T(8,128)(2,1)} %bitcast.8, f32[24,1280]{1,0:T(8,128)S(1)} %merge_out.1.after_ref), custom_call_target="tpu_custom_call" | custom-call | flops 15000000 | tf_op jit(solution)/shard_map/fetch_turned/pallas_call | solution.py:221
  36.7 0.0 copy-start
  36.7 0.0 copy-start.1
  36.7 6.5 %fetch_turned.5.refs_3_ = bf16[2560,3072]{1,0:T(8,128)(2,1)S(1)} custom-call(bf16[8000,2560]{1,0:T(8,128)(2,1)} %bitcast.9, f32[24,1280]{1,0:T(8,128)S(1)} %add.3.after_ref.own_ref), custom_call_target="tpu_custom_call" | custom-call | flops 30000000 | tf_op jit(solution)/shard_map/fetch_turned/pallas_call | solution.py:221
  43.2 0.0 collective-permute-done.3.other_ref
  43.2 0.0 copy-done
  43.2 0.0 copy-done.1
  43.2 3.4 %vocab_head.1 = (bf16[12,2560]{1,0:T(8,128)(2,1)}, bf16[12,2560]{1,0:T(8,128)(2,1)S(1)}, f32[24,1920]{1,0:T(8,128)S(1)}, bf16[832,2560]{1,0:T(8,128)(2,1)S(1)}) custom-call(f32[24,1280]{1,0:T(8,128)S(1)} %add.3.after_ref.own_ref, f32[24,1280]{1,0:T(8,128)S(1)} %collective-permute-done.3.other_ref, bf16[12,2560]{1,0:T(8,128)(2,1)S(1)} %copy-done, ...), custom_call_target="tpu_custom_call" | custom-call | flops 20000000 | tf_op jit(solution)/shard_map/vocab_head/pallas_call | solution.py:504
  46.6 0.0 copy-start.3
  46.6 3.6 %vocab_tail.1.own_ref = f32[24,2304]{1,0:T(8,128)S(1)} custom-call(bf16[12,2560]{1,0:T(8,128)(2,1)S(1)} %get-tuple-element.31.x_ref, bf16[2560,768]{1,0:T(8,128)(2,1)S(1)} %get-tuple-element.26.refs_0_, bf16[2560,1536]{1,0:T(8,128)(2,1)S(1)} %fetch_turned.3.refs_1_, bf16[2560,1792]{1,0:T(8,128)(2,1)S(1)} %fetch_turned.4.refs_2_, ...), custom_call_target="tpu_custom_call" | custom-call | flops 30000000 | tf_op jit(solution)/shard_map/vocab_tail/pallas_call | solution.py:534
  50.2 1.0 %collective-permute-start.5 = (f32[24,2304]{1,0:T(8,128)S(1)}, f32[24,2304]{1,0:T(8,128)S(1)}, u32[]{:S(2)}, u32[]{:S(2)}) collective-permute-start(f32[24,2304]{1,0:T(8,128)S(1)} %vocab_tail.1.own_ref), channel_id=1, source_target_pairs={{0,4},{4,0},{1,5},{5,1},{2,6},{6,2},{3,7},{7,3},{8,12},{12,8},{9,1... | collective-permute-start | bytes 663560 | tf_op jit(solution)/shard_map/ppermute | solution.py:78
  51.2 1.1 %collective-permute-start.4 = (f32[24,1920]{1,0:T(8,128)S(1)}, f32[24,1920]{1,0:T(8,128)S(1)}, u32[]{:S(2)}, u32[]{:S(2)}) collective-permute-start(f32[24,1920]{1,0:T(8,128)S(1)} %get-tuple-element.28.own_ref), channel_id=1, source_target_pairs={{0,4},{4,0},{1,5},{5,1},{2,6},{6,2},{3,7},{7,3},{8,12},{12,8},{9,1... | collective-permute-start | bytes 552968 | tf_op jit(solution)/shard_map/ppermute | solution.py:78
  52.2 6.1 %collective-permute-done.4.other_ref = f32[24,1920]{1,0:T(8,128)S(1)} collective-permute-done((f32[24,1920]{1,0:T(8,128)S(1)}, f32[24,1920]{1,0:T(8,128)S(1)}, u32[]{:S(2)}, u32[]{:S(2)}) %collective-permute-start.4) | collective-permute-done | bytes 184352 | tf_op jit(solution)/shard_map/ppermute | solution.py:78
  58.3 0.0 copy-done.3
  58.3 0.9 %vocab_front.1 = (f32[12,3584]{1,0:T(8,128)S(1)}, f32[24,128]{1,0:T(8,128)S(1)}) custom-call(s32[12]{0:T(128)S(1)} %copy-done.3, f32[24,1920]{1,0:T(8,128)S(1)} %get-tuple-element.28.own_ref, f32[24,1920]{1,0:T(8,128)S(1)} %collective-permute-done.4.other_ref), custom_call_target="tpu_custom_call" | custom-call | flops 5000000 | tf_op jit(solution)/shard_map/vocab_front/pallas_call | solution.py:569
  59.2 0.0 collective-permute-done.5.other_ref
  59.2 0.5 vocab_back.1
  59.6 1.4 %collective-permute-start.8 = (f32[12,128]{1,0:T(8,128)S(1)}, f32[12,128]{1,0:T(8,128)S(1)}, u32[]{:S(2)}, u32[]{:S(2)}) collective-permute-start(f32[12,128]{1,0:T(8,128)S(1)} %get-tuple-element.34.refs_0_), channel_id=1, source_target_pairs={{0,3},{1,2},{2,1},{3,0},{4,7},{5,6},{6,5},{7,4},{8,11},{9,10},{10,... | collective-permute-start | bytes 18440 | tf_op jit(solution)/shard_map/ppermute | solution.py:78
  61.0 1.7 %collective-permute-start.7 = (f32[12,128]{1,0:T(8,128)S(1)}, f32[12,128]{1,0:T(8,128)S(1)}, u32[]{:S(2)}, u32[]{:S(2)}) collective-permute-start(f32[12,128]{1,0:T(8,128)S(1)} %get-tuple-element.34.refs_0_), channel_id=1, source_target_pairs={{0,2},{1,3},{2,0},{3,1},{4,6},{5,7},{6,4},{7,5},{8,10},{9,11},{10,... | collective-permute-start | bytes 18440 | tf_op jit(solution)/shard_map/ppermute | solution.py:78
  62.7 1.3 %collective-permute-start.6 = (f32[12,128]{1,0:T(8,128)S(1)}, f32[12,128]{1,0:T(8,128)S(1)}, u32[]{:S(2)}, u32[]{:S(2)}) collective-permute-start(f32[12,128]{1,0:T(8,128)S(1)} %get-tuple-element.34.refs_0_), channel_id=1, source_target_pairs={{0,1},{1,0},{2,3},{3,2},{4,5},{5,4},{6,7},{7,6},{8,9},{9,8},{10,11... | collective-permute-start | bytes 18440 | tf_op jit(solution)/shard_map/ppermute | solution.py:78
  64.1 1.1 %collective-permute-done.8.refs_3_ = f32[12,128]{1,0:T(8,128)S(1)} collective-permute-done((f32[12,128]{1,0:T(8,128)S(1)}, f32[12,128]{1,0:T(8,128)S(1)}, u32[]{:S(2)}, u32[]{:S(2)}) %collective-permute-start.8) | collective-permute-done | bytes 6176 | tf_op jit(solution)/shard_map/ppermute | solution.py:78
  65.1 0.4 collective-permute-done.7.refs_2_
  65.6 0.8 %collective-permute-done.6.refs_1_ = f32[12,128]{1,0:T(8,128)S(1)} collective-permute-done((f32[12,128]{1,0:T(8,128)S(1)}, f32[12,128]{1,0:T(8,128)S(1)}, u32[]{:S(2)}, u32[]{:S(2)}) %collective-permute-start.6) | collective-permute-done | bytes 6176 | tf_op jit(solution)/shard_map/ppermute | solution.py:78
  66.4 1.1 %vocab_finish.1 = (f32[12,8000]{1,0:T(8,128)}, f32[1,12]{1,0:T(1,128)}) custom-call(f32[12,3584]{1,0:T(8,128)S(1)} %get-tuple-element.29.front_ref, f32[12,4416]{1,0:T(8,128)S(1)} %get-tuple-element.33.back_ref, f32[12,128]{1,0:T(8,128)S(1)} %get-tuple-element.34.refs_0_, f32[12,128]{1,0:T(8,128)S(1)} %collective-permute-done.6.refs_1_, ...), custom_call_target="tpu_custom_call" | custom-call | flops 5000000 | tf_op jit(solution)/shard_map/vocab_finish/pallas_call | solution.py:649
  (1 shorter events, 0.0 us)
Async XLA Ops:
  5.0 6.9 %collective-permute-start = (f32[24,1024]{1,0:T(8,128)S(1)}, f32[24,1024]{1,0:T(8,128)S(1)}, u32[]{:S(2)}, u32[]{:S(2)}) collective-permute-start(f32[24,1024]{1,0:T(8,128)S(1)} %project.1.after_ref.own_ref), channel_id=1, source_target_pairs={{0,4},{4,0},{1,5},{5,1},{2,6},{6,2},{3,7},{7,3},{8,12},{12,8},{9,1... | collective-permute-start | bytes 294920 | tf_op jit(solution)/shard_map/ppermute | solution.py:78
  8.0 3.9 %copy-start.2 = (s32[12]{0:T(128)S(1)}, s32[12]{0:T(128)}, u32[]{:S(2)}) copy-start(s32[12]{0:T(128)} %length_ref.1) | copy-start | bytes 148
  15.4 4.4 %collective-permute-start.1 = (f32[24,768]{1,0:T(8,128)S(1)}, f32[24,768]{1,0:T(8,128)S(1)}, u32[]{:S(2)}, u32[]{:S(2)}) collective-permute-start(f32[24,768]{1,0:T(8,128)S(1)} %get-tuple-element.23.own_ref.after_ref), channel_id=1, source_target_pairs={{0,4},{4,0},{1,5},{5,1},{2,6},{6,2},{3,7},{7,3},{8,12},{12,8},{9,1... | collective-permute-start | bytes 221192 | tf_op jit(solution)/shard_map/ppermute | solution.py:78
  20.9 4.9 %collective-permute-start.2 = (f32[24,1280]{1,0:T(8,128)S(1)}, f32[24,1280]{1,0:T(8,128)S(1)}, u32[]{:S(2)}, u32[]{:S(2)}) collective-permute-start(f32[24,1280]{1,0:T(8,128)S(1)} %merge_out.1.after_ref), channel_id=1, source_target_pairs={{0,1},{1,0},{2,3},{3,2},{4,5},{5,4},{6,7},{7,6},{8,9},{9,8},{10,11... | collective-permute-start | bytes 368648 | tf_op jit(solution)/shard_map/ppermute | solution.py:78
  25.8 17.4 %collective-permute-start.3 = (f32[24,1280]{1,0:T(8,128)S(1)}, f32[24,1280]{1,0:T(8,128)S(1)}, u32[]{:S(2)}, u32[]{:S(2)}) collective-permute-start(f32[24,1280]{1,0:T(8,128)S(1)} %add.3.after_ref.own_ref), channel_id=1, source_target_pairs={{0,2},{1,3},{2,0},{3,1},{4,6},{5,7},{6,4},{7,5},{8,10},{9,11},{10,... | collective-permute-start | bytes 368648 | tf_op jit(solution)/shard_map/ppermute | solution.py:78
  36.7 6.5 %copy-start = (bf16[12,2560]{1,0:T(8,128)(2,1)S(1)}, bf16[12,2560]{1,0:T(8,128)(2,1)}, u32[]{:S(2)}) copy-start(bf16[12,2560]{1,0:T(8,128)(2,1)} %x_ref.1) | copy-start | bytes 184324
  36.7 6.5 %copy-start.1 = (f32[2560]{0:T(1024)S(1)}, f32[2560]{0:T(1024)}, u32[]{:S(2)}) copy-start(f32[2560]{0:T(1024)} %gain_ref.1) | copy-start | bytes 30724
  46.6 11.7 %copy-start.3 = (s32[12]{0:T(128)S(1)}, s32[12]{0:T(128)}, u32[]{:S(2)}) copy-start(s32[12]{0:T(128)} %id_ref.1) | copy-start | bytes 148
  50.2 9.0 %collective-permute-start.5 = (f32[24,2304]{1,0:T(8,128)S(1)}, f32[24,2304]{1,0:T(8,128)S(1)}, u32[]{:S(2)}, u32[]{:S(2)}) collective-permute-start(f32[24,2304]{1,0:T(8,128)S(1)} %vocab_tail.1.own_ref), channel_id=1, source_target_pairs={{0,4},{4,0},{1,5},{5,1},{2,6},{6,2},{3,7},{7,3},{8,12},{12,8},{9,1... | collective-permute-start | bytes 663560 | tf_op jit(solution)/shard_map/ppermute | solution.py:78
  51.2 7.1 %collective-permute-start.4 = (f32[24,1920]{1,0:T(8,128)S(1)}, f32[24,1920]{1,0:T(8,128)S(1)}, u32[]{:S(2)}, u32[]{:S(2)}) collective-permute-start(f32[24,1920]{1,0:T(8,128)S(1)} %get-tuple-element.28.own_ref), channel_id=1, source_target_pairs={{0,4},{4,0},{1,5},{5,1},{2,6},{6,2},{3,7},{7,3},{8,12},{12,8},{9,1... | collective-permute-start | bytes 552968 | tf_op jit(solution)/shard_map/ppermute | solution.py:78
  59.6 5.5 %collective-permute-start.8 = (f32[12,128]{1,0:T(8,128)S(1)}, f32[12,128]{1,0:T(8,128)S(1)}, u32[]{:S(2)}, u32[]{:S(2)}) collective-permute-start(f32[12,128]{1,0:T(8,128)S(1)} %get-tuple-element.34.refs_0_), channel_id=1, source_target_pairs={{0,3},{1,2},{2,1},{3,0},{4,7},{5,6},{6,5},{7,4},{8,11},{9,10},{10,... | collective-permute-start | bytes 18440 | tf_op jit(solution)/shard_map/ppermute | solution.py:78
  61.0 4.5 %collective-permute-start.7 = (f32[12,128]{1,0:T(8,128)S(1)}, f32[12,128]{1,0:T(8,128)S(1)}, u32[]{:S(2)}, u32[]{:S(2)}) collective-permute-start(f32[12,128]{1,0:T(8,128)S(1)} %get-tuple-element.34.refs_0_), channel_id=1, source_target_pairs={{0,2},{1,3},{2,0},{3,1},{4,6},{5,7},{6,4},{7,5},{8,10},{9,11},{10,... | collective-permute-start | bytes 18440 | tf_op jit(solution)/shard_map/ppermute | solution.py:78
  62.7 3.7 %collective-permute-start.6 = (f32[12,128]{1,0:T(8,128)S(1)}, f32[12,128]{1,0:T(8,128)S(1)}, u32[]{:S(2)}, u32[]{:S(2)}) collective-permute-start(f32[12,128]{1,0:T(8,128)S(1)} %get-tuple-element.34.refs_0_), channel_id=1, source_target_pairs={{0,1},{1,0},{2,3},{3,2},{4,5},{5,4},{6,7},{7,6},{8,9},{9,8},{10,11... | collective-permute-start | bytes 18440 | tf_op jit(solution)/shard_map/ppermute | solution.py:78

commit v5 on v4

--- a/solution.py
+++ b/solution.py
@@ -13,6 +13,7 @@
 ROW_TILE = 16
 BLOCK = 256
 RING = 6
+LATE = 2
 EPSILON = 1e-05
 NEGATIVE = -1e30
 MIB = 1 << 20
@@ -93,7 +94,7 @@
     width = q_width + l_width + LANES
     fold = fold_of(rows, width)
     chunks = 5 if depth % (5 * LANES) == 0 else 1
-    step = depth // chunks
+    spans = [(depth * i // chunks, depth * (i + 1) // chunks) for i in range(chunks)]
 
     def kernel(x_hbm, gain_hbm, wq_ref, wl_ref, out_ref, x_ref, gain_ref, q_buf, l_buf, sems, ends, gate):
         small = [
@@ -104,8 +105,8 @@
             copy.start()
         fence(gate)
         copies = []
-        for c in range(chunks):
-            at = pl.ds(c * step, step)
+        for c, (a, b) in enumerate(spans):
+            at = pl.ds(a, b - a)
             copies.append(
                 (
                     pltpu.make_async_copy(wq_ref.at[at], q_buf.at[at], sems.at[0, c]),
@@ -121,16 +122,12 @@
         gained = (states * gain_ref[...].reshape(1, depth)).astype(jnp.bfloat16)
         square = jnp.sum(states * states, axis=1, keepdims=True)
         acc_q = acc_l = None
-        for c in range(chunks):
+        for c, (a, b) in enumerate(spans):
             for copy in copies[c]:
                 copy.wait()
-            x = gained[:, c * step : (c + 1) * step]
-            part_q = jnp.dot(
-                x, q_buf[c * step : (c + 1) * step, :], preferred_element_type=jnp.float32
-            )
-            part_l = jnp.dot(
-                x, l_buf[c * step : (c + 1) * step, :], preferred_element_type=jnp.float32
-            )
+            x = gained[:, a:b]
+            part_q = jnp.dot(x, q_buf[a:b, :], preferred_element_type=jnp.float32)
+            part_l = jnp.dot(x, l_buf[a:b, :], preferred_element_type=jnp.float32)
             acc_q = part_q if c == 0 else acc_q + part_q
             acc_l = part_l if c == 0 else acc_l + part_l
         put_folded(out_ref, rows, 0, acc_q)
@@ -268,7 +265,7 @@
     )(stored(cache), stored(key_up), stored(value_up), stored(table), after)
 
 
-def attend(own, other, lengths, cache, key_up, value_pad, features, w_out):
+def attend(own, other, lengths, cache, key_up, value_pad, features):
     requests, span, width = cache.shape
     rank = width // 2
     full = value_pad.shape[0]
@@ -281,15 +278,11 @@
     fold = fold_of(requests, send_width)
 
     def kernel(
-        own_ref, other_ref, length_ref, cache_ref, key_ref, value_ref, w_ref,
-        send_ref, local_ref, w_held, sems, gate, score_own, top_buf, total_buf, latent_buf, stack,
+        own_ref, other_ref, length_ref, cache_ref, key_ref, value_ref,
+        send_ref, local_ref, score_own, top_buf, total_buf, latent_buf, stack,
         score_buf, weight_buf, *tiles,
     ):
         absorbed, mixed = tiles[: full // LANES], tiles[full // LANES :]
-        copies = row_copies(w_ref, w_held, sems, 0, w_out.shape[0], w_out.shape[0] // 2)
-        for copy in copies:
-            copy.start()
-        fence(gate)
         refs = (own_ref, other_ref)
         square = get_folded(refs, requests, q_width + width, LANES)
         inv = lax.rsqrt(square[:, 0:1] / features + EPSILON)
@@ -325,8 +318,9 @@
                 jnp.sum(rows * latent_buf[b : b + 1, 0:full], axis=1, keepdims=True) * scaling,
                 (slot, LANES),
             )
+        lengths_row = length_ref[...].reshape(1, requests)
         for b, at in enumerate(spans):
-            live = positions < length_ref[b]
+            live = positions < lengths_row[:, b : b + 1]
             scores = jnp.where(live, score_buf[at, :] * scaling, NEGATIVE)
             top = jnp.max(scores, axis=1, keepdims=True)
             weights = jnp.where(live, jnp.exp(scores - top), 0.0)
@@ -368,8 +362,6 @@
         put_folded(send_ref, requests, q_width, tops)
         put_folded(send_ref, requests, q_width + LANES, totals)
         local_ref[:, q_width : q_width + LANES] = owns
-        for copy in copies:
-            copy.wait()
 
     tall = requests * slot
     return pl.pallas_call(
@@ -377,13 +369,10 @@
         out_shape=(
             jax.ShapeDtypeStruct((requests * fold, send_width // fold), jnp.float32),
             jax.ShapeDtypeStruct((requests, q_width + LANES), jnp.float32),
-            pltpu.VMEM(w_out.shape, w_out.dtype),
         ),
-        in_specs=[VMEM, VMEM, SMEM, VMEM, VMEM, VMEM, ANY],
-        out_specs=(VMEM,) * 3,
+        in_specs=[VMEM] * 6,
+        out_specs=(VMEM,) * 2,
         scratch_shapes=[
-            pltpu.SemaphoreType.DMA((2,)),
-            pltpu.SemaphoreType.REGULAR,
             pltpu.VMEM((tall, LANES), jnp.float32),
             pltpu.VMEM((tall, LANES), jnp.float32),
             pltpu.VMEM((tall, LANES), jnp.float32),
@@ -398,7 +387,6 @@
         name="attend",
     )(
         own, other, lengths, resident(cache), resident(key_up), resident(value_pad),
-        stored(w_out),
     )
 
 
@@ -454,8 +442,7 @@
 def put_terms(out_ref, rows, x, parts, low, high):
     depth = x.shape[1]
     half = depth // 2 if depth % (2 * LANES) == 0 else depth
-    base = 0
-    for ref, turned in parts:
+    for ref, turned, base in parts:
         count = ref.shape[1] if turned else ref.shape[0]
         first, last = max(low, base), min(high, base + count)
         for at in range(first, last, 2 * BLOCK):
@@ -473,20 +460,28 @@
                     )
                 total = term if total is None else total + term
             put_folded(out_ref, rows, at - low, total)
-        base += count
-
-
-def vocab_head(own, other, hidden, gain, turned, split, table, low_row, high_row, width):
+
+
+def late_scratch():
+    return [pltpu.SemaphoreType.DMA((LATE,)), pltpu.SemaphoreType.REGULAR]
+
+
+def late_copies(table_ref, held, sems, span):
+    step = round_up(-(-(span[1] - span[0]) // LATE), ROW_TILE)
+    return row_copies(table_ref, held, sems, span[0], span[1], step)
+
+
+def vocab_head(own, other, hidden, gain, parts, span, table, late):
     rows, depth = hidden.shape
+    low, high = span
+    width = round_up(high - low + LANES, 2 * LANES)
     fold = fold_of(rows, width)
-    count = len(turned)
-    pieces = 2
-    step = round_up(-(-(high_row - low_row) // pieces), ROW_TILE)
+    count = len(parts)
 
     def kernel(own_ref, other_ref, x_ref, gain_ref, *refs):
         table_ref = refs[count]
         new_ref, scaled_ref, out_ref, held, sems, gate = refs[count + 1 :]
-        copies = row_copies(table_ref, held, sems, low_row, high_row, step)
+        copies = late_copies(table_ref, held, sems, late)
         for copy in copies:
             copy.start()
         fence(gate)
@@ -496,71 +491,86 @@
         scaled = (updated * gain_ref[...].reshape(1, depth)).astype(jnp.bfloat16)
         scaled_ref[...] = scaled
         square = jnp.sum(updated * updated, axis=1, keepdims=True)
-        put_folded(out_ref, rows, split, jnp.broadcast_to(square, (rows, width - split)))
-        put_terms(out_ref, rows, scaled, [(ref, True) for ref in refs[:count]], 0, split)
+        used = high - low
+        put_folded(out_ref, rows, used, jnp.broadcast_to(square, (rows, width - used)))
+        held_parts = [(ref, True, part[2]) for ref, part in zip(refs[:count], parts)]
+        put_terms(out_ref, rows, scaled, held_parts, low, high)
         for copy in copies:
             copy.wait()
 
     return pl.pallas_call(
         kernel,
         out_shape=(
-            jax.ShapeDtypeStruct((rows, depth), jnp.bfloat16),
+            pltpu.VMEM((rows, depth), jnp.bfloat16),
             jax.ShapeDtypeStruct((rows, depth), jnp.bfloat16),
             jax.ShapeDtypeStruct((rows * fold, width // fold), jnp.float32),
-            pltpu.VMEM((high_row - low_row, depth), table.dtype),
+            pltpu.VMEM((late[1] - late[0], depth), table.dtype),
         ),
         in_specs=[VMEM] * (4 + count) + [ANY],
         out_specs=(VMEM,) * 4,
-        scratch_shapes=[pltpu.SemaphoreType.DMA((pieces,)), pltpu.SemaphoreType.REGULAR],
+        scratch_shapes=late_scratch(),
         compiler_params=params(3),
         cost_estimate=cost(4),
         name="vocab_head",
-    )(own, other, hidden, gain, *[resident(part) for part in turned], stored(table))
-
-
-def vocab_tail(scaled, turned, late_part, split, columns, width):
+    )(own, other, hidden, gain, *[resident(part[0]) for part in parts], stored(table))
+
+
+def vocab_more(scaled, parts, span):
     rows = scaled.shape[0]
+    low, high = span
+    width = round_up(high - low, 2 * LANES)
     fold = fold_of(rows, width)
-    count = len(turned)
+    count = len(parts)
 
     def kernel(x_ref, *refs):
-        late_ref, out_ref = refs[count:]
-        used = columns - split
+        out_ref = refs[count]
+        used = high - low
         if used < width:
             put_folded(out_ref, rows, used, jnp.zeros((rows, width - used), jnp.float32))
-        parts = [(ref, True) for ref in refs[:count]] + [(late_ref, False)]
-        put_terms(out_ref, rows, x_ref[...], parts, split, columns)
+        held_parts = [(ref, part[1], part[2]) for ref, part in zip(refs[:count], parts)]
+        put_terms(out_ref, rows, x_ref[...], held_parts, low, high)
 
     return pl.pallas_call(
         kernel,
         out_shape=jax.ShapeDtypeStruct((rows * fold, width // fold), jnp.float32),
-        in_specs=[VMEM] * (2 + count),
+        in_specs=[VMEM] * (1 + count),
         out_specs=VMEM,
         compiler_params=params(3),
         cost_estimate=cost(6),
-        name="vocab_tail",
-    )(scaled, *[resident(part) for part in turned], resident(late_part))
-
-
-def vocab_front(own, other, draft_ids, last, columns, features):
+        name="vocab_more",
+    )(scaled, *[resident(part[0]) for part in parts])
+
+
+def vocab_front(pairs, spans, draft_ids, columns, features, hidden):
     rows = draft_ids.shape[0]
-    width = own.shape[0] * own.shape[1] // rows
-
-    def kernel(id_ref, own_ref, other_ref, logit_ref, stat_ref):
-        pair = (own_ref, other_ref)
-        square = get_folded(pair, rows, width - LANES, LANES)
+    count = len(pairs)
+    width = pairs[0][0].shape[0] * pairs[0][0].shape[1] // rows
+
+    def kernel(id_ref, hidden_ref, *refs):
+        inputs = [refs[2 * i : 2 * i + 2] for i in range(count)]
+        logit_refs, (stat_ref, hidden_out) = refs[2 * count : 3 * count], refs[3 * count :]
+        hidden_out[...] = hidden_ref[...]
+        square = get_folded(inputs[0], rows, width - LANES, LANES)
         inv = lax.rsqrt(square[:, 0:1] / features + EPSILON)
         row = lax.broadcasted_iota(jnp.int32, (rows, 1), 0)
         wanted = jnp.zeros((rows, 1), jnp.int32)
         for r in range(rows):
             wanted = jnp.where(row == r, id_ref[r], wanted)
         wanted = wanted - lax.axis_index("heads") * columns
-        logits = get_folded(pair, rows, 0, last) * inv
-        logit_ref[...] = logits
-        column = lax.broadcasted_iota(jnp.int32, logits.shape, 1)
-        picked = jnp.sum(jnp.where(column == wanted, logits, 0.0), axis=1, keepdims=True)
-        top = jnp.max(logits, axis=1, keepdims=True)
-        total = jnp.sum(jnp.exp(logits - top), axis=1, keepdims=True)
+        top = jnp.full((rows, 1), NEGATIVE, jnp.float32)
+        picked = total = jnp.zeros((rows, 1), jnp.float32)
+        for pair, (low, high), logit_ref in zip(inputs, spans, logit_refs):
+            logits = get_folded(pair, rows, 0, high - low) * inv
+            logit_ref[...] = logits
+            column = low + lax.broadcasted_iota(jnp.int32, logits.shape, 1)
+            picked = picked + jnp.sum(
+                jnp.where(column == wanted, logits, 0.0), axis=1, keepdims=True
+            )
+            joined = jnp.maximum(top, jnp.max(logits, axis=1, keepdims=True))
+            total = total * jnp.exp(top - joined) + jnp.sum(
+                jnp.exp(logits - joined), axis=1, keepdims=True
+            )
+            top = joined
         lane = lax.broadcasted_iota(jnp.int32, (rows, LANES), 1)
         stats = jnp.where(lane == 1, total, jnp.where(lane == 2, picked, inv))
         stat_ref[0:rows, :] = jnp.where(lane == 0, top, stats)
@@ -568,28 +578,30 @@
 
     return pl.pallas_call(
         kernel,
-        out_shape=(
-            pltpu.VMEM((rows, last), jnp.float32),
+        out_shape=tuple(pltpu.VMEM((rows, high - low), jnp.float32) for low, high in spans)
+        + (
             jax.ShapeDtypeStruct((2 * rows, LANES), jnp.float32),
+            jax.ShapeDtypeStruct(hidden.shape, hidden.dtype),
         ),
-        in_specs=[SMEM, VMEM, VMEM],
-        out_specs=(VMEM, VMEM),
+        in_specs=[SMEM] + [VMEM] * (2 * count + 1),
+        out_specs=(VMEM,) * (count + 2),
         compiler_params=params(4),
         cost_estimate=cost(1),
         name="vocab_front",
-    )(draft_ids, own, other)
-
-
-def vocab_back(own, other, front_stats, first, count):
+    )(draft_ids, resident(hidden), *[array for pair in pairs for array in pair])
+
+
+def vocab_back(own, other, front_stats, span):
     rows = front_stats.shape[0] // 2
+    low, high = span
 
     def kernel(front_ref, own_ref, other_ref, logit_ref, stat_ref):
         top_front, total_front = front_ref[0:rows, 0:1], front_ref[0:rows, 1:2]
         picked_front, inv = front_ref[0:rows, 2:3], front_ref[0:rows, 3:4]
         wanted = front_ref[rows : 2 * rows, 0:1].astype(jnp.int32)
-        logits = get_folded((own_ref, other_ref), rows, 0, count) * inv
+        logits = get_folded((own_ref, other_ref), rows, 0, high - low) * inv
         logit_ref[...] = logits
-        column = first + lax.broadcasted_iota(jnp.int32, logits.shape, 1)
+        column = low + lax.broadcasted_iota(jnp.int32, logits.shape, 1)
         picked = picked_front + jnp.sum(
             jnp.where(column == wanted, logits, 0.0), axis=1, keepdims=True
         )
@@ -605,7 +617,7 @@
     return pl.pallas_call(
         kernel,
         out_shape=(
-            pltpu.VMEM((rows, count), jnp.float32),
+            pltpu.VMEM((rows, high - low), jnp.float32),
             jax.ShapeDtypeStruct((rows, LANES), jnp.float32),
         ),
         in_specs=[VMEM] * 3,
@@ -616,13 +628,14 @@
     )(front_stats, own, other)
 
 
-def vocab_finish(front, back, stats):
-    rows, split = front.shape
-    columns = split + back.shape[1]
-    count = len(stats)
-
-    def kernel(front_ref, back_ref, *refs):
-        stat_refs, out_ref, draft_ref = refs[:count], refs[count], refs[count + 1]
+def vocab_finish(pieces, spans, stats):
+    rows = pieces[0].shape[0]
+    columns = sum(high - low for low, high in spans)
+    count = len(pieces)
+
+    def kernel(*refs):
+        piece_refs, stat_refs = refs[:count], refs[count:-2]
+        out_ref, draft_ref = refs[-2:]
         state = [(ref[:, 0:1], ref[:, 1:2], ref[:, 2:3]) for ref in stat_refs]
         while len(state) > 1:
             joined = []
@@ -638,8 +651,8 @@
             state = joined
         top, total, picked = state[0]
         log_total = top + jnp.log(total)
-        out_ref[:, 0:split] = front_ref[...] - log_total
-        out_ref[:, split:columns] = back_ref[...] - log_total
+        for ref, (low, high) in zip(piece_refs, spans):
+            out_ref[:, low:high] = ref[...] - log_total
         draft = picked - log_total
         row = lax.broadcasted_iota(jnp.int32, (rows, LANES), 0)
         lane = lax.broadcasted_iota(jnp.int32, (rows, LANES), 1)
@@ -652,12 +665,12 @@
             jax.ShapeDtypeStruct((rows, columns), jnp.float32),
             jax.ShapeDtypeStruct((1, rows), jnp.float32),
         ),
-        in_specs=[VMEM] * (2 + count),
+        in_specs=[VMEM] * (count + len(stats)),
         out_specs=(VMEM, VMEM),
         compiler_params=params(4),
         cost_estimate=cost(1),
         name="vocab_finish",
-    )(resident(front), resident(back), *stats)
+    )(*[resident(piece) for piece in pieces], *stats)
 
 
 def pair_sum(array, axis):
@@ -719,8 +732,8 @@
     def mark(share):
         return int(columns * share) // BLOCK * BLOCK
 
-    marks = [0, mark(0.096), mark(0.288), mark(0.512), mark(0.896), columns]
-    split = mark(0.448)
+    marks = [mark(0.16), mark(0.256), mark(0.352), mark(0.576), columns]
+    spans = [(mark(0.544), columns), (0, mark(0.544))]
 
     sums = project(
         hidden_in,
@@ -733,12 +746,12 @@
         latent_cache[:, 0], key_up[0], value_up[0], table, sums, marks[0], marks[1], 3
     )
     turned = [turned]
-    packed, local, out_table = attend(
-        own, other, lengths, cache, keys, values, features, w_out
+    packed, local = attend(
+        own, other, lengths, cache, keys, values, features
     )
     own, other = pair_softmax(packed, "seq", rows, q_width)
     turned.append(fetch_turned(table, packed, marks[1], marks[2], 3))
-    part = merge_out(own, other, local, out_table, rows)
+    part = merge_out(own, other, local, w_out, rows)
 
     heads = lax.axis_size("heads")
     first = part
@@ -755,26 +768,27 @@
     turned.append(fetch_turned(table, first, marks[2], marks[3], 3))
     turned.append(fetch_turned(table, part, marks[3], marks[4], 6))
 
-    new_hidden, scaled, piece, late_part = vocab_head(
-        part, received, hidden_in, final_gain,
-        turned, split,
-        table, marks[4], columns, round_up(split + LANES, 2 * LANES),
+    parts = [(part_, True, low) for part_, low in zip(turned, marks)]
+    updated, scaled, piece, late_part = vocab_head(
+        part, received, hidden_in, final_gain, parts, spans[0], table, (0, marks[0])
     )
+    pairs = [pair_sum(piece, "seq")]
+    piece = vocab_more(scaled, parts + [(late_part, False, 0)], spans[1])
     own, other = pair_sum(piece, "seq")
-    piece = vocab_tail(
-        scaled, turned, late_part, split, columns, round_up(columns - split, 2 * LANES)
+    *logits, front_stats, new_hidden = vocab_front(
+        pairs, spans[:1], draft_ids, columns, features, updated
     )
-    front, front_stats = vocab_front(own, other, draft_ids, split, columns, features)
-    own, other = pair_sum(piece, "seq")
-    back, stats = vocab_back(own, other, front_stats, split, columns - split)
+    back, stats = vocab_back(own, other, front_stats, spans[1])
     if is_power(heads):
-        every = [stats] + [swap(stats, "heads", m) for m in range(1, heads)]
+        every = [stats]
+        for mask in range(1, heads):
+            every.append(swap(stats, "heads", mask))
     else:
         gathered = lax.all_gather(stats, "heads")
         every = [gathered[i] for i in range(heads)]
         while not is_power(len(every)):
             every.append(jnp.concatenate([jnp.full_like(stats[:, :1], NEGATIVE), jnp.zeros_like(stats[:, 1:])], axis=1))
-    log_probs, draft = vocab_finish(front, back, every)
+    log_probs, draft = vocab_finish(logits + [back], spans, every)
     return (new_hidden, log_probs, draft.reshape(rows))
 
 

time: 67.6 us -> 65.5 us (0.969)
  Pallas kernels: 36.7 us -> 34.8 us
    pallas_call x1, Pallas kernels: 3.49 us -> 1.8 us  [attend(): pl.pallas_call(kernel, out_shape=(jax.ShapeDtypeStruct((requests * fold,...]
    pallas_call x3, Pallas kernels: 14.5 us -> 13.8 us  [fetch_turned(): pl.pallas_call(kernel, out_shape=pltpu.VMEM((table.shape[1], high - low),...]
  transfers between devices with their start and end apart: 9 -> 9, of which waited for: 6 -> 6; matrix products, arithmetic and copies ran while one was open for 0% -> 0% of each run, Pallas kernels for 28% -> 29%
where the time goes in v5:
time: 65.5 us; the launch traced here: 65.3 us
  Pallas kernels  34.8 us (53%)
  waiting for transfers between devices  15.2 us (23%)
  starting transfers between devices  14.6 us (22%)
  between operations  0.76 us (1%)
    ppermute x9, waiting for transfers between devices, swap(): return lax.ppermute(array, axis, [(i, i ^ mask) for i in range(size)])  15.2 us
    ppermute x9, starting transfers between devices, swap(): return lax.ppermute(array, axis, [(i, i ^ mask) for i in range(size)])  14.6 us
    pallas_call x3, Pallas kernels, fetch_turned(): pl.pallas_call(kernel, out_shape=pltpu.VMEM((table.shape[1], high - low),...  13.8 us
    pallas_call x1, Pallas kernels, project(): pl.pallas_call(kernel, out_shape=jax.ShapeDtypeStruct((rows * fold, width...  4.35 us
    pallas_call x1, Pallas kernels, fetch_attention(): pl.pallas_call(kernel, out_shape=(pltpu.VMEM(cache.shape, cache.dtype), p...  3.99 us
    pallas_call x1, Pallas kernels, vocab_more(): pl.pallas_call(kernel, out_shape=jax.ShapeDtypeStruct((rows * fold, width...  3.82 us
    pallas_call x1, Pallas kernels, vocab_head(): pl.pallas_call(kernel, out_shape=(pltpu.VMEM((rows, depth), jnp.bfloat16)...  2.96 us
    pallas_call x1, Pallas kernels, attend(): pl.pallas_call(kernel, out_shape=(jax.ShapeDtypeStruct((requests * fold,...  1.8 us
  transfers between devices with their start and end apart: 9, of which 6 were waited for; matrix products, arithmetic and copies ran while one was open for 0% of the time, Pallas kernels for 29%

profile of v5, /device:TPU:0, one launch (start us, length us, event | category | flops | bytes accessed | tf_op | source)
XLA Modules:
  0.0 65.3 jit_solution(7567680007895892567)
XLA Ops:
  0.6 4.3 %project.1.after_ref.own_ref = f32[24,1024]{1,0:T(8,128)S(1)} custom-call(bf16[12,2560]{1,0:T(8,128)(2,1)} %x_ref.1, f32[2560]{0:T(1024)} %gain_hbm.1, bf16[2560,1280]{1,0:T(8,128)(2,1)} %wq_ref.1, bf16[2560,640]{1,0:T(8,128)(2,1)} %bitcast.14), custom_call_target="tpu_custom_call" | custom-call | flops 25000000 | tf_op jit(solution)/shard_map/project/pallas_call | solution.py:137
  5.0 3.1 %collective-permute-start = (f32[24,1024]{1,0:T(8,128)S(1)}, f32[24,1024]{1,0:T(8,128)S(1)}, u32[]{:S(2)}, u32[]{:S(2)}) collective-permute-start(f32[24,1024]{1,0:T(8,128)S(1)} %project.1.after_ref.own_ref), channel_id=1, source_target_pairs={{0,4},{4,0},{1,5},{5,1},{2,6},{6,2},{3,7},{7,3},{8,12},{12,8},{9,1... | collective-permute-start | bytes 294920 | tf_op jit(solution)/shard_map/ppermute | solution.py:79
  8.0 0.0 slice-start
  8.1 0.0 copy-start.2
  8.1 0.0 slice-start.1
  8.1 4.0 %fetch_attention.1 = (bf16[12,256,640]{2,1,0:T(8,128)(2,1)S(1)}, bf16[320,1280]{1,0:T(8,128)(2,1)S(1)}, bf16[384,1280]{1,0:T(8,128)(2,1)S(1)}, bf16[2560,768]{1,0:T(8,128)(2,1)S(1)}) custom-call(bf16[12,256,640]{2,1,0:T(8,128)(2,1)} %bitcast.13, bf16[320,1280]{1,0:T(8,128)(2,1)} %bitcast.15, bf16[320,1280]{1,0:T(8,128)(2,1)} %bitcast.16, ...), custom_call_target="tpu_custom_call" | custom-call | flops 15000000 | tf_op jit(solution)/shard_map/fetch_attention/pallas_call | solution.py:251
  12.1 0.0 collective-permute-done.other_ref
  12.1 0.0 copy-done.2
  12.1 1.8 %attend.1 = (f32[24,768]{1,0:T(8,128)S(1)}, f32[12,1408]{1,0:T(8,128)S(1)}) custom-call(f32[24,1024]{1,0:T(8,128)S(1)} %project.1.after_ref.own_ref, f32[24,1024]{1,0:T(8,128)S(1)} %collective-permute-done.other_ref, s32[12]{0:T(128)S(1)} %copy-done.2, bf16[12,256,640]{2,1,0:T(8,128)(2,1)S(1)} %get-tuple-element.20.cache_ref, ...), custom_call_target="tpu_custom_call" | custom-call | flops 25000000 | tf_op jit(solution)/shard_map/attend/pallas_call | solution.py:367
  13.9 0.7 %collective-permute-start.1 = (f32[24,768]{1,0:T(8,128)S(1)}, f32[24,768]{1,0:T(8,128)S(1)}, u32[]{:S(2)}, u32[]{:S(2)}) collective-permute-start(f32[24,768]{1,0:T(8,128)S(1)} %get-tuple-element.23.own_ref.after_ref), channel_id=1, source_target_pairs={{0,4},{4,0},{1,5},{5,1},{2,6},{6,2},{3,7},{7,3},{8,12},{12,8},{9,1... | collective-permute-start | bytes 221192 | tf_op jit(solution)/shard_map/ppermute | solution.py:79
  14.5 3.8 %collective-permute-done.1.other_ref = f32[24,768]{1,0:T(8,128)S(1)} collective-permute-done((f32[24,768]{1,0:T(8,128)S(1)}, f32[24,768]{1,0:T(8,128)S(1)}, u32[]{:S(2)}, u32[]{:S(2)}) %collective-permute-start.1) | collective-permute-done | bytes 73760 | tf_op jit(solution)/shard_map/ppermute | solution.py:79
  18.3 0.0 slice-done
  18.3 0.0 slice-done.1
  18.3 1.1 %merge_out.1.after_ref = f32[24,1280]{1,0:T(8,128)S(1)} custom-call(f32[24,768]{1,0:T(8,128)S(1)} %get-tuple-element.23.own_ref.after_ref, f32[24,768]{1,0:T(8,128)S(1)} %collective-permute-done.1.other_ref, f32[12,1408]{1,0:T(8,128)S(1)} %get-tuple-element.24.local_ref, bf16[1280,2560]{1,0:T(8,128)(2,1)S(1)} %bitcast.7), custom_call_target="tpu_custom_call" | custom-call | flops 10000000 | tf_op jit(solution)/shard_map/merge_out/pallas_call | solution.py:430
  19.4 1.6 %collective-permute-start.2 = (f32[24,1280]{1,0:T(8,128)S(1)}, f32[24,1280]{1,0:T(8,128)S(1)}, u32[]{:S(2)}, u32[]{:S(2)}) collective-permute-start(f32[24,1280]{1,0:T(8,128)S(1)} %merge_out.1.after_ref), channel_id=1, source_target_pairs={{0,1},{1,0},{2,3},{3,2},{4,5},{5,4},{6,7},{7,6},{8,9},{9,8},{10,11... | collective-permute-start | bytes 368648 | tf_op jit(solution)/shard_map/ppermute | solution.py:79
  21.0 3.3 %collective-permute-done.2 = f32[24,1280]{1,0:T(8,128)S(1)} collective-permute-done((f32[24,1280]{1,0:T(8,128)S(1)}, f32[24,1280]{1,0:T(8,128)S(1)}, u32[]{:S(2)}, u32[]{:S(2)}) %collective-permute-start.2) | collective-permute-done | bytes 122912 | tf_op jit(solution)/shard_map/ppermute | solution.py:79
  24.3 2.8 %collective-permute-start.3 = (f32[24,1280]{1,0:T(8,128)S(1)}, f32[24,1280]{1,0:T(8,128)S(1)}, u32[]{:S(2)}, u32[]{:S(2)}) collective-permute-start(f32[24,1280]{1,0:T(8,128)S(1)} %add.3.after_ref.own_ref), channel_id=1, source_target_pairs={{0,2},{1,3},{2,0},{3,1},{4,6},{5,7},{6,4},{7,5},{8,10},{9,11},{10,... | collective-permute-start | bytes 368648 | tf_op jit(solution)/shard_map/ppermute | solution.py:79
  27.1 2.5 %fetch_turned.3.refs_1_ = bf16[2560,768]{1,0:T(8,128)(2,1)S(1)} custom-call(bf16[8000,2560]{1,0:T(8,128)(2,1)} %bitcast.9, f32[24,768]{1,0:T(8,128)S(1)} %get-tuple-element.23.own_ref.after_ref), custom_call_target="tpu_custom_call" | custom-call | flops 15000000 | tf_op jit(solution)/shard_map/fetch_turned/pallas_call | solution.py:218
  29.6 4.3 %fetch_turned.4.refs_2_ = bf16[2560,1792]{1,0:T(8,128)(2,1)S(1)} custom-call(bf16[8000,2560]{1,0:T(8,128)(2,1)} %bitcast.10, f32[24,1280]{1,0:T(8,128)S(1)} %merge_out.1.after_ref), custom_call_target="tpu_custom_call" | custom-call | flops 15000000 | tf_op jit(solution)/shard_map/fetch_turned/pallas_call | solution.py:218
  34.0 0.0 copy-start
  34.0 0.0 copy-start.1
  34.0 6.9 %fetch_turned.5.refs_3_ = bf16[2560,3392]{1,0:T(8,128)(2,1)S(1)} custom-call(bf16[8000,2560]{1,0:T(8,128)(2,1)} %bitcast.11, f32[24,1280]{1,0:T(8,128)S(1)} %add.3.after_ref.own_ref), custom_call_target="tpu_custom_call" | custom-call | flops 30000000 | tf_op jit(solution)/shard_map/fetch_turned/pallas_call | solution.py:218
  40.9 0.0 collective-permute-done.3.other_ref
  40.9 0.0 copy-done
  40.9 0.0 copy-done.1
  41.0 3.0 %vocab_head.1 = (bf16[12,2560]{1,0:T(8,128)(2,1)S(1)}, bf16[12,2560]{1,0:T(8,128)(2,1)S(1)}, f32[24,1920]{1,0:T(8,128)S(1)}, bf16[1280,2560]{1,0:T(8,128)(2,1)S(1)}) custom-call(f32[24,1280]{1,0:T(8,128)S(1)} %add.3.after_ref.own_ref, f32[24,1280]{1,0:T(8,128)S(1)} %collective-permute-done.3.other_ref, bf16[12,2560]{1,0:T(8,128)(2,1)S(1)} %copy-done, ...), custom_call_target="tpu_custom_call" | custom-call | flops 20000000 | tf_op jit(solution)/shard_map/vocab_head/pallas_call | solution.py:501
  43.9 0.0 copy-start.3
  43.9 3.8 %vocab_more.1.own_ref = f32[24,2176]{1,0:T(8,128)S(1)} custom-call(bf16[12,2560]{1,0:T(8,128)(2,1)S(1)} %get-tuple-element.31.x_ref, bf16[2560,768]{1,0:T(8,128)(2,1)S(1)} %get-tuple-element.25.refs_0_, bf16[2560,768]{1,0:T(8,128)(2,1)S(1)} %fetch_turned.3.refs_1_, bf16[2560,1792]{1,0:T(8,128)(2,1)S(1)} %fetch_turned.4.refs_2_, ...), custom_call_target="tpu_custom_call" | custom-call | flops 30000000 | tf_op jit(solution)/shard_map/vocab_more/pallas_call | solution.py:533
  47.8 0.7 %collective-permute-start.5 = (f32[24,2176]{1,0:T(8,128)S(1)}, f32[24,2176]{1,0:T(8,128)S(1)}, u32[]{:S(2)}, u32[]{:S(2)}) collective-permute-start(f32[24,2176]{1,0:T(8,128)S(1)} %vocab_more.1.own_ref), channel_id=1, source_target_pairs={{0,4},{4,0},{1,5},{5,1},{2,6},{6,2},{3,7},{7,3},{8,12},{12,8},{9,1... | collective-permute-start | bytes 626696 | tf_op jit(solution)/shard_map/ppermute | solution.py:79
  48.5 1.3 %collective-permute-start.4 = (f32[24,1920]{1,0:T(8,128)S(1)}, f32[24,1920]{1,0:T(8,128)S(1)}, u32[]{:S(2)}, u32[]{:S(2)}) collective-permute-start(f32[24,1920]{1,0:T(8,128)S(1)} %get-tuple-element.27.refs_0_), channel_id=1, source_target_pairs={{0,4},{4,0},{1,5},{5,1},{2,6},{6,2},{3,7},{7,3},{8,12},{12,8},{9,1... | collective-permute-start | bytes 552968 | tf_op jit(solution)/shard_map/ppermute | solution.py:79
  49.8 5.8 %collective-permute-done.4.refs_1_ = f32[24,1920]{1,0:T(8,128)S(1)} collective-permute-done((f32[24,1920]{1,0:T(8,128)S(1)}, f32[24,1920]{1,0:T(8,128)S(1)}, u32[]{:S(2)}, u32[]{:S(2)}) %collective-permute-start.4) | collective-permute-done | bytes 184352 | tf_op jit(solution)/shard_map/ppermute | solution.py:79
  55.6 0.0 copy-done.3
  55.6 1.4 %vocab_front.1 = (f32[12,3648]{1,0:T(8,128)S(1)}, f32[24,128]{1,0:T(8,128)S(1)}, bf16[12,2560]{1,0:T(8,128)(2,1)}) custom-call(s32[12]{0:T(128)S(1)} %copy-done.3, bf16[12,2560]{1,0:T(8,128)(2,1)S(1)} %get-tuple-element.26.hidden_ref, f32[24,1920]{1,0:T(8,128)S(1)} %get-tuple-element.27.refs_0_, f32[24,1920]{1,0:T(8,128)S(1)} %collective-permute-done.4.refs_1_), custom_call_target="tpu_custom_call" | custom-call | flops 5000000 | tf_op jit(solution)/shard_map/vocab_front/pallas_call | solution.py:579
  57.0 0.0 collective-permute-done.5.other_ref
  57.0 0.5 vocab_back.1
  57.5 1.4 %collective-permute-start.8 = (f32[12,128]{1,0:T(8,128)S(1)}, f32[12,128]{1,0:T(8,128)S(1)}, u32[]{:S(2)}, u32[]{:S(2)}) collective-permute-start(f32[12,128]{1,0:T(8,128)S(1)} %get-tuple-element.34.refs_2_), channel_id=1, source_target_pairs={{0,3},{1,2},{2,1},{3,0},{4,7},{5,6},{6,5},{7,4},{8,11},{9,10},{10,... | collective-permute-start | bytes 18440 | tf_op jit(solution)/shard_map/ppermute | solution.py:79
  58.9 1.7 %collective-permute-start.7 = (f32[12,128]{1,0:T(8,128)S(1)}, f32[12,128]{1,0:T(8,128)S(1)}, u32[]{:S(2)}, u32[]{:S(2)}) collective-permute-start(f32[12,128]{1,0:T(8,128)S(1)} %get-tuple-element.34.refs_2_), channel_id=1, source_target_pairs={{0,2},{1,3},{2,0},{3,1},{4,6},{5,7},{6,4},{7,5},{8,10},{9,11},{10,... | collective-permute-start | bytes 18440 | tf_op jit(solution)/shard_map/ppermute | solution.py:79
  60.5 1.3 %collective-permute-start.6 = (f32[12,128]{1,0:T(8,128)S(1)}, f32[12,128]{1,0:T(8,128)S(1)}, u32[]{:S(2)}, u32[]{:S(2)}) collective-permute-start(f32[12,128]{1,0:T(8,128)S(1)} %get-tuple-element.34.refs_2_), channel_id=1, source_target_pairs={{0,1},{1,0},{2,3},{3,2},{4,5},{5,4},{6,7},{7,6},{8,9},{9,8},{10,11... | collective-permute-start | bytes 18440 | tf_op jit(solution)/shard_map/ppermute | solution.py:79
  61.9 1.1 %collective-permute-done.8.refs_5_ = f32[12,128]{1,0:T(8,128)S(1)} collective-permute-done((f32[12,128]{1,0:T(8,128)S(1)}, f32[12,128]{1,0:T(8,128)S(1)}, u32[]{:S(2)}, u32[]{:S(2)}) %collective-permute-start.8) | collective-permute-done | bytes 6176 | tf_op jit(solution)/shard_map/ppermute | solution.py:79
  63.0 0.4 collective-permute-done.7.refs_4_
  63.4 0.8 %collective-permute-done.6.refs_3_ = f32[12,128]{1,0:T(8,128)S(1)} collective-permute-done((f32[12,128]{1,0:T(8,128)S(1)}, f32[12,128]{1,0:T(8,128)S(1)}, u32[]{:S(2)}, u32[]{:S(2)}) %collective-permute-start.6) | collective-permute-done | bytes 6176 | tf_op jit(solution)/shard_map/ppermute | solution.py:79
  64.2 1.1 %vocab_finish.1 = (f32[12,8000]{1,0:T(8,128)}, f32[1,12]{1,0:T(1,128)}) custom-call(f32[12,3648]{1,0:T(8,128)S(1)} %get-tuple-element.29.refs_0_, f32[12,4352]{1,0:T(8,128)S(1)} %get-tuple-element.33.refs_1_, f32[12,128]{1,0:T(8,128)S(1)} %get-tuple-element.34.refs_2_, f32[12,128]{1,0:T(8,128)S(1)} %collective-permute-done.6.refs_3_, ...), custom_call_target="tpu_custom_call" | custom-call | flops 5000000 | tf_op jit(solution)/shard_map/vocab_finish/pallas_call | solution.py:662
  (2 shorter events, 0.0 us)
Async XLA Ops:
  5.0 7.1 %collective-permute-start = (f32[24,1024]{1,0:T(8,128)S(1)}, f32[24,1024]{1,0:T(8,128)S(1)}, u32[]{:S(2)}, u32[]{:S(2)}) collective-permute-start(f32[24,1024]{1,0:T(8,128)S(1)} %project.1.after_ref.own_ref), channel_id=1, source_target_pairs={{0,4},{4,0},{1,5},{5,1},{2,6},{6,2},{3,7},{7,3},{8,12},{12,8},{9,1... | collective-permute-start | bytes 294920 | tf_op jit(solution)/shard_map/ppermute | solution.py:79
  8.0 10.3 %slice-start = ((s8[6553600]{0:T(1024)(128)(4,1)}), s8[4194304]{0:T(1024)(128)(4,1)S(1)}, s32[]{:S(2)}) async-start(s8[6553600]{0:T(1024)(128)(4,1)} %bitcast.6), calls=%async_computation | async-start | bytes 8388608
  8.1 4.0 %copy-start.2 = (s32[12]{0:T(128)S(1)}, s32[12]{0:T(128)}, u32[]{:S(2)}) copy-start(s32[12]{0:T(128)} %length_ref.1) | copy-start | bytes 148
  8.1 10.3 %slice-start.1 = ((s8[6553600]{0:T(1024)(128)(4,1)}), s8[2359296]{0:T(1024)(128)(4,1)S(1)}, s32[]{:S(2)}) async-start(s8[6553600]{0:T(1024)(128)(4,1)} %bitcast.6), calls=%async_computation.1 | async-start | bytes 4718592
  13.9 4.4 %collective-permute-start.1 = (f32[24,768]{1,0:T(8,128)S(1)}, f32[24,768]{1,0:T(8,128)S(1)}, u32[]{:S(2)}, u32[]{:S(2)}) collective-permute-start(f32[24,768]{1,0:T(8,128)S(1)} %get-tuple-element.23.own_ref.after_ref), channel_id=1, source_target_pairs={{0,4},{4,0},{1,5},{5,1},{2,6},{6,2},{3,7},{7,3},{8,12},{12,8},{9,1... | collective-permute-start | bytes 221192 | tf_op jit(solution)/shard_map/ppermute | solution.py:79
  19.4 4.9 %collective-permute-start.2 = (f32[24,1280]{1,0:T(8,128)S(1)}, f32[24,1280]{1,0:T(8,128)S(1)}, u32[]{:S(2)}, u32[]{:S(2)}) collective-permute-start(f32[24,1280]{1,0:T(8,128)S(1)} %merge_out.1.after_ref), channel_id=1, source_target_pairs={{0,1},{1,0},{2,3},{3,2},{4,5},{5,4},{6,7},{7,6},{8,9},{9,8},{10,11... | collective-permute-start | bytes 368648 | tf_op jit(solution)/shard_map/ppermute | solution.py:79
  24.3 16.6 %collective-permute-start.3 = (f32[24,1280]{1,0:T(8,128)S(1)}, f32[24,1280]{1,0:T(8,128)S(1)}, u32[]{:S(2)}, u32[]{:S(2)}) collective-permute-start(f32[24,1280]{1,0:T(8,128)S(1)} %add.3.after_ref.own_ref), channel_id=1, source_target_pairs={{0,2},{1,3},{2,0},{3,1},{4,6},{5,7},{6,4},{7,5},{8,10},{9,11},{10,... | collective-permute-start | bytes 368648 | tf_op jit(solution)/shard_map/ppermute | solution.py:79
  34.0 7.0 %copy-start = (bf16[12,2560]{1,0:T(8,128)(2,1)S(1)}, bf16[12,2560]{1,0:T(8,128)(2,1)}, u32[]{:S(2)}) copy-start(bf16[12,2560]{1,0:T(8,128)(2,1)} %x_ref.1) | copy-start | bytes 184324
  34.0 7.0 %copy-start.1 = (f32[2560]{0:T(1024)S(1)}, f32[2560]{0:T(1024)}, u32[]{:S(2)}) copy-start(f32[2560]{0:T(1024)} %gain_ref.1) | copy-start | bytes 30724
  43.9 11.7 %copy-start.3 = (s32[12]{0:T(128)S(1)}, s32[12]{0:T(128)}, u32[]{:S(2)}) copy-start(s32[12]{0:T(128)} %id_ref.1) | copy-start | bytes 148
  47.8 9.3 %collective-permute-start.5 = (f32[24,2176]{1,0:T(8,128)S(1)}, f32[24,2176]{1,0:T(8,128)S(1)}, u32[]{:S(2)}, u32[]{:S(2)}) collective-permute-start(f32[24,2176]{1,0:T(8,128)S(1)} %vocab_more.1.own_ref), channel_id=1, source_target_pairs={{0,4},{4,0},{1,5},{5,1},{2,6},{6,2},{3,7},{7,3},{8,12},{12,8},{9,1... | collective-permute-start | bytes 626696 | tf_op jit(solution)/shard_map/ppermute | solution.py:79
  48.5 7.1 %collective-permute-start.4 = (f32[24,1920]{1,0:T(8,128)S(1)}, f32[24,1920]{1,0:T(8,128)S(1)}, u32[]{:S(2)}, u32[]{:S(2)}) collective-permute-start(f32[24,1920]{1,0:T(8,128)S(1)} %get-tuple-element.27.refs_0_), channel_id=1, source_target_pairs={{0,4},{4,0},{1,5},{5,1},{2,6},{6,2},{3,7},{7,3},{8,12},{12,8},{9,1... | collective-permute-start | bytes 552968 | tf_op jit(solution)/shard_map/ppermute | solution.py:79
  57.5 5.5 %collective-permute-start.8 = (f32[12,128]{1,0:T(8,128)S(1)}, f32[12,128]{1,0:T(8,128)S(1)}, u32[]{:S(2)}, u32[]{:S(2)}) collective-permute-start(f32[12,128]{1,0:T(8,128)S(1)} %get-tuple-element.34.refs_2_), channel_id=1, source_target_pairs={{0,3},{1,2},{2,1},{3,0},{4,7},{5,6},{6,5},{7,4},{8,11},{9,10},{10,... | collective-permute-start | bytes 18440 | tf_op jit(solution)/shard_map/ppermute | solution.py:79
  58.9 4.5 %collective-permute-start.7 = (f32[12,128]{1,0:T(8,128)S(1)}, f32[12,128]{1,0:T(8,128)S(1)}, u32[]{:S(2)}, u32[]{:S(2)}) collective-permute-start(f32[12,128]{1,0:T(8,128)S(1)} %get-tuple-element.34.refs_2_), channel_id=1, source_target_pairs={{0,2},{1,3},{2,0},{3,1},{4,6},{5,7},{6,4},{7,5},{8,10},{9,11},{10,... | collective-permute-start | bytes 18440 | tf_op jit(solution)/shard_map/ppermute | solution.py:79
  60.5 3.7 %collective-permute-start.6 = (f32[12,128]{1,0:T(8,128)S(1)}, f32[12,128]{1,0:T(8,128)S(1)}, u32[]{:S(2)}, u32[]{:S(2)}) collective-permute-start(f32[12,128]{1,0:T(8,128)S(1)} %get-tuple-element.34.refs_2_), channel_id=1, source_target_pairs={{0,1},{1,0},{2,3},{3,2},{4,5},{5,4},{6,7},{7,6},{8,9},{9,8},{10,11... | collective-permute-start | bytes 18440 | tf_op jit(solution)/shard_map/ppermute | solution.py:79

commit v6 on v5

--- a/solution.py
+++ b/solution.py
@@ -12,7 +12,7 @@
 LANES = 128
 ROW_TILE = 16
 BLOCK = 256
-RING = 6
+RING = 7
 LATE = 2
 EPSILON = 1e-05
 NEGATIVE = -1e30
@@ -182,12 +182,19 @@
 def turn_rows(copies, held_ref, out_ref):
     slots, _, depth = held_ref.shape
     count = out_ref.shape[1]
+    one = lax.broadcasted_iota(jnp.int32, (BLOCK, BLOCK), 0)
+    one = (one == lax.broadcasted_iota(jnp.int32, (BLOCK, BLOCK), 1)).astype(out_ref.dtype)
     for i, copy in enumerate(copies):
         copy.wait()
         a, b = i * BLOCK, min((i + 1) * BLOCK, count)
         for k in range(0, depth, BLOCK):
             end = min(k + BLOCK, depth)
-            out_ref[k:end, a:b] = held_ref[i % slots, 0 : b - a, k:end].T
+            tile = held_ref[i % slots, 0 : b - a, k:end]
+            if k // BLOCK % 3 == 1 and end - k == BLOCK:
+                tile = lax.dot_general(one, tile, NT, preferred_element_type=jnp.float32)
+                out_ref[k:end, a:b] = tile.astype(out_ref.dtype)
+            else:
+                out_ref[k:end, a:b] = tile.T
         if i + slots < len(copies):
             copies[i + slots].start()
 
@@ -363,7 +370,7 @@
         put_folded(send_ref, requests, q_width + LANES, totals)
         local_ref[:, q_width : q_width + LANES] = owns
 
-    tall = requests * slot
+    tall = round_up(requests, 8) * slot
     return pl.pallas_call(
         kernel,
         out_shape=(
@@ -732,8 +739,8 @@
     def mark(share):
         return int(columns * share) // BLOCK * BLOCK
 
-    marks = [mark(0.16), mark(0.256), mark(0.352), mark(0.576), columns]
-    spans = [(mark(0.544), columns), (0, mark(0.544))]
+    marks = [mark(0.16), mark(0.256), mark(0.352), mark(0.592), columns]
+    spans = [(mark(0.48), columns), (0, mark(0.48))]
 
     sums = project(
         hidden_in,

time: 65.5 us -> 61.5 us (0.939)
  waiting for transfers between devices: 15.2 us -> 11.9 us
  Pallas kernels: 34.8 us -> 34 us
    ppermute x9, waiting for transfers between devices: 15.2 us -> 11.9 us  [swap(): return lax.ppermute(array, axis, [(i, i ^ mask) for i in range(size)])]
  transfers between devices with their start and end apart: 9 -> 9, of which waited for: 6 -> 7; matrix products, arithmetic and copies ran while one was open for 0% -> 0% of each run, Pallas kernels for 29% -> 36%
where the time goes in v6:
time: 61.5 us; the launch traced here: 61.4 us
  Pallas kernels  34 us (55%)
  starting transfers between devices  14.7 us (24%)
  waiting for transfers between devices  11.9 us (19%)
  between operations  0.76 us (1%)
    ppermute x9, starting transfers between devices, swap(): return lax.ppermute(array, axis, [(i, i ^ mask) for i in range(size)])  14.7 us
    pallas_call x3, Pallas kernels, fetch_turned(): pl.pallas_call(kernel, out_shape=pltpu.VMEM((table.shape[1], high - low),...  13.4 us
    ppermute x9, waiting for transfers between devices, swap(): return lax.ppermute(array, axis, [(i, i ^ mask) for i in range(size)])  11.9 us
    pallas_call x1, Pallas kernels, project(): pl.pallas_call(kernel, out_shape=jax.ShapeDtypeStruct((rows * fold, width...  4.35 us
    pallas_call x1, Pallas kernels, fetch_attention(): pl.pallas_call(kernel, out_shape=(pltpu.VMEM(cache.shape, cache.dtype), p...  3.99 us
    pallas_call x1, Pallas kernels, vocab_more(): pl.pallas_call(kernel, out_shape=jax.ShapeDtypeStruct((rows * fold, width...  3.48 us
    pallas_call x1, Pallas kernels, vocab_head(): pl.pallas_call(kernel, out_shape=(pltpu.VMEM((rows, depth), jnp.bfloat16)...  2.97 us
    pallas_call x1, Pallas kernels, attend(): pl.pallas_call(kernel, out_shape=(jax.ShapeDtypeStruct((requests * fold,...  1.8 us
  transfers between devices with their start and end apart: 9, of which 7 were waited for; matrix products, arithmetic and copies ran while one was open for 0% of the time, Pallas kernels for 36%

profile of v6, /device:TPU:0, one launch (start us, length us, event | category | flops | bytes accessed | tf_op | source)
XLA Modules:
  0.0 61.4 jit_solution(3003521089861544388)
XLA Ops:
  0.6 4.3 %project.1.after_ref.own_ref = f32[24,1024]{1,0:T(8,128)S(1)} custom-call(bf16[12,2560]{1,0:T(8,128)(2,1)} %x_ref.1, f32[2560]{0:T(1024)} %gain_hbm.1, bf16[2560,1280]{1,0:T(8,128)(2,1)} %wq_ref.1, bf16[2560,640]{1,0:T(8,128)(2,1)} %bitcast.14), custom_call_target="tpu_custom_call" | custom-call | flops 25000000 | tf_op jit(solution)/shard_map/project/pallas_call | solution.py:137
  5.0 3.1 %collective-permute-start = (f32[24,1024]{1,0:T(8,128)S(1)}, f32[24,1024]{1,0:T(8,128)S(1)}, u32[]{:S(2)}, u32[]{:S(2)}) collective-permute-start(f32[24,1024]{1,0:T(8,128)S(1)} %project.1.after_ref.own_ref), channel_id=1, source_target_pairs={{0,4},{4,0},{1,5},{5,1},{2,6},{6,2},{3,7},{7,3},{8,12},{12,8},{9,1... | collective-permute-start | bytes 294920 | tf_op jit(solution)/shard_map/ppermute | solution.py:79
  8.0 0.0 slice-start
  8.1 0.0 copy-start.2
  8.1 0.0 slice-start.1
  8.1 4.0 %fetch_attention.1 = (bf16[12,256,640]{2,1,0:T(8,128)(2,1)S(1)}, bf16[320,1280]{1,0:T(8,128)(2,1)S(1)}, bf16[384,1280]{1,0:T(8,128)(2,1)S(1)}, bf16[2560,768]{1,0:T(8,128)(2,1)S(1)}) custom-call(bf16[12,256,640]{2,1,0:T(8,128)(2,1)} %bitcast.13, bf16[320,1280]{1,0:T(8,128)(2,1)} %bitcast.15, bf16[320,1280]{1,0:T(8,128)(2,1)} %bitcast.16, ...), custom_call_target="tpu_custom_call" | custom-call | flops 15000000 | tf_op jit(solution)/shard_map/fetch_attention/pallas_call | solution.py:258
  12.1 0.0 collective-permute-done.other_ref
  12.1 0.0 copy-done.2
  12.1 1.8 %attend.1 = (f32[24,768]{1,0:T(8,128)S(1)}, f32[12,1408]{1,0:T(8,128)S(1)}) custom-call(f32[24,1024]{1,0:T(8,128)S(1)} %project.1.after_ref.own_ref, f32[24,1024]{1,0:T(8,128)S(1)} %collective-permute-done.other_ref, s32[12]{0:T(128)S(1)} %copy-done.2, bf16[12,256,640]{2,1,0:T(8,128)(2,1)S(1)} %get-tuple-element.20.cache_ref, ...), custom_call_target="tpu_custom_call" | custom-call | flops 25000000 | tf_op jit(solution)/shard_map/attend/pallas_call | solution.py:374
  13.9 0.7 %collective-permute-start.1 = (f32[24,768]{1,0:T(8,128)S(1)}, f32[24,768]{1,0:T(8,128)S(1)}, u32[]{:S(2)}, u32[]{:S(2)}) collective-permute-start(f32[24,768]{1,0:T(8,128)S(1)} %get-tuple-element.23.own_ref.after_ref), channel_id=1, source_target_pairs={{0,4},{4,0},{1,5},{5,1},{2,6},{6,2},{3,7},{7,3},{8,12},{12,8},{9,1... | collective-permute-start | bytes 221192 | tf_op jit(solution)/shard_map/ppermute | solution.py:79
  14.5 3.8 %collective-permute-done.1.other_ref = f32[24,768]{1,0:T(8,128)S(1)} collective-permute-done((f32[24,768]{1,0:T(8,128)S(1)}, f32[24,768]{1,0:T(8,128)S(1)}, u32[]{:S(2)}, u32[]{:S(2)}) %collective-permute-start.1) | collective-permute-done | bytes 73760 | tf_op jit(solution)/shard_map/ppermute | solution.py:79
  18.3 0.0 slice-done
  18.3 0.0 slice-done.1
  18.3 1.1 %merge_out.1.after_ref = f32[24,1280]{1,0:T(8,128)S(1)} custom-call(f32[24,768]{1,0:T(8,128)S(1)} %get-tuple-element.23.own_ref.after_ref, f32[24,768]{1,0:T(8,128)S(1)} %collective-permute-done.1.other_ref, f32[12,1408]{1,0:T(8,128)S(1)} %get-tuple-element.24.local_ref, bf16[1280,2560]{1,0:T(8,128)(2,1)S(1)} %bitcast.7), custom_call_target="tpu_custom_call" | custom-call | flops 10000000 | tf_op jit(solution)/shard_map/merge_out/pallas_call | solution.py:437
  19.4 1.6 %collective-permute-start.2 = (f32[24,1280]{1,0:T(8,128)S(1)}, f32[24,1280]{1,0:T(8,128)S(1)}, u32[]{:S(2)}, u32[]{:S(2)}) collective-permute-start(f32[24,1280]{1,0:T(8,128)S(1)} %merge_out.1.after_ref), channel_id=1, source_target_pairs={{0,1},{1,0},{2,3},{3,2},{4,5},{5,4},{6,7},{7,6},{8,9},{9,8},{10,11... | collective-permute-start | bytes 368648 | tf_op jit(solution)/shard_map/ppermute | solution.py:79
  21.0 3.3 %collective-permute-done.2 = f32[24,1280]{1,0:T(8,128)S(1)} collective-permute-done((f32[24,1280]{1,0:T(8,128)S(1)}, f32[24,1280]{1,0:T(8,128)S(1)}, u32[]{:S(2)}, u32[]{:S(2)}) %collective-permute-start.2) | collective-permute-done | bytes 122912 | tf_op jit(solution)/shard_map/ppermute | solution.py:79
  24.3 2.8 %collective-permute-start.3 = (f32[24,1280]{1,0:T(8,128)S(1)}, f32[24,1280]{1,0:T(8,128)S(1)}, u32[]{:S(2)}, u32[]{:S(2)}) collective-permute-start(f32[24,1280]{1,0:T(8,128)S(1)} %add.3.after_ref.own_ref), channel_id=1, source_target_pairs={{0,2},{1,3},{2,0},{3,1},{4,6},{5,7},{6,4},{7,5},{8,10},{9,11},{10,... | collective-permute-start | bytes 368648 | tf_op jit(solution)/shard_map/ppermute | solution.py:79
  27.1 2.4 %fetch_turned.3.refs_1_ = bf16[2560,768]{1,0:T(8,128)(2,1)S(1)} custom-call(bf16[8000,2560]{1,0:T(8,128)(2,1)} %bitcast.9, f32[24,768]{1,0:T(8,128)S(1)} %get-tuple-element.23.own_ref.after_ref), custom_call_target="tpu_custom_call" | custom-call | flops 15000000 | tf_op jit(solution)/shard_map/fetch_turned/pallas_call | solution.py:225
  29.6 4.0 %fetch_turned.4.refs_2_ = bf16[2560,1792]{1,0:T(8,128)(2,1)S(1)} custom-call(bf16[8000,2560]{1,0:T(8,128)(2,1)} %bitcast.10, f32[24,1280]{1,0:T(8,128)S(1)} %merge_out.1.after_ref), custom_call_target="tpu_custom_call" | custom-call | flops 15000000 | tf_op jit(solution)/shard_map/fetch_turned/pallas_call | solution.py:225
  33.6 0.0 copy-start
  33.6 0.0 copy-start.1
  33.6 6.9 %fetch_turned.5.refs_3_ = bf16[2560,3392]{1,0:T(8,128)(2,1)S(1)} custom-call(bf16[8000,2560]{1,0:T(8,128)(2,1)} %bitcast.11, f32[24,1280]{1,0:T(8,128)S(1)} %add.3.after_ref.own_ref), custom_call_target="tpu_custom_call" | custom-call | flops 30000000 | tf_op jit(solution)/shard_map/fetch_turned/pallas_call | solution.py:225
  40.6 0.0 collective-permute-done.3.other_ref
  40.6 0.0 copy-done
  40.6 0.0 copy-done.1
  40.6 3.0 %vocab_head.1 = (bf16[12,2560]{1,0:T(8,128)(2,1)S(1)}, bf16[12,2560]{1,0:T(8,128)(2,1)S(1)}, f32[24,2176]{1,0:T(8,128)S(1)}, bf16[1280,2560]{1,0:T(8,128)(2,1)S(1)}) custom-call(f32[24,1280]{1,0:T(8,128)S(1)} %add.3.after_ref.own_ref, f32[24,1280]{1,0:T(8,128)S(1)} %collective-permute-done.3.other_ref, bf16[12,2560]{1,0:T(8,128)(2,1)S(1)} %copy-done, ...), custom_call_target="tpu_custom_call" | custom-call | flops 20000000 | tf_op jit(solution)/shard_map/vocab_head/pallas_call | solution.py:508
  43.6 0.8 %collective-permute-start.4 = (f32[24,2176]{1,0:T(8,128)S(1)}, f32[24,2176]{1,0:T(8,128)S(1)}, u32[]{:S(2)}, u32[]{:S(2)}) collective-permute-start(f32[24,2176]{1,0:T(8,128)S(1)} %get-tuple-element.27.refs_0_), channel_id=1, source_target_pairs={{0,4},{4,0},{1,5},{5,1},{2,6},{6,2},{3,7},{7,3},{8,12},{12,8},{9,1... | collective-permute-start | bytes 626696 | tf_op jit(solution)/shard_map/ppermute | solution.py:79
  44.3 0.0 copy-start.3
  44.3 3.5 %vocab_more.1.own_ref = f32[24,1920]{1,0:T(8,128)S(1)} custom-call(bf16[12,2560]{1,0:T(8,128)(2,1)S(1)} %get-tuple-element.31.x_ref, bf16[2560,768]{1,0:T(8,128)(2,1)S(1)} %get-tuple-element.25.refs_0_, bf16[2560,768]{1,0:T(8,128)(2,1)S(1)} %fetch_turned.3.refs_1_, bf16[2560,1792]{1,0:T(8,128)(2,1)S(1)} %fetch_turned.4.refs_2_, ...), custom_call_target="tpu_custom_call" | custom-call | flops 30000000 | tf_op jit(solution)/shard_map/vocab_more/pallas_call | solution.py:540
  47.8 1.4 %collective-permute-start.5 = (f32[24,1920]{1,0:T(8,128)S(1)}, f32[24,1920]{1,0:T(8,128)S(1)}, u32[]{:S(2)}, u32[]{:S(2)}) collective-permute-start(f32[24,1920]{1,0:T(8,128)S(1)} %vocab_more.1.own_ref), channel_id=1, source_target_pairs={{0,4},{4,0},{1,5},{5,1},{2,6},{6,2},{3,7},{7,3},{8,12},{12,8},{9,1... | collective-permute-start | bytes 552968 | tf_op jit(solution)/shard_map/ppermute | solution.py:79
  49.2 1.8 %collective-permute-done.4.refs_1_ = f32[24,2176]{1,0:T(8,128)S(1)} collective-permute-done((f32[24,2176]{1,0:T(8,128)S(1)}, f32[24,2176]{1,0:T(8,128)S(1)}, u32[]{:S(2)}, u32[]{:S(2)}) %collective-permute-start.4) | collective-permute-done | bytes 208928 | tf_op jit(solution)/shard_map/ppermute | solution.py:79
  51.0 0.0 copy-done.3
  51.0 1.4 %vocab_front.1 = (f32[12,4160]{1,0:T(8,128)S(1)}, f32[24,128]{1,0:T(8,128)S(1)}, bf16[12,2560]{1,0:T(8,128)(2,1)}) custom-call(s32[12]{0:T(128)S(1)} %copy-done.3, bf16[12,2560]{1,0:T(8,128)(2,1)S(1)} %get-tuple-element.26.hidden_ref, f32[24,2176]{1,0:T(8,128)S(1)} %get-tuple-element.27.refs_0_, f32[24,2176]{1,0:T(8,128)S(1)} %collective-permute-done.4.refs_1_), custom_call_target="tpu_custom_call" | custom-call | flops 5000000 | tf_op jit(solution)/shard_map/vocab_front/pallas_call | solution.py:586
  52.4 1.0 %collective-permute-done.5.other_ref = f32[24,1920]{1,0:T(8,128)S(1)} collective-permute-done((f32[24,1920]{1,0:T(8,128)S(1)}, f32[24,1920]{1,0:T(8,128)S(1)}, u32[]{:S(2)}, u32[]{:S(2)}) %collective-permute-start.5) | collective-permute-done | bytes 184352 | tf_op jit(solution)/shard_map/ppermute | solution.py:79
  53.4 0.5 vocab_back.1
  53.8 1.1 %collective-permute-start.8 = (f32[12,128]{1,0:T(8,128)S(1)}, f32[12,128]{1,0:T(8,128)S(1)}, u32[]{:S(2)}, u32[]{:S(2)}) collective-permute-start(f32[12,128]{1,0:T(8,128)S(1)} %get-tuple-element.34.refs_2_), channel_id=1, source_target_pairs={{0,3},{1,2},{2,1},{3,0},{4,7},{5,6},{6,5},{7,4},{8,11},{9,10},{10,... | collective-permute-start | bytes 18440 | tf_op jit(solution)/shard_map/ppermute | solution.py:79
  54.9 1.7 %collective-permute-start.7 = (f32[12,128]{1,0:T(8,128)S(1)}, f32[12,128]{1,0:T(8,128)S(1)}, u32[]{:S(2)}, u32[]{:S(2)}) collective-permute-start(f32[12,128]{1,0:T(8,128)S(1)} %get-tuple-element.34.refs_2_), channel_id=1, source_target_pairs={{0,2},{1,3},{2,0},{3,1},{4,6},{5,7},{6,4},{7,5},{8,10},{9,11},{10,... | collective-permute-start | bytes 18440 | tf_op jit(solution)/shard_map/ppermute | solution.py:79
  56.6 1.6 %collective-permute-start.6 = (f32[12,128]{1,0:T(8,128)S(1)}, f32[12,128]{1,0:T(8,128)S(1)}, u32[]{:S(2)}, u32[]{:S(2)}) collective-permute-start(f32[12,128]{1,0:T(8,128)S(1)} %get-tuple-element.34.refs_2_), channel_id=1, source_target_pairs={{0,1},{1,0},{2,3},{3,2},{4,5},{5,4},{6,7},{7,6},{8,9},{9,8},{10,11... | collective-permute-start | bytes 18440 | tf_op jit(solution)/shard_map/ppermute | solution.py:79
  58.2 1.1 %collective-permute-done.8.refs_5_ = f32[12,128]{1,0:T(8,128)S(1)} collective-permute-done((f32[12,128]{1,0:T(8,128)S(1)}, f32[12,128]{1,0:T(8,128)S(1)}, u32[]{:S(2)}, u32[]{:S(2)}) %collective-permute-start.8) | collective-permute-done | bytes 6176 | tf_op jit(solution)/shard_map/ppermute | solution.py:79
  59.3 0.2 collective-permute-done.7.refs_4_
  59.5 0.8 %collective-permute-done.6.refs_3_ = f32[12,128]{1,0:T(8,128)S(1)} collective-permute-done((f32[12,128]{1,0:T(8,128)S(1)}, f32[12,128]{1,0:T(8,128)S(1)}, u32[]{:S(2)}, u32[]{:S(2)}) %collective-permute-start.6) | collective-permute-done | bytes 6176 | tf_op jit(solution)/shard_map/ppermute | solution.py:79
  60.3 1.1 %vocab_finish.1 = (f32[12,8000]{1,0:T(8,128)}, f32[1,12]{1,0:T(1,128)}) custom-call(f32[12,4160]{1,0:T(8,128)S(1)} %get-tuple-element.29.refs_0_, f32[12,3840]{1,0:T(8,128)S(1)} %get-tuple-element.33.refs_1_, f32[12,128]{1,0:T(8,128)S(1)} %get-tuple-element.34.refs_2_, f32[12,128]{1,0:T(8,128)S(1)} %collective-permute-done.6.refs_3_, ...), custom_call_target="tpu_custom_call" | custom-call | flops 5000000 | tf_op jit(solution)/shard_map/vocab_finish/pallas_call | solution.py:669
  (2 shorter events, 0.0 us)
Async XLA Ops:
  5.0 7.1 %collective-permute-start = (f32[24,1024]{1,0:T(8,128)S(1)}, f32[24,1024]{1,0:T(8,128)S(1)}, u32[]{:S(2)}, u32[]{:S(2)}) collective-permute-start(f32[24,1024]{1,0:T(8,128)S(1)} %project.1.after_ref.own_ref), channel_id=1, source_target_pairs={{0,4},{4,0},{1,5},{5,1},{2,6},{6,2},{3,7},{7,3},{8,12},{12,8},{9,1... | collective-permute-start | bytes 294920 | tf_op jit(solution)/shard_map/ppermute | solution.py:79
  8.0 10.3 %slice-start = ((s8[6553600]{0:T(1024)(128)(4,1)}), s8[4194304]{0:T(1024)(128)(4,1)S(1)}, s32[]{:S(2)}) async-start(s8[6553600]{0:T(1024)(128)(4,1)} %bitcast.6), calls=%async_computation | async-start | bytes 8388608
  8.1 4.0 %copy-start.2 = (s32[12]{0:T(128)S(1)}, s32[12]{0:T(128)}, u32[]{:S(2)}) copy-start(s32[12]{0:T(128)} %length_ref.1) | copy-start | bytes 148
  8.1 10.3 %slice-start.1 = ((s8[6553600]{0:T(1024)(128)(4,1)}), s8[2359296]{0:T(1024)(128)(4,1)S(1)}, s32[]{:S(2)}) async-start(s8[6553600]{0:T(1024)(128)(4,1)} %bitcast.6), calls=%async_computation.1 | async-start | bytes 4718592
  13.9 4.4 %collective-permute-start.1 = (f32[24,768]{1,0:T(8,128)S(1)}, f32[24,768]{1,0:T(8,128)S(1)}, u32[]{:S(2)}, u32[]{:S(2)}) collective-permute-start(f32[24,768]{1,0:T(8,128)S(1)} %get-tuple-element.23.own_ref.after_ref), channel_id=1, source_target_pairs={{0,4},{4,0},{1,5},{5,1},{2,6},{6,2},{3,7},{7,3},{8,12},{12,8},{9,1... | collective-permute-start | bytes 221192 | tf_op jit(solution)/shard_map/ppermute | solution.py:79
  19.4 4.9 %collective-permute-start.2 = (f32[24,1280]{1,0:T(8,128)S(1)}, f32[24,1280]{1,0:T(8,128)S(1)}, u32[]{:S(2)}, u32[]{:S(2)}) collective-permute-start(f32[24,1280]{1,0:T(8,128)S(1)} %merge_out.1.after_ref), channel_id=1, source_target_pairs={{0,1},{1,0},{2,3},{3,2},{4,5},{5,4},{6,7},{7,6},{8,9},{9,8},{10,11... | collective-permute-start | bytes 368648 | tf_op jit(solution)/shard_map/ppermute | solution.py:79
  24.3 16.3 %collective-permute-start.3 = (f32[24,1280]{1,0:T(8,128)S(1)}, f32[24,1280]{1,0:T(8,128)S(1)}, u32[]{:S(2)}, u32[]{:S(2)}) collective-permute-start(f32[24,1280]{1,0:T(8,128)S(1)} %add.3.after_ref.own_ref), channel_id=1, source_target_pairs={{0,2},{1,3},{2,0},{3,1},{4,6},{5,7},{6,4},{7,5},{8,10},{9,11},{10,... | collective-permute-start | bytes 368648 | tf_op jit(solution)/shard_map/ppermute | solution.py:79
  33.6 7.0 %copy-start = (bf16[12,2560]{1,0:T(8,128)(2,1)S(1)}, bf16[12,2560]{1,0:T(8,128)(2,1)}, u32[]{:S(2)}) copy-start(bf16[12,2560]{1,0:T(8,128)(2,1)} %x_ref.1) | copy-start | bytes 184324
  33.6 7.0 %copy-start.1 = (f32[2560]{0:T(1024)S(1)}, f32[2560]{0:T(1024)}, u32[]{:S(2)}) copy-start(f32[2560]{0:T(1024)} %gain_ref.1) | copy-start | bytes 30724
  43.6 7.4 %collective-permute-start.4 = (f32[24,2176]{1,0:T(8,128)S(1)}, f32[24,2176]{1,0:T(8,128)S(1)}, u32[]{:S(2)}, u32[]{:S(2)}) collective-permute-start(f32[24,2176]{1,0:T(8,128)S(1)} %get-tuple-element.27.refs_0_), channel_id=1, source_target_pairs={{0,4},{4,0},{1,5},{5,1},{2,6},{6,2},{3,7},{7,3},{8,12},{12,8},{9,1... | collective-permute-start | bytes 626696 | tf_op jit(solution)/shard_map/ppermute | solution.py:79
  44.3 6.7 %copy-start.3 = (s32[12]{0:T(128)S(1)}, s32[12]{0:T(128)}, u32[]{:S(2)}) copy-start(s32[12]{0:T(128)} %id_ref.1) | copy-start | bytes 148
  47.8 5.6 %collective-permute-start.5 = (f32[24,1920]{1,0:T(8,128)S(1)}, f32[24,1920]{1,0:T(8,128)S(1)}, u32[]{:S(2)}, u32[]{:S(2)}) collective-permute-start(f32[24,1920]{1,0:T(8,128)S(1)} %vocab_more.1.own_ref), channel_id=1, source_target_pairs={{0,4},{4,0},{1,5},{5,1},{2,6},{6,2},{3,7},{7,3},{8,12},{12,8},{9,1... | collective-permute-start | bytes 552968 | tf_op jit(solution)/shard_map/ppermute | solution.py:79
  53.8 5.5 %collective-permute-start.8 = (f32[12,128]{1,0:T(8,128)S(1)}, f32[12,128]{1,0:T(8,128)S(1)}, u32[]{:S(2)}, u32[]{:S(2)}) collective-permute-start(f32[12,128]{1,0:T(8,128)S(1)} %get-tuple-element.34.refs_2_), channel_id=1, source_target_pairs={{0,3},{1,2},{2,1},{3,0},{4,7},{5,6},{6,5},{7,4},{8,11},{9,10},{10,... | collective-permute-start | bytes 18440 | tf_op jit(solution)/shard_map/ppermute | solution.py:79
  54.9 4.6 %collective-permute-start.7 = (f32[12,128]{1,0:T(8,128)S(1)}, f32[12,128]{1,0:T(8,128)S(1)}, u32[]{:S(2)}, u32[]{:S(2)}) collective-permute-start(f32[12,128]{1,0:T(8,128)S(1)} %get-tuple-element.34.refs_2_), channel_id=1, source_target_pairs={{0,2},{1,3},{2,0},{3,1},{4,6},{5,7},{6,4},{7,5},{8,10},{9,11},{10,... | collective-permute-start | bytes 18440 | tf_op jit(solution)/shard_map/ppermute | solution.py:79
  56.6 3.7 %collective-permute-start.6 = (f32[12,128]{1,0:T(8,128)S(1)}, f32[12,128]{1,0:T(8,128)S(1)}, u32[]{:S(2)}, u32[]{:S(2)}) collective-permute-start(f32[12,128]{1,0:T(8,128)S(1)} %get-tuple-element.34.refs_2_), channel_id=1, source_target_pairs={{0,1},{1,0},{2,3},{3,2},{4,5},{5,4},{6,7},{7,6},{8,9},{9,8},{10,11... | collective-permute-start | bytes 18440 | tf_op jit(solution)/shard_map/ppermute | solution.py:79
